TPU v7x, 8 devices: a whole 2x2x1 slice. The times are simulated.
8 devices in a mesh: ep: 8 (over z, y, x, core).
Axes of the slice: x: 2, y: 2, z: 1, core: 2. Of those that a mesh axis runs over, the one named last changes fastest.
Arguments:
- tokens: bfloat16 [1024, 4096], P('ep')
- k_cache: bfloat16 [1024, 64, 32, 128], P('ep')
- v_cache: bfloat16 [1024, 64, 32, 128], P('ep')
- positions: int32 [1024], P('ep')
- expert_one: int32 [1024], P('ep')
- expert_two: int32 [1024], P('ep')
- eligible: int32 [1024, 16], P('ep')
- ln1_gain: bfloat16 [4096], replicated
- ln1_bias: bfloat16 [4096], replicated
- w_query: bfloat16 [4096, 4096], replicated
- b_query: bfloat16 [4096], replicated
- w_key: bfloat16 [4096, 4096], replicated
- b_key: bfloat16 [4096], replicated
- w_value: bfloat16 [4096, 4096], replicated
- b_value: bfloat16 [4096], replicated
- w_out: bfloat16 [4096, 4096], replicated
- b_out: bfloat16 [4096], replicated
- ln2_gain: bfloat16 [4096], replicated
- ln2_bias: bfloat16 [4096], replicated
- w_router: bfloat16 [4096, 16], replicated
- w_gate: bfloat16 [16, 4096, 688], P('ep')
- w_up: bfloat16 [16, 4096, 688], P('ep')
- w_down: bfloat16 [16, 688, 4096], P('ep')
Outputs:
- output 1: bfloat16 [1024, 4096], P('ep')
- output 2: bfloat16 [1024, 32, 128], P('ep')
- output 3: bfloat16 [1024, 32, 128], P('ep')
All inputs are finite; a program needn't handle non-finite values.
Results may differ from a plain program's by a relative error of at most 0.00972537.
Values are sent between devices in bfloat16 or wider.
A program may use at most 1.25 GiB of HBM per device.

v0:
```python
import jax
import jax.numpy as jnp
from jax import lax
from jax.sharding import PartitionSpec as P

ROPE_BASE = 10000.0
LN_EPS = 1e-5


def layer_norm(values_in, gain, bias):
    mean_val = jnp.mean(values_in, axis=-1, keepdims=True)
    centered = values_in - mean_val
    var_val = jnp.mean(centered * centered, axis=-1, keepdims=True)
    return centered * lax.rsqrt(var_val + LN_EPS) * gain.astype(jnp.float32) + bias.astype(jnp.float32)


def rope_tables(positions, head_dim):
    half_dim = head_dim // 2
    inv_freq = ROPE_BASE ** (jnp.arange(half_dim, dtype=jnp.float32) * (-2.0 / head_dim))
    angles = positions.astype(jnp.float32)[:, None] * inv_freq[None, :]
    angles = jnp.concatenate([angles, angles], axis=-1)
    return jnp.cos(angles), jnp.sin(angles)


def apply_rope(values_in, cos_tab, sin_tab):
    half_dim = values_in.shape[-1] // 2
    rotated = jnp.concatenate([-values_in[..., half_dim:], values_in[..., :half_dim]], axis=-1)
    return values_in * cos_tab[:, None, :] + rotated * sin_tab[:, None, :]


def attention_block(tokens, k_cache, v_cache, positions, ln1_gain, ln1_bias, w_query, b_query, w_key, b_key, w_value, b_value, w_out, b_out):
    tok_count, seq_len, kv_heads, head_dim = k_cache.shape
    num_heads = w_query.shape[1] // head_dim
    group_size = num_heads // kv_heads
    x_f = tokens.astype(jnp.float32)
    h_one = layer_norm(x_f, ln1_gain, ln1_bias).astype(jnp.bfloat16)
    cos_tab, sin_tab = rope_tables(positions, head_dim)
    q_lin = jnp.dot(h_one, w_query, preferred_element_type=jnp.float32) + b_query.astype(jnp.float32)
    q_rot = apply_rope(q_lin.reshape(tok_count, num_heads, head_dim), cos_tab, sin_tab).astype(jnp.bfloat16)
    q_grp = q_rot.reshape(tok_count, kv_heads, group_size, head_dim)
    k_lin = jnp.dot(h_one, w_key, preferred_element_type=jnp.float32) + b_key.astype(jnp.float32)
    key_new = apply_rope(k_lin.reshape(tok_count, kv_heads, head_dim), cos_tab, sin_tab).astype(jnp.bfloat16)
    v_lin = jnp.dot(h_one, w_value, preferred_element_type=jnp.float32) + b_value.astype(jnp.float32)
    value_new = v_lin.astype(jnp.bfloat16).reshape(tok_count, kv_heads, head_dim)
    score_scale = head_dim ** -0.5
    s_cache = jnp.einsum('tkgd,tskd->tkgs', q_grp, k_cache, preferred_element_type=jnp.float32) * score_scale
    valid_mask = jnp.arange(seq_len)[None, None, None, :] < positions[:, None, None, None]
    s_cache = jnp.where(valid_mask, s_cache, -jnp.inf)
    s_new = jnp.einsum('tkgd,tkd->tkg', q_grp, key_new, preferred_element_type=jnp.float32) * score_scale
    top_val = jnp.maximum(jnp.max(s_cache, axis=-1), s_new)
    e_cache = jnp.exp(s_cache - top_val[..., None])
    e_new = jnp.exp(s_new - top_val)
    denom_sum = jnp.sum(e_cache, axis=-1) + e_new
    p_cache = (e_cache / denom_sum[..., None]).astype(jnp.bfloat16)
    p_new = (e_new / denom_sum).astype(jnp.bfloat16)
    attn_vals = jnp.einsum('tkgs,tskd->tkgd', p_cache, v_cache, preferred_element_type=jnp.float32)
    attn_vals = attn_vals + p_new.astype(jnp.float32)[..., None] * value_new.astype(jnp.float32)[:, :, None, :]
    attn_flat = attn_vals.astype(jnp.bfloat16).reshape(tok_count, num_heads * head_dim)
    x_mid = (x_f + jnp.dot(attn_flat, w_out, preferred_element_type=jnp.float32) + b_out.astype(jnp.float32)).astype(jnp.bfloat16)
    return x_mid, key_new, value_new


def router_gates(h_two, w_router, expert_one, expert_two, eligible):
    logits = jnp.dot(h_two, w_router, preferred_element_type=jnp.float32)
    expert_ids = jnp.arange(logits.shape[1])[None, :]
    hit_one = expert_ids == expert_one[:, None]
    hit_two = expert_ids == expert_two[:, None]
    keep_one = eligible == 1
    keep_two = keep_one & jnp.logical_not(hit_one)
    prob_one = jax.nn.softmax(jnp.where(keep_one, logits, -jnp.inf), axis=-1)
    prob_two = jax.nn.softmax(jnp.where(keep_two, logits, -jnp.inf), axis=-1)
    gate_one = jnp.sum(jnp.where(hit_one, prob_one, 0.0), axis=-1)
    gate_two = jnp.sum(jnp.where(hit_two, prob_two, 0.0), axis=-1)
    return gate_one, gate_two


def send_plan(expert_one, expert_two, local_experts, groups, tok_count):
    num_experts = local_experts * groups
    pair_expert = jnp.concatenate([expert_one, expert_two])
    token_ids = jnp.arange(tok_count, dtype=jnp.int32)
    pair_token = jnp.concatenate([token_ids, token_ids])
    one_hot = (pair_expert[:, None] == jnp.arange(num_experts, dtype=jnp.int32)[None, :]).astype(jnp.int32)
    pair_slot = jnp.sum(one_hot * jnp.cumsum(one_hot, axis=0), axis=1) - 1
    buffer_row = ((pair_expert % local_experts) * groups + pair_expert // local_experts) * tok_count + pair_slot
    src_token = jax.ops.segment_sum(pair_token, buffer_row, num_segments=num_experts * tok_count)
    return buffer_row, src_token


def expert_mlp(expert_in, w_gate, w_up, w_down):
    u_val = jnp.einsum('emd,edf->emf', expert_in, w_gate, preferred_element_type=jnp.float32)
    v_val = jnp.einsum('emd,edf->emf', expert_in, w_up, preferred_element_type=jnp.float32)
    z_val = (jax.nn.silu(u_val) * v_val).astype(jnp.bfloat16)
    return jnp.einsum('emf,efd->emd', z_val, w_down, preferred_element_type=jnp.float32).astype(jnp.bfloat16)


def solution(mesh):
    groups = mesh.shape['ep']

    def local_step(tokens, k_cache, v_cache, positions, expert_one, expert_two, eligible, ln1_gain, ln1_bias, w_query, b_query, w_key, b_key, w_value, b_value, w_out, b_out, ln2_gain, ln2_bias, w_router, w_gate, w_up, w_down):
        x_mid, key_new, value_new = attention_block(tokens, k_cache, v_cache, positions, ln1_gain, ln1_bias, w_query, b_query, w_key, b_key, w_value, b_value, w_out, b_out)
        h_two = layer_norm(x_mid.astype(jnp.float32), ln2_gain, ln2_bias).astype(jnp.bfloat16)
        gate_one, gate_two = router_gates(h_two, w_router, expert_one, expert_two, eligible)
        tok_count, d_model = h_two.shape
        local_experts = w_gate.shape[0]
        num_experts = local_experts * groups
        buffer_row, src_token = send_plan(expert_one, expert_two, local_experts, groups, tok_count)
        send_rows = jnp.take(h_two, src_token, axis=0).reshape(local_experts, groups, tok_count, d_model)
        recv_rows = lax.all_to_all(send_rows, 'ep', 1, 1, tiled=True)
        expert_in = recv_rows.reshape(local_experts, groups * tok_count, d_model)
        expert_out = expert_mlp(expert_in, w_gate, w_up, w_down)
        back_rows = lax.all_to_all(expert_out.reshape(local_experts, groups, tok_count, d_model), 'ep', 1, 1, tiled=True)
        back_flat = back_rows.reshape(num_experts * tok_count, d_model)
        out_one = jnp.take(back_flat, buffer_row[:tok_count], axis=0)
        out_two = jnp.take(back_flat, buffer_row[tok_count:], axis=0)
        y_sum = gate_one[:, None] * out_one.astype(jnp.float32) + gate_two[:, None] * out_two.astype(jnp.float32)
        tokens_out = (x_mid.astype(jnp.float32) + y_sum).astype(jnp.bfloat16)
        return tokens_out, key_new, value_new

    row_spec = P('ep', None)
    cache_spec = P('ep', None, None, None)
    vec_spec = P('ep')
    rep_one = P(None)
    rep_two = P(None, None)
    expert_spec = P('ep', None, None)
    in_specs = (row_spec, cache_spec, cache_spec, vec_spec, vec_spec, vec_spec, row_spec, rep_one, rep_one, rep_two, rep_one, rep_two, rep_one, rep_two, rep_one, rep_two, rep_one, rep_one, rep_one, rep_two, expert_spec, expert_spec, expert_spec)
    out_specs = (row_spec, expert_spec, expert_spec)
    return jax.shard_map(local_step, mesh=mesh, in_specs=in_specs, out_specs=out_specs, check_vma=False)
```

profile of v0, /device:TPU:0, one launch (start us, length us, event | category | flops | bytes accessed | tf_op | source)
XLA Modules:
  0.0 692.3 jit_solution(5799089384771228457)
XLA Ops:
  0.7 0.7 convert_element_type.99
  1.5 0.7 iota_compare_fusion
  2.1 0.7 constant_dynamic-update-slice_fusion.1
  2.8 0.7 constant_dynamic-update-slice_fusion
  3.5 0.6 reduce-window.6
  4.4 0.6 multiply_add_fusion
  5.0 0.7 multiply_add_fusion.1
  5.7 1.9 scatter_custom_fusion
  7.6 1.5 convert_reduce_fusion
  9.1 1.7 fusion.10
  10.8 13.0 %fusion.20 = f32[16,8,32,128]{3,1,2,0:T(8,128)S(1)} fusion(bf16[4096,4096]{1,0:T(8,128)(2,1)} %param.34, f32[4096]{0:T(1024)S(1)} %convert_element_type.98, bf16[128,4096]{1,0:T(8,128)(2,1)S(1)} %copy-done.1, f32[4096]{0:T(1024)S(1)} %convert_element_type.96, f32[4096]{0:T(1024)S(1)} %convert_element_type.95, f32[128]{0:T(128)S(1)} %add_rsqrt_fusion.1, ...), kind=kOutput, calls=%fused_computation.42 | convolution fusion | flops 4298637312 | bytes 36750336 | tf_op jit(solution)/shard_map/dot_general | solution.py:38
  23.9 0.4 copy.57
  24.2 0.3 copy-done.11
  24.5 13.0 %fusion.21 = f32[16,8,32,128]{3,1,2,0:T(8,128)S(1)} fusion(bf16[4096,4096]{1,0:T(8,128)(2,1)} %param.36, f32[4096]{0:T(1024)S(1)} %convert_element_type.101, bf16[128,4096]{1,0:T(8,128)(2,1)S(1)} %copy-done.1, f32[4096]{0:T(1024)S(1)} %convert_element_type.96, f32[4096]{0:T(1024)S(1)} %convert_element_type.95, f32[128]{0:T(128)S(1)} %add_rsqrt_fusion.1, ...), kind=kOutput, calls=%fused_computation.43 | convolution fusion | flops 4298637312 | bytes 36750336 | tf_op jit(solution)/shard_map/dot_general | solution.py:41
  37.5 0.4 copy.58
  38.0 0.3 fusion.30
  38.3 1.5 slice_negate_fusion
  39.8 1.6 fusion.17
  41.4 0.9 copy-done.5
  42.4 41.1 %fusion.2 = f32[128,32,1,64]{3,2,1,0:T(1,128)} fusion(bf16[128,64,32,128]{3,2,1,0:T(8,128)(2,1)} %param.26, bf16[128,32,128,1]{2,1,0,3:T(8,128)(2,1)S(1)} %bitcast.83), kind=kOutput, calls=%fused_computation.6 | convolution fusion | flops 67108864 | bytes 69206016 | tf_op jit(solution)/shard_map/tkgd,tskd->tkgs/dot_general | solution.py:46
  83.5 4.7 copy.47
  88.2 1.8 fusion.18
  90.6 0.3 fusion.28
  90.8 3.9 copy.52
  94.9 15.1 %fusion.22 = bf16[16,8,32,128]{3,1,2,0:T(8,128)(2,1)S(1)} fusion(bf16[4096,4096]{1,0:T(8,128)(2,1)} %param.38, f32[4096]{0:T(1024)S(1)} %convert_element_type.106, bf16[128,4096]{1,0:T(8,128)(2,1)S(1)} %copy-done.1, f32[4096]{0:T(1024)S(1)} %convert_element_type.96, f32[4096]{0:T(1024)S(1)} %convert_element_type.95, f32[128]{0:T(128)S(1)} %add_rsqrt_fusion.1, ...), kind=kOutput, calls=%fused_computation.44 | convolution fusion | flops 4299161600 | bytes 35701760 | tf_op jit(solution)/shard_map/dot_general | solution.py:43
  110.3 0.4 copy-done.13
  110.7 42.2 %fusion = f32[128,32,1,128]{3,2,1,0:T(1,128)} fusion(bf16[128,32,64,1]{2,3,1,0:T(2,128)(2,1)} %copy.52, bf16[128,64,32,128]{3,2,1,0:T(8,128)(2,1)} %param.27), kind=kOutput, calls=%fused_computation.4 | convolution fusion | flops 67108864 | bytes 69730304 | tf_op jit(solution)/shard_map/tkgs,tskd->tkgd/dot_general | solution.py:56
  153.0 1.9 add_convert_fusion.2
  154.9 13.6 %fusion.53 = (f32[128]{0:T(128)S(1)}, f32[128,4096]{1,0:T(8,128)S(1)}) fusion(f32[4096]{0:T(1024)S(1)} %convert_element_type.110, bf16[4096,4096]{1,0:T(8,128)(2,1)} %param.40, bf16[16,8,32,128]{3,2,1,0:T(8,128)(2,1)S(1)} %bitcast.82, bf16[128,4096]{1,0:T(8,128)(2,1)S(1)} %copy-done.1), kind=kOutput, calls=%fused_computation.124 | convolution fusion | flops 4298113024 | bytes 37765632 | tf_op jit(solution)/shard_map/dot_general | solution.py:59
  168.6 0.4 multiply_reduce_fusion
  169.0 0.3 copy-done.14
  169.4 0.5 copy-done.2
  169.9 0.4 add_convert_fusion.1
  170.3 14.3 %gather_fusion = bf16[2048,4096]{1,0:T(8,128)(2,1)} fusion(bf16[128,4096]{1,0:T(8,128)(2,1)S(1)} %add_convert_fusion.1, s32[2048]{0:T(1024)S(1)} %fusion.40), kind=kCustom, calls=%fused_computation.2 | custom fusion | bytes 33562624 | tf_op jit(solution)/shard_map/jit(_take)/gather | solution.py:107
  184.6 8.5 %copy_select_fusion = bf16[2,8,128,4096]{3,2,0,1:T(8,128)(2,1)S(1)} fusion(bf16[2,8,128,4096]{3,2,1,0:T(8,128)(2,1)} %bitcast.74, pred[2,8,128]{2,0,1:T(4,128)(4,1)S(1)} %copy.40), kind=kLoop, calls=%fused_computation.8 | loop fusion | flops 8388608 | bytes 33556480 | tf_op jit(solution)/shard_map/jit(_take)/select_n | solution.py:107
  193.1 188.0 %all_to_all.10 = bf16[2,8,128,4096]{3,2,0,1:T(8,128)(2,1)S(1)} all-to-all(bf16[2,8,128,4096]{3,2,0,1:T(8,128)(2,1)S(1)} %copy_select_fusion), channel_id=1, replica_groups=mesh['ep'=8] {'ep'}, dimensions={1} | all-to-all | bytes 33554432 | tf_op jit(solution)/shard_map/all_to_all | solution.py:108
  381.1 6.6 copy.42
  387.7 20.2 %fusion.54 = f32[2,1024,688]{1,2,0:T(8,128)} fusion(bf16[2,1024,4096]{2,1,0:T(8,128)(2,1)} %bitcast.79, bf16[2,4096,688]{1,2,0:T(8,128)(2,1)} %param.45), kind=kOutput, calls=%fused_computation.125 | convolution fusion | flops 11542724608 | bytes 33685504 | tf_op jit(solution)/shard_map/emd,edf->emf/dot_general | solution.py:90
  407.9 21.0 %multiply_convert_fusion = bf16[2,1024,688]{1,2,0:T(8,128)(2,1)} fusion(f32[2,1024,688]{1,2,0:T(8,128)} %fusion.54, bf16[2,1024,4096]{2,1,0:T(8,128)(2,1)} %bitcast.80, bf16[2,4096,688]{1,2,0:T(8,128)(2,1)} %param.46), kind=kOutput, calls=%fused_computation.10 | convolution fusion | flops 11551178752 | bytes 36503552 | tf_op jit(solution)/shard_map/emd,edf->emf/dot_general | solution.py:91
  428.9 21.6 %convolution_convert_fusion = bf16[2,1024,4096]{2,1,0:T(8,128)(2,1)} fusion(bf16[2,1024,688]{1,2,0:T(8,128)(2,1)} %multiply_convert_fusion, bf16[2,688,4096]{2,1,0:T(8,128)(2,1)} %param.47), kind=kOutput, calls=%fused_computation.9 | convolution fusion | flops 11551113216 | bytes 30867456 | tf_op jit(solution)/shard_map/emf,efd->emd/dot_general | solution.py:93
  450.6 14.0 %copy.43 = bf16[2,8,128,4096]{3,2,0,1:T(8,128)(2,1)} copy(bf16[2,8,128,4096]{3,2,1,0:T(8,128)(2,1)} %bitcast.81) | data formatting | bytes 33554432 | tf_op jit(solution)/shard_map/reshape | solution.py:111
  464.6 4.9 all-to-all-start.1
  469.5 0.4 fusion.44
  470.1 183.4 %all-to-all-done.1 = bf16[2,8,128,4096]{3,2,0,1:T(8,128)(2,1)} async-done(((bf16[2,8,128,4096]{3,2,0,1:T(8,128)(2,1)}), bf16[2,8,128,4096]{3,2,0,1:T(8,128)(2,1)}, u32[]{:S(2)}, u32[]{:S(2)}) %all-to-all-start.1) | async-done | bytes 16777248 | tf_op jit(solution)/shard_map/all_to_all | solution.py:111
  653.4 14.0 %copy.44 = bf16[2,8,128,4096]{3,2,1,0:T(8,128)(2,1)} copy(bf16[2,8,128,4096]{3,2,0,1:T(8,128)(2,1)} %all-to-all-done.1) | data formatting | bytes 33554432 | tf_op jit(solution)/shard_map/all_to_all | solution.py:111
  667.4 10.1 %gather_fusion.1 = bf16[128,4096]{1,0:T(8,128)(2,1)S(1)} fusion(bf16[2048,4096]{1,0:T(8,128)(2,1)} %bitcast.75, s32[1024]{0:T(1024)S(1)} %get-tuple-element.34), kind=kCustom, calls=%fused_computation.clone | custom fusion | bytes 2097664 | tf_op jit(solution)/shard_map/jit(_take)/gather | solution.py:113
  677.6 11.2 %gather_fusion.2 = bf16[128,4096]{1,0:T(8,128)(2,1)} fusion(bf16[2048,4096]{1,0:T(8,128)(2,1)} %bitcast.76, s32[1024]{0:T(1024)S(1)} %get-tuple-element.33), kind=kCustom, calls=%fused_computation.1.clone | custom fusion | bytes 2097664 | tf_op jit(solution)/shard_map/jit(_take)/gather | solution.py:114
  688.8 3.0 add_convert_fusion
  (70 shorter events, 1.6 us)
Async XLA Ops:
  0.6 468.9 %copy-start = (bf16[4096,16]{0,1:T(8,128)(2,1)S(1)}, bf16[4096,16]{0,1:T(8,128)(2,1)}, u32[]{:S(2)}) copy-start(bf16[4096,16]{0,1:T(8,128)(2,1)} %param.44) | copy-start | bytes 393220
  0.6 10.2 %copy-start.1 = (bf16[128,4096]{1,0:T(8,128)(2,1)S(1)}, bf16[128,4096]{1,0:T(8,128)(2,1)}, u32[]{:S(2)}) copy-start(bf16[128,4096]{1,0:T(8,128)(2,1)} %param.25) | copy-start | bytes 3145732
  0.7 10.1 %copy-start.8 = (bf16[4096]{0:T(1024)(128)(2,1)S(1)}, bf16[4096]{0:T(1024)(128)(2,1)}, u32[]{:S(2)}) copy-start(bf16[4096]{0:T(1024)(128)(2,1)} %param.32) | copy-start | bytes 24580
  0.7 10.1 %copy-start.9 = (bf16[4096]{0:T(1024)(128)(2,1)S(1)}, bf16[4096]{0:T(1024)(128)(2,1)}, u32[]{:S(2)}) copy-start(bf16[4096]{0:T(1024)(128)(2,1)} %param.33) | copy-start | bytes 24580
  0.7 10.1 %copy-start.10 = (bf16[4096]{0:T(1024)(128)(2,1)S(1)}, bf16[4096]{0:T(1024)(128)(2,1)}, u32[]{:S(2)}) copy-start(bf16[4096]{0:T(1024)(128)(2,1)} %param.35) | copy-start | bytes 24580
  23.8 0.7 copy-start.11
  41.4 1.0 copy-start.5
  41.4 46.8 %copy-start.4 = (bf16[128,32,128]{2,1,0:T(8,128)(2,1)}, bf16[128,32,128]{2,1,0:T(8,128)(2,1)S(1)}, u32[]{:S(2)}) copy-start(bf16[128,32,128]{2,1,0:T(8,128)(2,1)S(1)} %get-tuple-element.18) | copy-start | bytes 3145732
  90.5 4.3 copy-start.12
  110.0 0.7 copy-start.13
  110.7 42.3 %copy-start.6 = (bf16[16,8,32,128]{3,2,1,0:T(8,128)(2,1)}, bf16[16,8,32,128]{3,2,1,0:T(8,128)(2,1)S(1)}, u32[]{:S(2)}) copy-start(bf16[16,8,32,128]{3,2,1,0:T(8,128)(2,1)S(1)} %copy.59) | copy-start | bytes 3145732
  168.6 1.3 copy-start.2
  168.6 0.7 copy-start.14
  168.6 0.8 copy-start.15
  464.6 4.9 copy-start.17
  464.6 5.0 copy-start.7
  464.6 5.4 copy-start.16
  464.6 5.4 copy-start.18
  464.6 188.9 %all-to-all-start.1 = ((bf16[2,8,128,4096]{3,2,0,1:T(8,128)(2,1)}), bf16[2,8,128,4096]{3,2,0,1:T(8,128)(2,1)}, u32[]{:S(2)}, u32[]{:S(2)}) async-start(bf16[2,8,128,4096]{3,2,0,1:T(8,128)(2,1)} %copy.43), calls=%async_computation.1 | async-start | bytes 33554432 | tf_op jit(solution)/shard_map/all_to_all | solution.py:111
  677.6 11.3 %copy-start.3 = (f32[128,4096]{1,0:T(8,128)S(1)}, f32[128,4096]{1,0:T(8,128)}, u32[]{:S(2)}) copy-start(f32[128,4096]{1,0:T(8,128)} %copy-done.2) | copy-start | bytes 6291460
where the time goes:
time: 701 us; the launch traced here: 692 us
  matrix products  201 us (29%)
  blocking collectives  188 us (27%)
  waiting for transfers between devices  183 us (26%)
  local copies, waits for them, and re-layouts  84.2 us (12%)
  other arithmetic  28.9 us (4%)
    all_to_all x1, blocking collectives, local_step(): recv_rows = lax.all_to_all(send_rows, 'ep', 1, 1, tiled=True)  188 us
    all_to_all x1, waiting for transfers between devices, local_step(): lax.all_to_all(expert_out.reshape(local_experts, groups, tok_count, d_mod...  183 us
    dot_general x1, matrix products, attention_block(): jnp.einsum('tkgs,tskd->tkgd', p_cache, v_cache, preferred_element_type=jn...  42.2 us
    dot_general x1, matrix products, attention_block(): jnp.einsum('tkgd,tskd->tkgs', q_grp, k_cache, preferred_element_type=jnp....  41.1 us
    dot_general x1, matrix products, expert_mlp(): jnp.einsum('emf,efd->emd', z_val, w_down, preferred_element_type=jnp.floa...  21.6 us
    dot_general x1, matrix products, expert_mlp(): jnp.einsum('emd,edf->emf', expert_in, w_up, preferred_element_type=jnp.fl...  21 us
    dot_general x1, matrix products, expert_mlp(): jnp.einsum('emd,edf->emf', expert_in, w_gate, preferred_element_type=jnp....  20.2 us
    dot_general x1, matrix products, attention_block(): jnp.dot(h_one, w_value, preferred_element_type=jnp.float32)  15.1 us
  transfers between devices with their start and end apart: 1, of which 1 were waited for; matrix products, arithmetic and copies ran while one was open for 0% of the time, Pallas kernels for 0%

commit v1 on v0

--- a/solution.py
+++ b/solution.py
@@ -74,21 +74,9 @@
     return gate_one, gate_two
 
 
-def send_plan(expert_one, expert_two, local_experts, groups, tok_count):
-    num_experts = local_experts * groups
-    pair_expert = jnp.concatenate([expert_one, expert_two])
-    token_ids = jnp.arange(tok_count, dtype=jnp.int32)
-    pair_token = jnp.concatenate([token_ids, token_ids])
-    one_hot = (pair_expert[:, None] == jnp.arange(num_experts, dtype=jnp.int32)[None, :]).astype(jnp.int32)
-    pair_slot = jnp.sum(one_hot * jnp.cumsum(one_hot, axis=0), axis=1) - 1
-    buffer_row = ((pair_expert % local_experts) * groups + pair_expert // local_experts) * tok_count + pair_slot
-    src_token = jax.ops.segment_sum(pair_token, buffer_row, num_segments=num_experts * tok_count)
-    return buffer_row, src_token
-
-
 def expert_mlp(expert_in, w_gate, w_up, w_down):
-    u_val = jnp.einsum('emd,edf->emf', expert_in, w_gate, preferred_element_type=jnp.float32)
-    v_val = jnp.einsum('emd,edf->emf', expert_in, w_up, preferred_element_type=jnp.float32)
+    u_val = jnp.einsum('md,edf->emf', expert_in, w_gate, preferred_element_type=jnp.float32)
+    v_val = jnp.einsum('md,edf->emf', expert_in, w_up, preferred_element_type=jnp.float32)
     z_val = (jax.nn.silu(u_val) * v_val).astype(jnp.bfloat16)
     return jnp.einsum('emf,efd->emd', z_val, w_down, preferred_element_type=jnp.float32).astype(jnp.bfloat16)
 
@@ -102,16 +90,18 @@
         gate_one, gate_two = router_gates(h_two, w_router, expert_one, expert_two, eligible)
         tok_count, d_model = h_two.shape
         local_experts = w_gate.shape[0]
-        num_experts = local_experts * groups
-        buffer_row, src_token = send_plan(expert_one, expert_two, local_experts, groups, tok_count)
-        send_rows = jnp.take(h_two, src_token, axis=0).reshape(local_experts, groups, tok_count, d_model)
-        recv_rows = lax.all_to_all(send_rows, 'ep', 1, 1, tiled=True)
-        expert_in = recv_rows.reshape(local_experts, groups * tok_count, d_model)
-        expert_out = expert_mlp(expert_in, w_gate, w_up, w_down)
-        back_rows = lax.all_to_all(expert_out.reshape(local_experts, groups, tok_count, d_model), 'ep', 1, 1, tiled=True)
-        back_flat = back_rows.reshape(num_experts * tok_count, d_model)
-        out_one = jnp.take(back_flat, buffer_row[:tok_count], axis=0)
-        out_two = jnp.take(back_flat, buffer_row[tok_count:], axis=0)
+        all_rows = lax.all_gather(h_two, 'ep', axis=0, tiled=True)
+        choices = lax.all_gather(jnp.stack([expert_one, expert_two], axis=1), 'ep', axis=0, tiled=True)
+        expert_out = expert_mlp(all_rows, w_gate, w_up, w_down)
+        local_ids = lax.axis_index('ep') * local_experts + jnp.arange(local_experts, dtype=jnp.int32)
+        slots = []
+        for slot in range(2):
+            hit = choices[:, slot][None, :] == local_ids[:, None]
+            slots.append(jnp.sum(jnp.where(hit[:, :, None], expert_out, 0), axis=0, dtype=jnp.bfloat16))
+        by_owner = jnp.stack([x.reshape(groups, tok_count, d_model) for x in slots], axis=1).reshape(groups * 2 * tok_count, d_model)
+        mine = lax.psum_scatter(by_owner, 'ep', scatter_dimension=0, tiled=True)
+        out_one = mine[:tok_count]
+        out_two = mine[tok_count:]
         y_sum = gate_one[:, None] * out_one.astype(jnp.float32) + gate_two[:, None] * out_two.astype(jnp.float32)
         tokens_out = (x_mid.astype(jnp.float32) + y_sum).astype(jnp.bfloat16)
         return tokens_out, key_new, value_new

time: 701 us -> 446 us (0.64)
  blocking collectives: 188 us -> 13.7 us
  local copies, waits for them, and re-layouts: 84.2 us -> 13.4 us
  waiting for transfers between devices: 183 us -> 143 us
  matrix products: 201 us -> 225 us
  between operations: 1.56 us -> 14.7 us
    all_to_all x1 -> x0, blocking collectives: 188 us -> none  [local_step(): recv_rows = lax.all_to_all(send_rows, 'ep', 1, 1, tiled=True)]
    all_to_all x1 -> x0, waiting for transfers between devices: 183 us -> none  [local_step(): lax.all_to_all(expert_out.reshape(local_experts, groups, tok_count, d_mod...]
    reduce_scatter x0 -> x1, waiting for transfers between devices: none -> 105 us  [local_step(): mine = lax.psum_scatter(by_owner, 'ep', scatter_dimension=0, tiled=True)]
    all_gather x0 -> x1, waiting for transfers between devices: none -> 37.5 us  [local_step(): all_rows = lax.all_gather(h_two, 'ep', axis=0, tiled=True)]
    gather x3 -> x0, local copies, waits for them, and re-layouts: 35.7 us -> none  [the longest x1 14.3 us: local_step(): jnp.take(h_two, src_token, axis=0)]
    dot_general x1, matrix products: 21.6 us -> 53.7 us  [expert_mlp(): jnp.einsum('emf,efd->emd', z_val, w_down, preferred_element_type=jnp.floa...]
    all_to_all x2 -> x0, local copies, waits for them, and re-layouts: 20.6 us -> none  [the longest x1 14 us: local_step(): lax.all_to_all(expert_out.reshape(local_experts, groups, tok_count, d_mod...]
    reshape x1 -> x0, local copies, waits for them, and re-layouts: 14 us -> none  [local_step(): expert_out.reshape(local_experts, groups, tok_count, d_model)]
  transfers between devices with their start and end apart: 1 -> 2, of which waited for: 1 -> 2; matrix products, arithmetic and copies ran while one was open for 0% -> 0% of each run, Pallas kernels for 0% -> 0%
where the time goes in v1:
time: 446 us; the launch traced here: 441 us
  matrix products  225 us (50%)
  waiting for transfers between devices  143 us (32%)
  other arithmetic  30.9 us (7%)
  between operations  14.7 us (3%)
  blocking collectives  13.7 us (3%)
  local copies, waits for them, and re-layouts  13.4 us (3%)
    reduce_scatter x1, waiting for transfers between devices, local_step(): mine = lax.psum_scatter(by_owner, 'ep', scatter_dimension=0, tiled=True)  105 us
    dot_general x1, matrix products, expert_mlp(): jnp.einsum('emf,efd->emd', z_val, w_down, preferred_element_type=jnp.floa...  53.7 us
    dot_general x1, matrix products, attention_block(): jnp.einsum('tkgs,tskd->tkgd', p_cache, v_cache, preferred_element_type=jn...  42.2 us
    dot_general x1, matrix products, attention_block(): jnp.einsum('tkgd,tskd->tkgs', q_grp, k_cache, preferred_element_type=jnp....  41.1 us
    all_gather x1, waiting for transfers between devices, local_step(): all_rows = lax.all_gather(h_two, 'ep', axis=0, tiled=True)  37.5 us
    dot_general x1, matrix products, expert_mlp(): jnp.einsum('md,edf->emf', expert_in, w_up, preferred_element_type=jnp.flo...  16.6 us
    dot_general x1, matrix products, expert_mlp(): jnp.einsum('md,edf->emf', expert_in, w_gate, preferred_element_type=jnp.f...  16.3 us
    dot_general x1, matrix products, attention_block(): jnp.dot(h_one, w_value, preferred_element_type=jnp.float32)  15.2 us
  transfers between devices with their start and end apart: 2, of which 2 were waited for; matrix products, arithmetic and copies ran while one was open for 0% of the time, Pallas kernels for 0%

profile of v1, /device:TPU:0, one launch (start us, length us, event | category | flops | bytes accessed | tf_op | source)
XLA Modules:
  0.0 441.0 jit_solution(4625524891124955747)
XLA Ops:
  7.2 0.0 copy-start
  7.2 0.0 copy-start.1
  7.3 0.0 all-gather.2.cloned.1.call-start
  7.3 0.7 convert_element_type.97
  8.1 0.7 iota_compare_fusion
  8.7 1.5 convert_reduce_fusion
  10.2 1.7 fusion.20
  12.0 0.1 broadcast_multiply_fusion
  12.1 0.3 fusion.40
  12.4 15.2 %fusion.32 = bf16[16,8,32,128]{3,1,2,0:T(8,128)(2,1)S(1)} fusion(bf16[4096,4096]{1,0:T(8,128)(2,1)} %param.36, f32[4096]{0:T(1024)S(1)} %convert_element_type.104, bf16[128,4096]{1,0:T(8,128)(2,1)S(1)} %copy-done.1, f32[4096]{0:T(1024)S(1)} %convert_element_type.94, f32[4096]{0:T(1024)S(1)} %convert_element_type.93, f32[128]{0:T(128)S(1)} %add_rsqrt_fusion.1, ...), kind=kOutput, calls=%fused_computation.52 | convolution fusion | flops 4299161600 | bytes 35701760 | tf_op jit(solution)/shard_map/dot_general | solution.py:43
  27.6 0.2 copy.40
  27.9 0.0 copy-start.4
  27.9 13.4 %fusion.31 = f32[16,8,32,128]{3,1,2,0:T(8,128)S(1)} fusion(bf16[4096,4096]{1,0:T(8,128)(2,1)} %param.34, f32[4096]{0:T(1024)S(1)} %convert_element_type.99, bf16[128,4096]{1,0:T(8,128)(2,1)S(1)} %copy-done.1, f32[4096]{0:T(1024)S(1)} %convert_element_type.94, f32[4096]{0:T(1024)S(1)} %convert_element_type.93, f32[128]{0:T(128)S(1)} %add_rsqrt_fusion.1, ...), kind=kOutput, calls=%fused_computation.51 | convolution fusion | flops 4298637312 | bytes 36750336 | tf_op jit(solution)/shard_map/dot_general | solution.py:41
  41.2 0.4 copy.39
  41.6 13.0 %fusion.30 = f32[16,8,32,128]{3,1,2,0:T(8,128)S(1)} fusion(bf16[4096,4096]{1,0:T(8,128)(2,1)} %param.32, f32[4096]{0:T(1024)S(1)} %convert_element_type.96, bf16[128,4096]{1,0:T(8,128)(2,1)S(1)} %copy-done.1, f32[4096]{0:T(1024)S(1)} %convert_element_type.94, f32[4096]{0:T(1024)S(1)} %convert_element_type.93, f32[128]{0:T(128)S(1)} %add_rsqrt_fusion.1, ...), kind=kOutput, calls=%fused_computation.50 | convolution fusion | flops 4298637312 | bytes 36750336 | tf_op jit(solution)/shard_map/dot_general | solution.py:38
  54.6 0.4 copy.38
  55.0 1.5 slice_negate_fusion
  56.5 1.6 fusion.27
  58.1 0.0 copy-start.3
  58.1 1.0 copy-done.3
  59.1 0.6 fusion.28
  59.7 0.1 copy.33
  59.8 41.1 %fusion.2 = f32[128,32,1,64]{3,2,1,0:T(1,128)} fusion(bf16[128,64,32,128]{3,2,1,0:T(8,128)(2,1)} %param.24, bf16[128,32,128,1]{2,1,0,3:T(8,128)(2,1)S(1)} %bitcast.83), kind=kOutput, calls=%fused_computation.2 | convolution fusion | flops 67108864 | bytes 69206016 | tf_op jit(solution)/shard_map/tkgd,tskd->tkgs/dot_general | solution.py:46
  100.9 4.7 %copy.29 = f32[128,32,1,64]{0,3,1,2:T(8,128)S(1)} copy(f32[128,32,1,64]{3,2,1,0:T(1,128)} %fusion.2) | data formatting | bytes 2097152 | tf_op jit(solution)/shard_map/tkgd,tskd->tkgs/dot_general | solution.py:46
  105.6 0.1 fusion.37
  105.8 0.3 fusion.36
  106.0 1.1 fusion.38
  107.1 0.1 copy.26
  107.2 5.3 %copy.34 = bf16[128,32,64,1]{2,3,1,0:T(2,128)(2,1)} copy(bf16[128,32,64,1]{0,2,1,3:T(8,128)(2,1)} %fusion.38) | data formatting | bytes 1048576 | tf_op jit(solution)/shard_map/convert_element_type | solution.py:54
  112.5 42.2 %fusion = f32[128,32,1,128]{3,2,1,0:T(1,128)} fusion(bf16[128,32,64,1]{2,3,1,0:T(2,128)(2,1)} %copy.34, bf16[128,64,32,128]{3,2,1,0:T(8,128)(2,1)} %param.25), kind=kOutput, calls=%fused_computation | convolution fusion | flops 67108864 | bytes 69730304 | tf_op jit(solution)/shard_map/tkgs,tskd->tkgd/dot_general | solution.py:56
  154.7 1.9 add_convert_fusion.2
  156.6 13.4 %fusion.54 = (f32[128]{0:T(128)S(1)}, f32[128,4096]{1,0:T(8,128)S(1)}) fusion(f32[4096]{0:T(1024)S(1)} %convert_element_type.108, bf16[4096,4096]{1,0:T(8,128)(2,1)} %param.38, bf16[16,8,32,128]{3,2,1,0:T(8,128)(2,1)S(1)} %bitcast.82, bf16[128,4096]{1,0:T(8,128)(2,1)S(1)} %copy-done.1), kind=kOutput, calls=%fused_computation.97 | convolution fusion | flops 4298113024 | bytes 37765632 | tf_op jit(solution)/shard_map/dot_general | solution.py:59
  170.1 0.4 multiply_reduce_fusion
  170.5 1.4 add_convert_fusion.1
  171.9 0.0 all-gather.2.cloned.1.call-update
  171.9 0.0 reduce-scatter.2.cloned.1.call-start
  172.0 13.7 %all_gather.6 = s32[1024,2]{0,1:T(2,128)S(1)} all-gather(s32[128,2]{0,1:T(2,128)S(1)} %pad_add_fusion), channel_id=1, replica_groups=mesh['ep'=8] {'ep'}, dimensions={0}, use_global_device_ids=true | all-gather | bytes 9216 | tf_op jit(solution)/shard_map/all_gather | solution.py:94
  185.7 0.1 broadcast_compare_fusion
  185.8 37.5 %all-gather.2.cloned.1.call-done = bf16[1024,4096]{1,0:T(8,128)(2,1)} async-done(((bf16[128,4096]{1,0:T(8,128)(2,1)}), bf16[1024,4096]{1,0:T(8,128)(2,1)}) %all-gather.2.cloned.1.call-update) | async-done | bytes 8388624 | tf_op jit(solution)/shard_map/all_gather | solution.py:93
  223.3 16.6 %fusion.4 = f32[1024,2,688]{0,2,1:T(8,128)S(1)} fusion(bf16[2,4096,688]{1,2,0:T(8,128)(2,1)} %param.44, bf16[1024,4096]{1,0:T(8,128)(2,1)} %all-gather.2.cloned.1.call-done), kind=kOutput, calls=%fused_computation.8 | convolution fusion | flops 11542724608 | bytes 25296896 | tf_op jit(solution)/shard_map/md,edf->emf/dot_general | solution.py:79
  239.9 16.3 %fusion.8 = bf16[2,1024,688]{1,2,0:T(8,128)(2,1)} fusion(f32[1024,2,688]{0,2,1:T(8,128)S(1)} %fusion.4, bf16[2,4096,688]{1,2,0:T(8,128)(2,1)} %param.43, bf16[1024,4096]{1,0:T(8,128)(2,1)S(1)} %copy-done.16), kind=kOutput, calls=%fused_computation.13 | convolution fusion | flops 11551178752 | bytes 28114944 | tf_op jit(solution)/shard_map/md,edf->emf/dot_general | solution.py:78
  256.2 53.7 %select_reduce_fusion.1 = (bf16[1024,4096]{1,0:T(8,128)(2,1)}, bf16[1024,4096]{1,0:T(8,128)(2,1)}) fusion(pred[2,1024]{1,0:T(4,128)(4,1)S(1)} %get-tuple-element.24, pred[2,1024]{1,0:T(4,128)(4,1)S(1)} %get-tuple-element.23, bf16[2,1024,688]{1,2,0:T(8,128)(2,1)} %fusion.8, bf16[2,688,4096]{2,1,0:T(8,128)(2,1)} %param.45), kind=kOutput, calls=%fused_computation.6 | convolution fusion | flops 11576279040 | bytes 30871552 | tf_op jit(solution)/shard_map/emf,efd->emd/dot_general | solution.py:81
  309.9 13.8 %pad_maximum_fusion = bf16[8,2,128,4096]{3,2,1,0:T(8,128)(2,1)} fusion(bf16[8,1,128,4096]{3,2,1,0:T(8,128)(2,1)} %bitcast.81, bf16[8,1,128,4096]{3,2,1,0:T(8,128)(2,1)} %bitcast.80), kind=kLoop, calls=%fused_computation.4 | loop fusion | flops 8388608 | bytes 33554432 | tf_op jit(solution)/shard_map/stack | solution.py:101
  323.7 0.0 reduce-scatter.2.cloned.1.call-update
  323.7 1.2 copy-done.2
  324.9 0.4 fusion.48
  325.4 105.4 %reduce-scatter.2.cloned.1.call-done = bf16[256,4096]{1,0:T(8,128)(2,1)} async-done(((bf16[2048,4096]{1,0:T(8,128)(2,1)}), bf16[256,4096]{1,0:T(8,128)(2,1)}) %reduce-scatter.2.cloned.1.call-update) | async-done | bytes 2097168 | tf_op jit(solution)/shard_map/reduce_scatter | solution.py:102
  430.8 3.1 add_convert_fusion
  (49 shorter events, 0.3 us)
Async XLA Ops:
  7.2 316.6 %copy-start = (bf16[4096,16]{0,1:T(8,128)(2,1)S(1)}, bf16[4096,16]{0,1:T(8,128)(2,1)}, u32[]{:S(2)}) copy-start(bf16[4096,16]{0,1:T(8,128)(2,1)} %param.42) | copy-start | bytes 393220
  7.2 5.3 %copy-start.1 = (bf16[128,4096]{1,0:T(8,128)(2,1)S(1)}, bf16[128,4096]{1,0:T(8,128)(2,1)}, u32[]{:S(2)}) copy-start(bf16[128,4096]{1,0:T(8,128)(2,1)} %param.23) | copy-start | bytes 3145732
  7.2 4.7 %copy-start.6 = (bf16[4096]{0:T(1024)(128)(2,1)S(1)}, bf16[4096]{0:T(1024)(128)(2,1)}, u32[]{:S(2)}) copy-start(bf16[4096]{0:T(1024)(128)(2,1)} %param.30) | copy-start | bytes 24580
  7.2 4.7 %copy-start.7 = (bf16[4096]{0:T(1024)(128)(2,1)S(1)}, bf16[4096]{0:T(1024)(128)(2,1)}, u32[]{:S(2)}) copy-start(bf16[4096]{0:T(1024)(128)(2,1)} %param.31) | copy-start | bytes 24580
  7.2 4.7 %copy-start.8 = (bf16[4096]{0:T(1024)(128)(2,1)S(1)}, bf16[4096]{0:T(1024)(128)(2,1)}, u32[]{:S(2)}) copy-start(bf16[4096]{0:T(1024)(128)(2,1)} %param.33) | copy-start | bytes 24580
  7.2 4.7 %copy-start.9 = (bf16[4096]{0:T(1024)(128)(2,1)S(1)}, bf16[4096]{0:T(1024)(128)(2,1)}, u32[]{:S(2)}) copy-start(bf16[4096]{0:T(1024)(128)(2,1)} %param.35) | copy-start | bytes 24580
  7.2 4.7 %copy-start.10 = (bf16[4096]{0:T(1024)(128)(2,1)S(1)}, bf16[4096]{0:T(1024)(128)(2,1)}, u32[]{:S(2)}) copy-start(bf16[4096]{0:T(1024)(128)(2,1)} %param.37) | copy-start | bytes 24580
  7.2 4.7 %copy-start.11 = (bf16[4096]{0:T(1024)(128)(2,1)S(1)}, bf16[4096]{0:T(1024)(128)(2,1)}, u32[]{:S(2)}) copy-start(bf16[4096]{0:T(1024)(128)(2,1)} %param.39) | copy-start | bytes 24580
  7.3 4.7 %copy-start.12 = (bf16[4096]{0:T(1024)(128)(2,1)S(1)}, bf16[4096]{0:T(1024)(128)(2,1)}, u32[]{:S(2)}) copy-start(bf16[4096]{0:T(1024)(128)(2,1)} %param.40) | copy-start | bytes 24580
  7.3 4.7 %copy-start.13 = (bf16[4096]{0:T(1024)(128)(2,1)S(1)}, bf16[4096]{0:T(1024)(128)(2,1)}, u32[]{:S(2)}) copy-start(bf16[4096]{0:T(1024)(128)(2,1)} %param.41) | copy-start | bytes 24580
  7.3 216.1 %all-gather.2.cloned.1.call-start = ((), (), s32[]{:S(2)}) async-start(), calls=%async_computation.1 | async-start | bytes 9437184 | tf_op jit(solution)/shard_map/all_gather | solution.py:93
  27.9 126.8 %copy-start.4 = (bf16[16,8,32,128]{3,2,1,0:T(8,128)(2,1)}, bf16[16,8,32,128]{3,2,1,0:T(8,128)(2,1)S(1)}, u32[]{:S(2)}) copy-start(bf16[16,8,32,128]{3,2,1,0:T(8,128)(2,1)S(1)} %copy.40) | copy-start | bytes 3145732
  58.1 1.0 copy-start.3
  170.5 1.5 copy-start.14
  170.5 1.5 copy-start.15
  171.9 258.9 %reduce-scatter.2.cloned.1.call-start = ((), (), s32[]{:S(2)}) async-start(), calls=%async_computation.2 | async-start | bytes 18874368 | tf_op jit(solution)/shard_map/reduce_scatter | solution.py:102
  223.3 16.6 %copy-start.16 = (bf16[1024,4096]{1,0:T(8,128)(2,1)S(1)}, bf16[1024,4096]{1,0:T(8,128)(2,1)}, u32[]{:S(2)}) copy-start(bf16[1024,4096]{1,0:T(8,128)(2,1)} %all-gather.2.cloned.1.call-done) | copy-start | bytes 25165828
  323.7 1.2 copy-start.2
  323.7 1.2 copy-start.5
Sparse Core Ops, SparseCore 0:
  172.0 51.2 all-gather.1
  323.8 106.9 reduce-scatter.1

commit v2 on v1

v2 whole, which is shorter than its diff:
```python
import jax
import jax.numpy as jnp
from jax import lax
from jax.experimental import pallas as pl
from jax.experimental.pallas import tpu as pltpu
from jax.sharding import PartitionSpec as P

ROPE_BASE = 10000.0
LN_EPS = 1e-5


def rope_tables(positions, head_dim):
    half_dim = head_dim // 2
    inv_freq = ROPE_BASE ** (jnp.arange(half_dim, dtype=jnp.float32) * (-2.0 / head_dim))
    angles = positions.astype(jnp.float32)[:, None] * inv_freq[None, :]
    angles = jnp.concatenate([angles, angles], axis=-1)
    return jnp.cos(angles), jnp.sin(angles)


def norm_rows(x_val, gain, bias):
    mean_val = jnp.mean(x_val, axis=-1, keepdims=True)
    centered = x_val - mean_val
    var_val = jnp.mean(centered * centered, axis=-1, keepdims=True)
    return centered * lax.rsqrt(var_val + LN_EPS) * gain.astype(jnp.float32) + bias.astype(jnp.float32)


def qkv_kernel(x_ref, gain_ref, bias_ref, cos_ref, sin_ref, wq_ref, wk_ref, wv_ref, bq_ref, bk_ref, bv_ref, q_ref, k_ref, v_ref, h_ref):
    @pl.when(pl.program_id(0) == 0)
    def _():
        h_ref[...] = norm_rows(x_ref[...].astype(jnp.float32), gain_ref[...], bias_ref[...]).astype(jnp.bfloat16)

    h_val = h_ref[...]
    head_dim = cos_ref.shape[1]
    cos_tab, sin_tab = cos_ref[...], sin_ref[...]
    for w_ref, b_ref, o_ref in ((wq_ref, bq_ref, q_ref), (wk_ref, bk_ref, k_ref)):
        lin = jnp.dot(h_val, w_ref[...], preferred_element_type=jnp.float32) + b_ref[...].astype(jnp.float32)
        for c in range(lin.shape[1] // head_dim):
            part = lin[:, c * head_dim:(c + 1) * head_dim]
            rot = part * cos_tab + pltpu.roll(part, head_dim // 2, 1) * sin_tab
            o_ref[:, c * head_dim:(c + 1) * head_dim] = rot.astype(jnp.bfloat16)
    lin = jnp.dot(h_val, wv_ref[...], preferred_element_type=jnp.float32) + bv_ref[...].astype(jnp.float32)
    v_ref[...] = lin.astype(jnp.bfloat16)


def qkv_call(tokens, gain, bias, cos_tab, sin_signed, w_query, b_query, w_key, b_key, w_value, b_value):
    rows, d_model = tokens.shape
    cols = w_query.shape[1]
    tile = 256
    whole = lambda shape: pl.BlockSpec(shape, lambda i: (0,) * len(shape))
    wide = pl.BlockSpec((d_model, tile), lambda i: (0, i))
    slim = pl.BlockSpec((1, tile), lambda i: (0, i))
    out = pl.BlockSpec((rows, tile), lambda i: (0, i))
    shape = jax.ShapeDtypeStruct((rows, cols), jnp.bfloat16)
    row = lambda t: t.reshape(1, -1)
    return pl.pallas_call(
        qkv_kernel,
        grid=(cols // tile,),
        in_specs=[whole((rows, d_model)), whole((1, d_model)), whole((1, d_model)), whole(cos_tab.shape), whole(cos_tab.shape), wide, wide, wide, slim, slim, slim],
        out_specs=[out, out, out],
        out_shape=[shape, shape, shape],
        scratch_shapes=[pltpu.VMEM((rows, d_model), jnp.bfloat16)],
        compiler_params=pltpu.CompilerParams(vmem_limit_bytes=40 * 2 ** 20),
        cost_estimate=pl.CostEstimate(flops=6 * rows * d_model * cols, bytes_accessed=6 * d_model * cols, transcendentals=0),
        name='qkv',
    )(tokens, row(gain), row(bias), cos_tab, sin_signed, w_query, w_key, w_value, row(b_query), row(b_key), row(b_value))


GROUP = 4
SLOTS = 3
STEP = 16


def attend_kernel(order_ref, pos_ref, q_ref, kn_ref, vn_ref, k_hbm, v_hbm, out_ref, k_buf, v_buf, sid_ref, sems):
    rows, heads, head_dim = q_ref.shape
    seq = k_hbm.shape[1]
    groups = rows // GROUP
    scale = head_dim ** -0.5
    key_id = lax.broadcasted_iota(jnp.int32, sid_ref.shape, 1)
    row_id = lax.broadcasted_iota(jnp.int32, sid_ref.shape, 0)
    sid_ref[...] = jnp.where(lax.rem(key_id, heads) == row_id, lax.div(key_id, heads), seq)
    v_buf[...] = jnp.zeros_like(v_buf)

    def copies(grp, act):
        slot = lax.rem(grp, SLOTS)
        for i in range(GROUP):
            tok = order_ref[grp * GROUP + i]
            need = (pos_ref[tok] + 3) // 4 * 4
            size = seq
            while size >= 4:
                first = need // (2 * size) * (2 * size)

                @pl.when((need // size) % 2 == 1)
                def _(size=size, first=first):
                    src = pl.ds(first, size)
                    for hbm, buf, n in ((k_hbm, k_buf, 0), (v_hbm, v_buf, 1)):
                        copy = pltpu.make_async_copy(hbm.at[tok, src], buf.at[slot, i, src], sems.at[n, slot])
                        if act == 'start':
                            copy.start()
                        else:
                            copy.wait()
                size //= 2

    def compute(grp, steps):
        slot = lax.rem(grp, SLOTS)
        keys = steps * STEP * heads
        toks = [order_ref[grp * GROUP + i] for i in range(GROUP)]
        q_val = [q_ref[t] for t in toks]
        scores = []
        for i in range(GROUP):
            k_val = k_buf[slot, i, pl.ds(0, steps * STEP)].reshape(keys, head_dim)
            raw = lax.dot_general(q_val[i], k_val, (((1,), (1,)), ((), ())), preferred_element_type=jnp.float32)
            scores.append(jnp.where(sid_ref[:, :keys] < pos_ref[toks[i]], raw * scale, -jnp.inf))
        for i in range(GROUP):
            t = toks[i]
            s_new = jnp.sum(q_val[i].astype(jnp.float32) * kn_ref[t].astype(jnp.float32), axis=-1, keepdims=True) * scale
            top = jnp.maximum(jnp.max(scores[i], axis=-1, keepdims=True), s_new)
            e_val = jnp.exp(scores[i] - top)
            e_new = jnp.exp(s_new - top)
            inv = 1.0 / (jnp.sum(e_val, axis=-1, keepdims=True) + e_new)
            p_val = (e_val * inv).astype(jnp.bfloat16)
            p_new = (e_new * inv).astype(jnp.bfloat16).astype(jnp.float32)
            v_val = v_buf[slot, i, pl.ds(0, steps * STEP)].reshape(keys, head_dim)
            res = jnp.dot(p_val, v_val, preferred_element_type=jnp.float32) + p_new * vn_ref[t].astype(jnp.float32)
            out_ref[t] = res.astype(jnp.bfloat16)

    for g in range(SLOTS - 1):
        copies(g, 'start')

    @pl.loop(0, groups)
    def _(grp):
        @pl.when(grp + SLOTS - 1 < groups)
        def _():
            copies(grp + SLOTS - 1, 'start')

        copies(grp, 'wait')
        most = pos_ref[order_ref[grp * GROUP]]
        for i in range(1, GROUP):
            most = jnp.maximum(most, pos_ref[order_ref[grp * GROUP + i]])
        steps = jnp.maximum((most + STEP - 1) // STEP, 1)
        for n in range(1, seq // STEP + 1):
            @pl.when(steps == n)
            def _(n=n):
                compute(grp, n)


def attend_call(order, positions, q_rot, key_new, value_new, k_cache, v_cache):
    rows, seq, heads, head_dim = k_cache.shape
    vmem = pl.BlockSpec(memory_space=pltpu.VMEM)
    smem = pl.BlockSpec(memory_space=pltpu.SMEM)
    hbm = pl.BlockSpec(memory_space=pl.ANY)
    return pl.pallas_call(
        attend_kernel,
        in_specs=[smem, smem, vmem, vmem, vmem, hbm, hbm],
        out_specs=vmem,
        out_shape=jax.ShapeDtypeStruct((rows, heads, head_dim), jnp.bfloat16),
        scratch_shapes=[
            pltpu.VMEM((SLOTS, GROUP, seq, heads, head_dim), jnp.bfloat16),
            pltpu.VMEM((SLOTS, GROUP, seq, heads, head_dim), jnp.bfloat16),
            pltpu.VMEM((heads, seq * heads), jnp.int32),
            pltpu.SemaphoreType.DMA((2, SLOTS)),
        ],
        compiler_params=pltpu.CompilerParams(vmem_limit_bytes=40 * 2 ** 20),
        cost_estimate=pl.CostEstimate(flops=4 * rows * seq * heads * heads * head_dim, bytes_accessed=2 * rows * seq * heads * head_dim, transcendentals=0),
        name='attend',
    )(order, positions, q_rot, key_new, value_new, k_cache, v_cache)


def out_kernel(tile, a_ref, x_ref, b_ref, gain_ref, bias_ref, wr_ref, one_ref, two_ref, elig_ref, w_ref, mid_ref, h_ref, gate_ref, mid_all):
    i = pl.program_id(0)
    cols = pl.ds(pl.multiple_of(i * tile, tile), tile)
    mid = x_ref[:, cols].astype(jnp.float32) + jnp.dot(a_ref[...], w_ref[...], preferred_element_type=jnp.float32) + b_ref[:, cols].astype(jnp.float32)
    mid = mid.astype(jnp.bfloat16)
    mid_ref[...] = mid
    mid_all[:, cols] = mid

    @pl.when(i == pl.num_programs(0) - 1)
    def _():
        h_two = norm_rows(mid_all[...].astype(jnp.float32), gain_ref[...], bias_ref[...]).astype(jnp.bfloat16)
        h_ref[...] = h_two
        logits = jnp.dot(h_two, wr_ref[...], preferred_element_type=jnp.float32)
        ids = lax.broadcasted_iota(jnp.int32, logits.shape, 1)
        hit_one = ids == one_ref[...]
        hit_two = ids == two_ref[...]
        keep_one = elig_ref[...] == 1
        gates = []
        for keep, hit in ((keep_one, hit_one), (keep_one & jnp.logical_not(hit_one), hit_two)):
            masked = jnp.where(keep, logits, -jnp.inf)
            e_val = jnp.exp(masked - jnp.max(masked, axis=-1, keepdims=True))
            top = jnp.sum(jnp.where(hit, e_val, 0.0), axis=-1, keepdims=True)
            gates.append(top / jnp.sum(e_val, axis=-1, keepdims=True))
        lane = lax.broadcasted_iota(jnp.int32, gate_ref.shape, 1)
        gate_ref[...] = jnp.where(lane == 0, gates[0], jnp.where(lane == 1, gates[1], 0.0))


def out_call(attn_flat, tokens, b_out, gain, bias, w_router, expert_one, expert_two, eligible, w_out):
    rows, d_model = tokens.shape
    tile = 512
    whole = lambda shape: pl.BlockSpec(shape, lambda i: (0,) * len(shape))
    row = lambda t: t.reshape(1, -1)
    col = lambda t: t.reshape(-1, 1)
    return pl.pallas_call(
        lambda *refs: out_kernel(tile, *refs),
        grid=(d_model // tile,),
        in_specs=[whole(attn_flat.shape), whole(tokens.shape), whole((1, d_model)), whole((1, d_model)), whole((1, d_model)), whole(w_router.shape), whole((rows, 1)), whole((rows, 1)), whole(eligible.shape), pl.BlockSpec((w_out.shape[0], tile), lambda i: (0, i))],
        out_specs=[pl.BlockSpec((rows, tile), lambda i: (0, i)), whole((rows, d_model)), whole((rows, 128))],
        out_shape=[jax.ShapeDtypeStruct((rows, d_model), jnp.bfloat16), jax.ShapeDtypeStruct((rows, d_model), jnp.bfloat16), jax.ShapeDtypeStruct((rows, 128), jnp.float32)],
        scratch_shapes=[pltpu.VMEM((rows, d_model), jnp.bfloat16)],
        compiler_params=pltpu.CompilerParams(vmem_limit_bytes=40 * 2 ** 20),
        cost_estimate=pl.CostEstimate(flops=2 * rows * d_model * d_model, bytes_accessed=2 * d_model * d_model, transcendentals=0),
        name='project',
    )(attn_flat, tokens, row(b_out), row(gain), row(bias), w_router, col(expert_one), col(expert_two), eligible, w_out)


def attention_order(positions):
    ids = jnp.arange(positions.shape[0], dtype=jnp.int32)
    ahead = (positions[None, :] > positions[:, None]) | ((positions[None, :] == positions[:, None]) & (ids[None, :] < ids[:, None]))
    rank = jnp.sum(ahead.astype(jnp.int32), axis=1)
    return jnp.sum(jnp.where(rank[:, None] == ids[None, :], ids[:, None], 0), axis=0)


def expert_mlp(expert_in, w_gate, w_up, w_down):
    u_val = jnp.einsum('md,edf->emf', expert_in, w_gate, preferred_element_type=jnp.float32)
    v_val = jnp.einsum('md,edf->emf', expert_in, w_up, preferred_element_type=jnp.float32)
    z_val = (jax.nn.silu(u_val) * v_val).astype(jnp.bfloat16)
    return jnp.einsum('emf,efd->emd', z_val, w_down, preferred_element_type=jnp.float32).astype(jnp.bfloat16)


def solution(mesh):
    groups = mesh.shape['ep']

    def local_step(tokens, k_cache, v_cache, positions, expert_one, expert_two, eligible, ln1_gain, ln1_bias, w_query, b_query, w_key, b_key, w_value, b_value, w_out, b_out, ln2_gain, ln2_bias, w_router, w_gate, w_up, w_down):
        tok_count, seq_len, heads, head_dim = k_cache.shape
        d_model = tokens.shape[1]
        cos_tab, sin_tab = rope_tables(positions, head_dim)
        sign = jnp.where(jnp.arange(head_dim) < head_dim // 2, -1.0, 1.0)
        q_flat, k_flat, v_flat = qkv_call(tokens, ln1_gain, ln1_bias, cos_tab, sin_tab * sign[None, :], w_query, b_query, w_key, b_key, w_value, b_value)
        split = lambda t: t.reshape(tok_count, heads, head_dim)
        key_new, value_new = split(k_flat), split(v_flat)
        attn = attend_call(attention_order(positions), positions, split(q_flat), key_new, value_new, k_cache, v_cache)
        x_mid, h_two, gates = out_call(attn.reshape(tok_count, heads * head_dim), tokens, b_out, ln2_gain, ln2_bias, w_router, expert_one, expert_two, eligible, w_out)
        gate_one, gate_two = gates[:, 0], gates[:, 1]
        local_experts = w_gate.shape[0]
        all_rows = lax.all_gather(h_two, 'ep', axis=0, tiled=True)
        choices = lax.all_gather(jnp.stack([expert_one, expert_two], axis=1), 'ep', axis=0, tiled=True)
        expert_out = expert_mlp(all_rows, w_gate, w_up, w_down)
        local_ids = lax.axis_index('ep') * local_experts + jnp.arange(local_experts, dtype=jnp.int32)
        slots = []
        for slot in range(2):
            hit = choices[:, slot][None, :] == local_ids[:, None]
            slots.append(jnp.sum(jnp.where(hit[:, :, None], expert_out, 0), axis=0, dtype=jnp.bfloat16))
        by_owner = jnp.stack([x.reshape(groups, tok_count, d_model) for x in slots], axis=1).reshape(groups * 2 * tok_count, d_model)
        mine = lax.psum_scatter(by_owner, 'ep', scatter_dimension=0, tiled=True)
        out_one = mine[:tok_count]
        out_two = mine[tok_count:]
        y_sum = gate_one[:, None] * out_one.astype(jnp.float32) + gate_two[:, None] * out_two.astype(jnp.float32)
        tokens_out = (x_mid.astype(jnp.float32) + y_sum).astype(jnp.bfloat16)
        return tokens_out, key_new, value_new

    row_spec = P('ep', None)
    cache_spec = P('ep', None, None, None)
    vec_spec = P('ep')
    rep_one = P(None)
    rep_two = P(None, None)
    expert_spec = P('ep', None, None)
    in_specs = (row_spec, cache_spec, cache_spec, vec_spec, vec_spec, vec_spec, row_spec, rep_one, rep_one, rep_two, rep_one, rep_two, rep_one, rep_two, rep_one, rep_two, rep_one, rep_one, rep_one, rep_two, expert_spec, expert_spec, expert_spec)
    out_specs = (row_spec, expert_spec, expert_spec)
    return jax.shard_map(local_step, mesh=mesh, in_specs=in_specs, out_specs=out_specs, check_vma=False)
```

time: 446 us -> 392 us (0.88); the launches traced: 441 us -> 392 us
  matrix products: 225 us -> 86.4 us
  Pallas kernels: 0 us -> 99.7 us
  other arithmetic: 30.9 us -> 19.1 us
    dot_general x7 -> x0, matrix products: 139 us -> none  [the longest x1 42.2 us: attention_block(): jnp.einsum('tkgs,tskd->tkgd', p_cache, v_cache, preferred_element_type=jn...]
    pallas_call x0 -> x3, Pallas kernels: none -> 99.7 us  [the longest x1 47.8 us: attend_call(): pl.pallas_call(attend_kernel, in_specs=[smem, smem, vmem, vmem, vmem, hbm...]
    reshape x0 -> x10, local copies, waits for them, and re-layouts: none -> 7.21 us  [the longest x5 3.55 us: qkv_call(): row = lambda t: t.reshape(1, -1)]
    convert_element_type x13 -> x0, other arithmetic: 6.03 us -> none  [the longest x1 1.93 us: attention_block(): attn_vals.astype(jnp.bfloat16).reshape(tok_count, num_heads * head_dim)]
    convert_element_type x2 -> x0, local copies, waits for them, and re-layouts: 5.43 us -> none  [the longest x1 5.34 us: attention_block(): p_cache = (e_cache / denom_sum[..., None]).astype(jnp.bfloat16)]
    dot_general x2 -> x0, local copies, waits for them, and re-layouts: 4.75 us -> none  [the longest x1 4.7 us: attention_block(): jnp.einsum('tkgd,tskd->tkgs', q_grp, k_cache, preferred_element_type=jnp....]
where the time goes in v2:
time: 392 us
  waiting for transfers between devices  145 us (37%)
  Pallas kernels  99.7 us (25%)
  matrix products  86.4 us (22%)
  other arithmetic  19.1 us (5%)
  blocking collectives  14.8 us (4%)
  between operations  14.3 us (4%)
  local copies, waits for them, and re-layouts  12 us (3%)
    reduce_scatter x1, waiting for transfers between devices, local_step(): mine = lax.psum_scatter(by_owner, 'ep', scatter_dimension=0, tiled=True)  107 us
    dot_general x1, matrix products, expert_mlp(): jnp.einsum('emf,efd->emd', z_val, w_down, preferred_element_type=jnp.floa...  53.7 us
    pallas_call x1, Pallas kernels, attend_call(): pl.pallas_call(attend_kernel, in_specs=[smem, smem, vmem, vmem, vmem, hbm...  47.8 us
    all_gather x1, waiting for transfers between devices, local_step(): all_rows = lax.all_gather(h_two, 'ep', axis=0, tiled=True)  38.5 us
    pallas_call x1, Pallas kernels, qkv_call(): pl.pallas_call(qkv_kernel, grid=(cols // tile,), in_specs=[whole((rows, d...  36.1 us
    dot_general x1, matrix products, expert_mlp(): jnp.einsum('md,edf->emf', expert_in, w_up, preferred_element_type=jnp.flo...  16.4 us
    dot_general x1, matrix products, expert_mlp(): jnp.einsum('md,edf->emf', expert_in, w_gate, preferred_element_type=jnp.f...  16.3 us
    pallas_call x1, Pallas kernels, out_call(): pl.pallas_call(lambda *refs: out_kernel(tile, *refs), grid=(d_model // ti...  15.8 us
  transfers between devices with their start and end apart: 2, of which 2 were waited for; matrix products, arithmetic and copies ran while one was open for 0% of the time, Pallas kernels for 0%

profile of v2, /device:TPU:0, one launch (start us, length us, event | category | flops | bytes accessed | tf_op | source)
XLA Modules:
  0.0 391.8 jit_solution(2390177765529365776)
XLA Ops:
  7.2 0.0 all-gather.2.cloned.1.call-start
  7.2 0.9 convert_reduce_fusion
  8.1 0.7 convert_element_type.28
  8.8 0.1 select_reduce_fusion.2.order_ref
  8.9 0.7 reshape.125.gain_ref
  9.6 0.7 reshape.126.bias_ref
  10.3 0.7 reshape.127.bq_ref
  11.0 0.7 reshape.128.bk_ref
  11.8 0.7 reshape.129.bv_ref
  12.5 0.7 reshape.134.refs_2_
  13.2 0.7 reshape.135.refs_3_
  13.9 0.7 reshape.136.refs_4_
  14.6 0.8 copy.35.refs_6_
  15.4 0.8 copy.36.refs_7_
  16.1 0.8 copy.37.refs_8_
  16.9 1.4 copy.34.refs_5_
  18.3 0.1 broadcast_multiply_fusion
  18.4 0.3 sine_multiply_fusion
  18.7 0.0 copy-start
  18.7 1.2 copy-done
  20.0 36.1 %qkv.1 = (bf16[128,4096]{1,0:T(8,128)(2,1)S(1)}, bf16[128,4096]{1,0:T(8,128)(2,1)S(1)}, bf16[128,4096]{1,0:T(8,128)(2,1)S(1)}) custom-call(bf16[128,4096]{1,0:T(8,128)(2,1)S(1)} %copy-done, bf16[1,4096]{1,0:T(2,128)(2,1)S(1)} %reshape.125.gain_ref, bf16[1,4096]{1,0:T(2,128)(2,1)S(1)} %reshape.126.bias_ref, f32[128,128]{1,0:T(8,128)S(1)} %get-tuple-element.20.cos_ref, ...), custom_call_target="tpu_custom_call" | custom-call | flops 12884901888 | bytes 100663296 | tf_op jit(solution)/shard_map/qkv/pallas_call | solution.py:55
  56.0 0.2 copy.38
  56.3 0.2 copy.39
  56.5 0.0 copy-start.2
  56.5 0.2 copy.40
  56.8 0.0 copy-start.3
  56.8 0.0 copy-done.4
  56.8 0.0 copy-start.1
  56.8 47.8 %attend.1 = bf16[128,32,128]{2,1,0:T(8,128)(2,1)S(1)} custom-call(s32[128]{0:T(128)S(1)} %select_reduce_fusion.2.order_ref, s32[128]{0:T(128)S(1)} %copy-done.4, bf16[128,32,128]{2,1,0:T(8,128)(2,1)S(1)} %bitcast.49, bf16[128,32,128]{2,1,0:T(8,128)(2,1)S(1)} %bitcast.45, bf16[128,32,128]{2,1,0:T(8,128)(2,1)S(1)} %bitcast.47, ...), custom_call_target="tpu_custom_call" | custom-call | flops 4294967296 | bytes 67108864 | tf_op jit(solution)/shard_map/attend/pallas_call | solution.py:151
  104.6 0.0 copy-done.2
  104.7 0.0 copy-done.3
  104.7 0.5 copy.43
  105.1 0.0 copy-start.5
  105.1 0.0 copy-start.6
  105.2 15.8 %project.1 = (bf16[128,4096]{1,0:T(8,128)(2,1)S(1)}, bf16[128,4096]{1,0:T(8,128)(2,1)}, f32[128,128]{1,0:T(8,128)S(1)}) custom-call(bf16[128,4096]{1,0:T(8,128)(2,1)S(1)} %bitcast.51, bf16[128,4096]{1,0:T(8,128)(2,1)S(1)} %copy-done.1, bf16[1,4096]{1,0:T(2,128)(2,1)S(1)} %reshape.134.refs_2_, bf16[1,4096]{1,0:T(2,128)(2,1)S(1)} %reshape.135.refs_3_, ...), custom_call_target="tpu_custom_call" | custom-call | flops 4294967296 | bytes 33554432 | tf_op jit(solution)/shard_map/project/pallas_call | solution.py:201
  121.0 0.0 all-gather.2.cloned.1.call-update
  121.0 0.0 reduce-scatter.2.cloned.1.call-start
  121.1 14.8 %all_gather.6 = s32[1024,2]{0,1:T(2,128)S(1)} all-gather(s32[128,2]{0,1:T(2,128)S(1)} %pad_add_fusion), channel_id=1, replica_groups=mesh['ep'=8] {'ep'}, dimensions={0}, use_global_device_ids=true | all-gather | bytes 9216 | tf_op jit(solution)/shard_map/all_gather | solution.py:244
  135.9 0.1 broadcast_compare_fusion
  136.0 38.5 %all-gather.2.cloned.1.call-done = bf16[1024,4096]{1,0:T(8,128)(2,1)} async-done(((bf16[128,4096]{1,0:T(8,128)(2,1)}), bf16[1024,4096]{1,0:T(8,128)(2,1)}) %all-gather.2.cloned.1.call-update) | async-done | bytes 8388624 | tf_op jit(solution)/shard_map/all_gather | solution.py:243
  174.4 16.4 %fusion = f32[1024,2,688]{0,2,1:T(8,128)S(1)} fusion(bf16[2,4096,688]{1,2,0:T(8,128)(2,1)} %param.44, bf16[1024,4096]{1,0:T(8,128)(2,1)} %all-gather.2.cloned.1.call-done), kind=kOutput, calls=%fused_computation.4 | convolution fusion | flops 11542724608 | bytes 25296896 | tf_op jit(solution)/shard_map/md,edf->emf/dot_general | solution.py:223
  190.9 16.3 %fusion.4 = bf16[2,1024,688]{1,2,0:T(8,128)(2,1)} fusion(f32[1024,2,688]{0,2,1:T(8,128)S(1)} %fusion, bf16[2,4096,688]{1,2,0:T(8,128)(2,1)} %param.43, bf16[1024,4096]{1,0:T(8,128)(2,1)S(1)} %copy-done.7), kind=kOutput, calls=%fused_computation.9 | convolution fusion | flops 11551178752 | bytes 28114944 | tf_op jit(solution)/shard_map/md,edf->emf/dot_general | solution.py:222
  207.2 53.7 %select_reduce_fusion.1 = (bf16[1024,4096]{1,0:T(8,128)(2,1)}, bf16[1024,4096]{1,0:T(8,128)(2,1)}) fusion(pred[2,1024]{1,0:T(4,128)(4,1)S(1)} %get-tuple-element.24, pred[2,1024]{1,0:T(4,128)(4,1)S(1)} %get-tuple-element.23, bf16[2,1024,688]{1,2,0:T(8,128)(2,1)} %fusion.4, bf16[2,688,4096]{2,1,0:T(8,128)(2,1)} %param.45), kind=kOutput, calls=%fused_computation.2 | convolution fusion | flops 11576279040 | bytes 30871552 | tf_op jit(solution)/shard_map/emf,efd->emd/dot_general | solution.py:225
  260.9 13.7 %pad_maximum_fusion = bf16[8,2,128,4096]{3,2,1,0:T(8,128)(2,1)} fusion(bf16[8,1,128,4096]{3,2,1,0:T(8,128)(2,1)} %bitcast.57, bf16[8,1,128,4096]{3,2,1,0:T(8,128)(2,1)} %bitcast.56), kind=kLoop, calls=%fused_computation | loop fusion | flops 8388608 | bytes 33554432 | tf_op jit(solution)/shard_map/stack | solution.py:251
  274.6 0.0 reduce-scatter.2.cloned.1.call-update
  274.7 0.2 slice_reduce_fusion.1
  274.8 106.9 %reduce-scatter.2.cloned.1.call-done = bf16[256,4096]{1,0:T(8,128)(2,1)} async-done(((bf16[2048,4096]{1,0:T(8,128)(2,1)}), bf16[256,4096]{1,0:T(8,128)(2,1)}) %reduce-scatter.2.cloned.1.call-update) | async-done | bytes 2097168 | tf_op jit(solution)/shard_map/reduce_scatter | solution.py:252
  381.7 3.2 add_convert_fusion
  (11 shorter events, 0.0 us)
Async XLA Ops:
  7.2 167.3 %all-gather.2.cloned.1.call-start = ((), (), s32[]{:S(2)}) async-start(), calls=%async_computation.1 | async-start | bytes 9437184 | tf_op jit(solution)/shard_map/all_gather | solution.py:243
  18.7 1.2 copy-start
  19.9 36.9 %copy-start.4 = (s32[128]{0:T(128)S(1)}, s32[128]{0:T(128)}, u32[]{:S(2)}) copy-start(s32[128]{0:T(128)} %pos_ref.1) | copy-start | bytes 1540
  56.5 48.1 %copy-start.2 = (bf16[16,8,32,128]{3,2,1,0:T(8,128)(2,1)}, bf16[16,8,32,128]{3,2,1,0:T(8,128)(2,1)S(1)}, u32[]{:S(2)}) copy-start(bf16[16,8,32,128]{3,2,1,0:T(8,128)(2,1)S(1)} %copy.39) | copy-start | bytes 3145732
  56.8 47.9 %copy-start.3 = (bf16[16,8,32,128]{3,2,1,0:T(8,128)(2,1)}, bf16[16,8,32,128]{3,2,1,0:T(8,128)(2,1)S(1)}, u32[]{:S(2)}) copy-start(bf16[16,8,32,128]{3,2,1,0:T(8,128)(2,1)S(1)} %copy.40) | copy-start | bytes 3145732
  56.8 48.3 %copy-start.1 = (bf16[128,4096]{1,0:T(8,128)(2,1)S(1)}, bf16[128,4096]{1,0:T(8,128)(2,1)}, u32[]{:S(2)}) copy-start(bf16[128,4096]{1,0:T(8,128)(2,1)} %refs_1_.1) | copy-start | bytes 3145732
  105.1 15.9 %copy-start.5 = (s32[128]{0:T(128)S(1)}, s32[128]{0:T(128)}, u32[]{:S(2)}) copy-start(s32[128]{0:T(128)} %param.27) | copy-start | bytes 1540
  105.1 15.9 %copy-start.6 = (s32[128]{0:T(128)S(1)}, s32[128]{0:T(128)}, u32[]{:S(2)}) copy-start(s32[128]{0:T(128)} %param.28) | copy-start | bytes 1540
  121.0 260.7 %reduce-scatter.2.cloned.1.call-start = ((), (), s32[]{:S(2)}) async-start(), calls=%async_computation.2 | async-start | bytes 18874368 | tf_op jit(solution)/shard_map/reduce_scatter | solution.py:252
  174.4 16.4 %copy-start.7 = (bf16[1024,4096]{1,0:T(8,128)(2,1)S(1)}, bf16[1024,4096]{1,0:T(8,128)(2,1)}, u32[]{:S(2)}) copy-start(bf16[1024,4096]{1,0:T(8,128)(2,1)} %all-gather.2.cloned.1.call-done) | copy-start | bytes 25165828
Sparse Core Ops, SparseCore 0:
  121.1 53.2 all-gather.1
  274.8 106.9 reduce-scatter.1

commit v3 on v2

--- a/solution.py
+++ b/solution.py
@@ -24,45 +24,52 @@
     return centered * lax.rsqrt(var_val + LN_EPS) * gain.astype(jnp.float32) + bias.astype(jnp.float32)
 
 
-def qkv_kernel(x_ref, gain_ref, bias_ref, cos_ref, sin_ref, wq_ref, wk_ref, wv_ref, bq_ref, bk_ref, bv_ref, q_ref, k_ref, v_ref, h_ref):
+def row_stack(vectors):
+    which = lax.broadcasted_iota(jnp.int32, (len(vectors), vectors[0].shape[0]), 0)
+    out = jnp.zeros((len(vectors), vectors[0].shape[0]), vectors[0].dtype)
+    for n, vec in enumerate(vectors):
+        out = jnp.where(which == n, vec[None, :], out)
+    return out
+
+
+def qkv_kernel(x_ref, norm_ref, cos_ref, sin_ref, wq_ref, wk_ref, wv_ref, b_ref, q_ref, k_ref, v_ref, h_ref):
     @pl.when(pl.program_id(0) == 0)
     def _():
-        h_ref[...] = norm_rows(x_ref[...].astype(jnp.float32), gain_ref[...], bias_ref[...]).astype(jnp.bfloat16)
+        h_ref[...] = norm_rows(x_ref[...].astype(jnp.float32), norm_ref[0:1], norm_ref[1:2]).astype(jnp.bfloat16)
 
     h_val = h_ref[...]
     head_dim = cos_ref.shape[1]
     cos_tab, sin_tab = cos_ref[...], sin_ref[...]
-    for w_ref, b_ref, o_ref in ((wq_ref, bq_ref, q_ref), (wk_ref, bk_ref, k_ref)):
-        lin = jnp.dot(h_val, w_ref[...], preferred_element_type=jnp.float32) + b_ref[...].astype(jnp.float32)
+    for w_ref, n, o_ref in ((wq_ref, 2, q_ref), (wk_ref, 3, k_ref)):
+        lin = jnp.dot(h_val, w_ref[...], preferred_element_type=jnp.float32) + b_ref[n:n + 1].astype(jnp.float32)
         for c in range(lin.shape[1] // head_dim):
             part = lin[:, c * head_dim:(c + 1) * head_dim]
             rot = part * cos_tab + pltpu.roll(part, head_dim // 2, 1) * sin_tab
             o_ref[:, c * head_dim:(c + 1) * head_dim] = rot.astype(jnp.bfloat16)
-    lin = jnp.dot(h_val, wv_ref[...], preferred_element_type=jnp.float32) + bv_ref[...].astype(jnp.float32)
+    lin = jnp.dot(h_val, wv_ref[...], preferred_element_type=jnp.float32) + b_ref[4:5].astype(jnp.float32)
     v_ref[...] = lin.astype(jnp.bfloat16)
 
 
-def qkv_call(tokens, gain, bias, cos_tab, sin_signed, w_query, b_query, w_key, b_key, w_value, b_value):
+def qkv_call(tokens, vectors, cos_tab, sin_signed, w_query, w_key, w_value):
     rows, d_model = tokens.shape
     cols = w_query.shape[1]
     tile = 256
     whole = lambda shape: pl.BlockSpec(shape, lambda i: (0,) * len(shape))
     wide = pl.BlockSpec((d_model, tile), lambda i: (0, i))
-    slim = pl.BlockSpec((1, tile), lambda i: (0, i))
+    slim = pl.BlockSpec((8, tile), lambda i: (0, i))
     out = pl.BlockSpec((rows, tile), lambda i: (0, i))
     shape = jax.ShapeDtypeStruct((rows, cols), jnp.bfloat16)
-    row = lambda t: t.reshape(1, -1)
     return pl.pallas_call(
         qkv_kernel,
         grid=(cols // tile,),
-        in_specs=[whole((rows, d_model)), whole((1, d_model)), whole((1, d_model)), whole(cos_tab.shape), whole(cos_tab.shape), wide, wide, wide, slim, slim, slim],
+        in_specs=[whole((rows, d_model)), whole((8, d_model)), whole(cos_tab.shape), whole(cos_tab.shape), wide, wide, wide, slim],
         out_specs=[out, out, out],
         out_shape=[shape, shape, shape],
         scratch_shapes=[pltpu.VMEM((rows, d_model), jnp.bfloat16)],
         compiler_params=pltpu.CompilerParams(vmem_limit_bytes=40 * 2 ** 20),
         cost_estimate=pl.CostEstimate(flops=6 * rows * d_model * cols, bytes_accessed=6 * d_model * cols, transcendentals=0),
         name='qkv',
-    )(tokens, row(gain), row(bias), cos_tab, sin_signed, w_query, w_key, w_value, row(b_query), row(b_key), row(b_value))
+    )(tokens, vectors, cos_tab, sin_signed, w_query, w_key, w_value, vectors)
 
 
 GROUP = 4
@@ -165,23 +172,27 @@
     )(order, positions, q_rot, key_new, value_new, k_cache, v_cache)
 
 
-def out_kernel(tile, a_ref, x_ref, b_ref, gain_ref, bias_ref, wr_ref, one_ref, two_ref, elig_ref, w_ref, mid_ref, h_ref, gate_ref, mid_all):
+def out_kernel(tile, a_ref, x_ref, vec_ref, wr_ref, pick_ref, w_ref, mid_ref, h_ref, gate_ref, mid_all):
     i = pl.program_id(0)
     cols = pl.ds(pl.multiple_of(i * tile, tile), tile)
-    mid = x_ref[:, cols].astype(jnp.float32) + jnp.dot(a_ref[...], w_ref[...], preferred_element_type=jnp.float32) + b_ref[:, cols].astype(jnp.float32)
+    mid = x_ref[:, cols].astype(jnp.float32) + jnp.dot(a_ref[...], w_ref[...], preferred_element_type=jnp.float32) + vec_ref[5:6, cols].astype(jnp.float32)
     mid = mid.astype(jnp.bfloat16)
     mid_ref[...] = mid
     mid_all[:, cols] = mid
 
     @pl.when(i == pl.num_programs(0) - 1)
     def _():
-        h_two = norm_rows(mid_all[...].astype(jnp.float32), gain_ref[...], bias_ref[...]).astype(jnp.bfloat16)
-        h_ref[...] = h_two
-        logits = jnp.dot(h_two, wr_ref[...], preferred_element_type=jnp.float32)
-        ids = lax.broadcasted_iota(jnp.int32, logits.shape, 1)
-        hit_one = ids == one_ref[...]
-        hit_two = ids == two_ref[...]
-        keep_one = elig_ref[...] == 1
+        h_two = norm_rows(mid_all[...].astype(jnp.float32), vec_ref[6:7], vec_ref[7:8]).astype(jnp.bfloat16)
+        lanes = lax.broadcasted_iota(jnp.int32, (h_two.shape[0], 128), 1)
+        pick_val = jnp.transpose(pick_ref[...].astype(jnp.float32))
+        picks = jnp.where(lanes < 2, pick_val, 0.0)
+        h_ref[:, :h_two.shape[1]] = h_two
+        h_ref[:, h_two.shape[1]:] = picks.astype(jnp.bfloat16)
+        logits = lax.dot_general(h_two, wr_ref[...], (((1,), (1,)), ((), ())), preferred_element_type=jnp.float32)
+        ids = lax.broadcasted_iota(jnp.int32, logits.shape, 1).astype(jnp.float32)
+        hit_one = ids == pick_val[:, 0:1]
+        hit_two = ids == pick_val[:, 1:2]
+        keep_one = pick_val[:, 2:2 + logits.shape[1]] == 1.0
         gates = []
         for keep, hit in ((keep_one, hit_one), (keep_one & jnp.logical_not(hit_one), hit_two)):
             masked = jnp.where(keep, logits, -jnp.inf)
@@ -192,23 +203,21 @@
         gate_ref[...] = jnp.where(lane == 0, gates[0], jnp.where(lane == 1, gates[1], 0.0))
 
 
-def out_call(attn_flat, tokens, b_out, gain, bias, w_router, expert_one, expert_two, eligible, w_out):
+def out_call(attn_flat, tokens, vectors, w_router, picks, w_out):
     rows, d_model = tokens.shape
     tile = 512
     whole = lambda shape: pl.BlockSpec(shape, lambda i: (0,) * len(shape))
-    row = lambda t: t.reshape(1, -1)
-    col = lambda t: t.reshape(-1, 1)
     return pl.pallas_call(
         lambda *refs: out_kernel(tile, *refs),
         grid=(d_model // tile,),
-        in_specs=[whole(attn_flat.shape), whole(tokens.shape), whole((1, d_model)), whole((1, d_model)), whole((1, d_model)), whole(w_router.shape), whole((rows, 1)), whole((rows, 1)), whole(eligible.shape), pl.BlockSpec((w_out.shape[0], tile), lambda i: (0, i))],
-        out_specs=[pl.BlockSpec((rows, tile), lambda i: (0, i)), whole((rows, d_model)), whole((rows, 128))],
-        out_shape=[jax.ShapeDtypeStruct((rows, d_model), jnp.bfloat16), jax.ShapeDtypeStruct((rows, d_model), jnp.bfloat16), jax.ShapeDtypeStruct((rows, 128), jnp.float32)],
+        in_specs=[whole(attn_flat.shape), whole(tokens.shape), whole((8, d_model)), whole(w_router.shape), whole(picks.shape), pl.BlockSpec((w_out.shape[0], tile), lambda i: (0, i))],
+        out_specs=[pl.BlockSpec((rows, tile), lambda i: (0, i)), whole((rows, d_model + 128)), whole((rows, 128))],
+        out_shape=[jax.ShapeDtypeStruct((rows, d_model), jnp.bfloat16), jax.ShapeDtypeStruct((rows, d_model + 128), jnp.bfloat16), jax.ShapeDtypeStruct((rows, 128), jnp.float32)],
         scratch_shapes=[pltpu.VMEM((rows, d_model), jnp.bfloat16)],
         compiler_params=pltpu.CompilerParams(vmem_limit_bytes=40 * 2 ** 20),
         cost_estimate=pl.CostEstimate(flops=2 * rows * d_model * d_model, bytes_accessed=2 * d_model * d_model, transcendentals=0),
         name='project',
-    )(attn_flat, tokens, row(b_out), row(gain), row(bias), w_router, col(expert_one), col(expert_two), eligible, w_out)
+    )(attn_flat, tokens, vectors, w_router, picks, w_out)
 
 
 def attention_order(positions):
@@ -218,42 +227,276 @@
     return jnp.sum(jnp.where(rank[:, None] == ids[None, :], ids[:, None], 0), axis=0)
 
 
-def expert_mlp(expert_in, w_gate, w_up, w_down):
-    u_val = jnp.einsum('md,edf->emf', expert_in, w_gate, preferred_element_type=jnp.float32)
-    v_val = jnp.einsum('md,edf->emf', expert_in, w_up, preferred_element_type=jnp.float32)
-    z_val = (jax.nn.silu(u_val) * v_val).astype(jnp.bfloat16)
-    return jnp.einsum('emf,efd->emd', z_val, w_down, preferred_element_type=jnp.float32).astype(jnp.bfloat16)
+def moe_kernel(h_in, x_hbm, gate_ref, wg_hbm, wu_hbm, wd_hbm, out_hbm, hb, wg, wu, wd, xblk, zt_ref, z_ref, acc, stg, d2d, p1a, p1b, p2a, p2b, wsem, xsem, gsend, grecv, dsend, drecv, rsend, rrecv, credit):
+    me = lax.axis_index('ep')
+    core = lax.rem(me, 2)
+    x_pos = lax.rem(lax.div(me, 2), 2)
+    y_pos = lax.div(me, 4)
+    partner = me + 1 - 2 * core
+    xn = me + 2 - 4 * x_pos
+    yn = me + 4 - 8 * y_pos
+    rows = h_in.shape[0]
+    half_rows = rows // 2
+    d_model = x_hbm.shape[1]
+    half = d_model // 2
+    ff = wd.shape[1]
+    tile = 512
+    zt_ref[...] = jnp.zeros_like(zt_ref)
+    mesh_id = pl.DeviceIdType.MESH
+
+    def remote(src, dst, send, recv, dev):
+        return pltpu.make_async_remote_copy(src_ref=src, dst_ref=dst, send_sem=send, recv_sem=recv, device_id=(dev,), device_id_type=mesh_id)
+
+    low, high = pl.ds(0, half_rows), pl.ds(half_rows, half_rows)
+    gather = [
+        remote(h_in, hb.at[1], gsend.at[0], grecv.at[0], partner),
+        remote(h_in, hb.at[2], gsend.at[1], grecv.at[1], xn),
+        remote(h_in, hb.at[4], gsend.at[2], grecv.at[2], yn),
+        remote(hb.at[2], hb.at[3], gsend.at[3], grecv.at[3], partner),
+        remote(hb.at[2, low], hb.at[6, low], gsend.at[4], grecv.at[4], yn),
+        remote(hb.at[4], hb.at[5], gsend.at[5], grecv.at[5], partner),
+        remote(hb.at[4, high], hb.at[6, high], gsend.at[6], grecv.at[6], xn),
+        remote(hb.at[6, low], hb.at[7, low], gsend.at[7], grecv.at[7], partner),
+        remote(hb.at[6, high], hb.at[7, high], gsend.at[8], grecv.at[8], partner),
+    ]
+    scatter = [
+        remote(acc.at[1, 0], p1a.at[0], rsend.at[0], rrecv.at[0], xn),
+        remote(acc.at[2, 1], p1b.at[0], rsend.at[1], rrecv.at[1], yn),
+        remote(acc.at[3, 0], p1a.at[1], rsend.at[2], rrecv.at[2], xn),
+        remote(acc.at[3, 1], p1b.at[1], rsend.at[3], rrecv.at[3], yn),
+        remote(acc.at[1, 1], p2b, rsend.at[4], rrecv.at[4], xn),
+        remote(acc.at[2, 0], p2a, rsend.at[5], rrecv.at[5], yn),
+    ]
+
+    def weight(e):
+        return [pltpu.make_async_copy(hbm.at[e], buf.at[e], wsem.at[n, e]) for n, (hbm, buf) in enumerate(((wg_hbm, wg), (wu_hbm, wu), (wd_hbm, wd)))]
+
+    barrier = pltpu.get_barrier_semaphore()
+    for dev in (partner, xn, yn):
+        pl.semaphore_signal(barrier, inc=1, device_id=(dev,), device_id_type=mesh_id)
+    for e in range(2):
+        for copy in weight(e):
+            copy.start()
+    pl.semaphore_wait(barrier, 3)
+    for i in (1, 2, 0):
+        gather[i].start()
+
+    def load(first, second):
+        copies = [pltpu.make_async_copy(src, xblk.at[pl.ds(n * rows, rows)], xsem.at[n]) for n, src in enumerate((first, second))]
+        for copy in copies:
+            copy.start()
+        for copy in copies:
+            copy.wait()
+
+    def merge(dst, src):
+        @pl.loop(0, 2 * (rows // 32))
+        def _(i):
+            slot = lax.div(i, rows // 32)
+            at = pl.ds(pl.multiple_of(lax.rem(i, rows // 32) * 32, 32), 32)
+            dst[slot, at] = dst[slot, at] + src[slot, at]
+
+    def shared(r, part):
+        return remote(stg.at[part], d2d.at[lax.rem(r, 2), part], dsend.at[part], drecv.at[r, part], partner)
+
+    @pl.loop(0, 4)
+    def _(r):
+        @pl.when(r == 0)
+        def _():
+            gather[0].wait_recv()
+            load(h_in, hb.at[1])
+
+        @pl.when(r == 1)
+        def _():
+            gather[1].wait_recv()
+            gather[3].start()
+            gather[4].start()
+            gather[2].wait_recv()
+            gather[5].start()
+            gather[6].start()
+            gather[3].wait_recv()
+            load(hb.at[2], hb.at[3])
+
+        @pl.when(r == 2)
+        def _():
+            gather[5].wait_recv()
+            load(hb.at[4], hb.at[5])
+
+        @pl.when(r == 3)
+        def _():
+            gather[7].wait_recv()
+            gather[8].wait_recv()
+            load(hb.at[6], hb.at[7])
+
+        @pl.loop(0, 2)
+        def _(e):
+            @pl.when(r == 0)
+            def _():
+                for copy in weight(e)[:2]:
+                    copy.wait()
+
+            x_val = xblk[:, :d_model]
+            dims = (((1,), (1,)), ((), ()))
+            u_val = lax.dot_general(wg[e], x_val, dims, preferred_element_type=jnp.float32)
+            v_val = lax.dot_general(wu[e], x_val, dims, preferred_element_type=jnp.float32)
+            zt_ref[:ff] = (jax.nn.silu(u_val) * v_val).astype(jnp.bfloat16)
+            z_ref[e] = jnp.transpose(zt_ref[...])
+
+        @pl.when(r == 0)
+        def _():
+            for e in range(2):
+                weight(e)[2].wait()
+
+        @pl.when(r == 2)
+        def _():
+            gather[4].wait_recv()
+            gather[7].start()
+            gather[6].wait_recv()
+            gather[8].start()
+
+        @pl.loop(0, 2)
+        def _(part):
+            @pl.when(r > 0)
+            def _():
+                shared(r - 1, part).wait_send()
+
+            @pl.loop(0, half // tile)
+            def _(n):
+                wide = pl.ds(pl.multiple_of(part * half + n * tile, tile), tile)
+                slim = pl.ds(pl.multiple_of(n * tile, tile), tile)
+                first = jnp.dot(z_ref[0, :, :ff], wd[0, :, wide], preferred_element_type=jnp.float32)
+                second = jnp.dot(z_ref[1, :, :ff], wd[1, :, wide], preferred_element_type=jnp.float32)
+                for slot in range(2):
+                    choice = xblk[:, d_model:][:, slot:slot + 1].astype(jnp.float32)
+                    lead = (2 * me).astype(jnp.float32)
+                    val = jnp.where(choice == lead, first, jnp.where(choice == lead + 1.0, second, 0.0)).astype(jnp.bfloat16)
+                    acc[r, part, slot, :, slim] = val[:rows]
+                    stg[part, slot, :, slim] = val[rows:]
+
+            @pl.when((r >= 2) & (part == 0))
+            def _():
+                pl.semaphore_wait(credit, 1)
+
+            shared(r, part).start()
+
+        @pl.loop(0, 2)
+        def _(part):
+            shared(r, part).wait_recv()
+            merge(acc.at[r, part], d2d.at[lax.rem(r, 2), part])
+
+            @pl.when((r == 1) & (part == 0))
+            def _():
+                scatter[0].start()
+
+            @pl.when((r == 2) & (part == 1))
+            def _():
+                scatter[1].start()
+
+            @pl.when((r == 3) & (part == 0))
+            def _():
+                scatter[2].start()
+
+            @pl.when((r == 3) & (part == 1))
+            def _():
+                scatter[3].start()
+
+        @pl.when(r < 2)
+        def _():
+            pl.semaphore_signal(credit, inc=1, device_id=(partner,), device_id_type=mesh_id)
+
+    x_copy = pltpu.make_async_copy(x_hbm, xblk.at[pl.ds(0, rows), pl.ds(0, d_model)], xsem.at[0])
+    x_copy.start()
+    scatter[2].wait_recv()
+    merge(acc.at[2, 0], p1a.at[1])
+    scatter[5].start()
+    scatter[3].wait_recv()
+    merge(acc.at[1, 1], p1b.at[1])
+    scatter[4].start()
+    scatter[0].wait_recv()
+    merge(acc.at[0, 0], p1a.at[0])
+    scatter[1].wait_recv()
+    merge(acc.at[0, 1], p1b.at[0])
+    x_copy.wait()
+    result = xblk.at[pl.ds(rows, rows), pl.ds(0, d_model)]
+    for part, last, buf in ((0, 5, p2a), (1, 4, p2b)):
+        scatter[last].wait_recv()
+
+        @pl.loop(0, rows // 16)
+        def _(i, part=part, buf=buf):
+            at = pl.ds(pl.multiple_of(i * 16, 16), 16)
+            wide = pl.ds(part * half, half)
+            gates = gate_ref[at]
+            y_val = [(acc[0, part, slot, at] + buf[slot, at]).astype(jnp.float32) * gates[:, slot:slot + 1] for slot in range(2)]
+            result[at, wide] = (xblk[at, wide].astype(jnp.float32) + (y_val[0] + y_val[1])).astype(jnp.bfloat16)
+
+    out_copy = pltpu.make_async_copy(result, out_hbm, xsem.at[1])
+    out_copy.start()
+    for copy in gather + scatter:
+        copy.wait_send()
+    for part in range(2):
+        shared(3, part).wait_send()
+    out_copy.wait()
+
+
+def moe_call(h_ext, x_mid, gates, w_gate, w_up, w_down):
+    rows, d_model = x_mid.shape
+    half = d_model // 2
+    ff = w_gate.shape[2]
+    ff_pad = pl.cdiv(ff, 128) * 128
+    width = h_ext.shape[1]
+    vmem = pl.BlockSpec(memory_space=pltpu.VMEM)
+    hbm = pl.BlockSpec(memory_space=pl.ANY)
+    bf = jnp.bfloat16
+    dma = pltpu.SemaphoreType.DMA
+    out, _ = pl.pallas_call(
+        moe_kernel,
+        in_specs=[hbm, hbm, vmem, hbm, hbm, hbm],
+        out_specs=[hbm, hbm],
+        out_shape=[jax.ShapeDtypeStruct((rows, d_model), bf), jax.ShapeDtypeStruct((8, rows, width), bf)],
+        scratch_shapes=[
+            pltpu.VMEM((2, ff, d_model), bf),
+            pltpu.VMEM((2, ff, d_model), bf),
+            pltpu.VMEM((2, ff, d_model), bf),
+            pltpu.VMEM((2 * rows, width), bf),
+            pltpu.VMEM((ff_pad, 2 * rows), bf),
+            pltpu.VMEM((2, 2 * rows, ff_pad), bf),
+            pltpu.VMEM((4, 2, 2, rows, half), bf),
+            pltpu.VMEM((2, 2, rows, half), bf),
+            pltpu.VMEM((2, 2, 2, rows, half), bf),
+            pltpu.VMEM((2, 2, rows, half), bf),
+            pltpu.VMEM((2, 2, rows, half), bf),
+            pltpu.VMEM((2, rows, half), bf),
+            pltpu.VMEM((2, rows, half), bf),
+            dma((3, 2)),
+            dma((2,)),
+            dma((9,)),
+            dma((9,)),
+            dma((2,)),
+            dma((4, 2)),
+            dma((6,)),
+            dma((6,)),
+            pltpu.SemaphoreType.REGULAR,
+        ],
+        compiler_params=pltpu.CompilerParams(vmem_limit_bytes=67043328, collective_id=0, has_side_effects=True),
+        name='moe',
+    )(h_ext, x_mid, gates, jnp.swapaxes(w_gate, 1, 2), jnp.swapaxes(w_up, 1, 2), w_down)
+    return out
 
 
 def solution(mesh):
-    groups = mesh.shape['ep']
-
     def local_step(tokens, k_cache, v_cache, positions, expert_one, expert_two, eligible, ln1_gain, ln1_bias, w_query, b_query, w_key, b_key, w_value, b_value, w_out, b_out, ln2_gain, ln2_bias, w_router, w_gate, w_up, w_down):
         tok_count, seq_len, heads, head_dim = k_cache.shape
         d_model = tokens.shape[1]
         cos_tab, sin_tab = rope_tables(positions, head_dim)
         sign = jnp.where(jnp.arange(head_dim) < head_dim // 2, -1.0, 1.0)
-        q_flat, k_flat, v_flat = qkv_call(tokens, ln1_gain, ln1_bias, cos_tab, sin_tab * sign[None, :], w_query, b_query, w_key, b_key, w_value, b_value)
+        vectors = row_stack([ln1_gain, ln1_bias, b_query, b_key, b_value, b_out, ln2_gain, ln2_bias])
+        which = lax.broadcasted_iota(jnp.int32, (128, tok_count), 0)
+        picks = jnp.where(which == 0, expert_one[None, :], jnp.where(which == 1, expert_two[None, :], jnp.pad(eligible.T, ((2, 110), (0, 0)))))
+        q_flat, k_flat, v_flat = qkv_call(tokens, vectors, cos_tab, sin_tab * sign[None, :], w_query, w_key, w_value)
         split = lambda t: t.reshape(tok_count, heads, head_dim)
         key_new, value_new = split(k_flat), split(v_flat)
         attn = attend_call(attention_order(positions), positions, split(q_flat), key_new, value_new, k_cache, v_cache)
-        x_mid, h_two, gates = out_call(attn.reshape(tok_count, heads * head_dim), tokens, b_out, ln2_gain, ln2_bias, w_router, expert_one, expert_two, eligible, w_out)
-        gate_one, gate_two = gates[:, 0], gates[:, 1]
-        local_experts = w_gate.shape[0]
-        all_rows = lax.all_gather(h_two, 'ep', axis=0, tiled=True)
-        choices = lax.all_gather(jnp.stack([expert_one, expert_two], axis=1), 'ep', axis=0, tiled=True)
-        expert_out = expert_mlp(all_rows, w_gate, w_up, w_down)
-        local_ids = lax.axis_index('ep') * local_experts + jnp.arange(local_experts, dtype=jnp.int32)
-        slots = []
-        for slot in range(2):
-            hit = choices[:, slot][None, :] == local_ids[:, None]
-            slots.append(jnp.sum(jnp.where(hit[:, :, None], expert_out, 0), axis=0, dtype=jnp.bfloat16))
-        by_owner = jnp.stack([x.reshape(groups, tok_count, d_model) for x in slots], axis=1).reshape(groups * 2 * tok_count, d_model)
-        mine = lax.psum_scatter(by_owner, 'ep', scatter_dimension=0, tiled=True)
-        out_one = mine[:tok_count]
-        out_two = mine[tok_count:]
-        y_sum = gate_one[:, None] * out_one.astype(jnp.float32) + gate_two[:, None] * out_two.astype(jnp.float32)
-        tokens_out = (x_mid.astype(jnp.float32) + y_sum).astype(jnp.bfloat16)
+        x_mid, h_ext, gates = out_call(attn.reshape(tok_count, heads * head_dim), tokens, vectors, w_router.T, picks, w_out)
+        tokens_out = moe_call(h_ext, x_mid, gates, w_gate, w_up, w_down)
         return tokens_out, key_new, value_new
 
     row_spec = P('ep', None)

time: 392 us -> 249 us (0.64)
  waiting for transfers between devices: 145 us -> 0 us
  Pallas kernels: 99.7 us -> 236 us
  matrix products: 86.4 us -> 0 us
  other arithmetic: 19.1 us -> 3.84 us
  blocking collectives: 14.8 us -> 0 us
  between operations: 14.3 us -> 0.85 us
  local copies, waits for them, and re-layouts: 12 us -> 7.37 us
    pallas_call x0 -> x1, Pallas kernels: none -> 137 us  [moe_call(): pl.pallas_call(moe_kernel, in_specs=[hbm, hbm, vmem, hbm, hbm, hbm], out_...]
    reduce_scatter x1 -> x0, waiting for transfers between devices: 107 us -> none  [local_step(): mine = lax.psum_scatter(by_owner, 'ep', scatter_dimension=0, tiled=True)]
    dot_general x3 -> x0, matrix products: 86.4 us -> none  [the longest x1 53.7 us: expert_mlp(): jnp.einsum('emf,efd->emd', z_val, w_down, preferred_element_type=jnp.floa...]
    all_gather x1 -> x0, waiting for transfers between devices: 38.5 us -> none  [local_step(): all_rows = lax.all_gather(h_two, 'ep', axis=0, tiled=True)]
    all_gather x1 -> x0, blocking collectives: 14.8 us -> none  [local_step(): lax.all_gather(jnp.stack([expert_one, expert_two], axis=1), 'ep', axis=0,...]
    another operation x2 -> x0, other arithmetic: 13.8 us -> none  [the longest x1 13.7 us: local_step(): jnp.stack([x.reshape(groups, tok_count, d_model) for x in slots], axis=1)]
    reshape x10 -> x0, local copies, waits for them, and re-layouts: 7.21 us -> none  [the longest x5 3.55 us: qkv_call(): row = lambda t: t.reshape(1, -1)]
  transfers between devices with their start and end apart: 2 -> 0, of which waited for: 2 -> 0; matrix products, arithmetic and copies ran while one was open for 0% -> 0% of each run, Pallas kernels for 0% -> 0%
where the time goes in v3:
time: 249 us; the launch traced here: 248 us
  Pallas kernels  236 us (95%)
  local copies, waits for them, and re-layouts  7.37 us (3%)
  other arithmetic  3.84 us (2%)
    pallas_call x1, Pallas kernels, moe_call(): pl.pallas_call(moe_kernel, in_specs=[hbm, hbm, vmem, hbm, hbm, hbm], out_...  137 us
    pallas_call x1, Pallas kernels, attend_call(): pl.pallas_call(attend_kernel, in_specs=[smem, smem, vmem, vmem, vmem, hbm...  48.3 us
    pallas_call x1, Pallas kernels, qkv_call(): pl.pallas_call(qkv_kernel, grid=(cols // tile,), in_specs=[whole((rows, d...  36 us
    pallas_call x1, Pallas kernels, out_call(): pl.pallas_call(lambda *refs: out_kernel(tile, *refs), grid=(d_model // ti...  15 us
    unnamed x23, local copies, waits for them, and re-layouts  7.37 us

profile of v3, /device:TPU:0, one launch (start us, length us, event | category | flops | bytes accessed | tf_op | source)
XLA Modules:
  0.0 247.9 jit_solution(4120136035471658660)
XLA Ops:
  0.6 0.9 convert_reduce_fusion
  1.5 0.1 select_reduce_fusion.order_ref
  1.6 0.7 convert_element_type.7
  2.4 0.9 select_select_fusion.1.norm_ref.b_ref.refs_2_
  3.3 0.8 select_select_fusion.refs_4_
  4.1 0.1 broadcast_multiply_fusion
  4.2 0.3 sine_multiply_fusion
  4.5 0.0 copy-start
  4.5 1.2 copy-done
  5.8 0.0 copy-start.8
  5.8 36.0 %qkv.1 = (bf16[128,4096]{1,0:T(8,128)(2,1)S(1)}, bf16[128,4096]{1,0:T(8,128)(2,1)S(1)}, bf16[128,4096]{1,0:T(8,128)(2,1)S(1)}) custom-call(bf16[128,4096]{1,0:T(8,128)(2,1)S(1)} %copy-done, bf16[8,4096]{1,0:T(8,128)(2,1)S(1)} %select_select_fusion.1.norm_ref.b_ref.refs_2_, f32[128,128]{1,0:T(8,128)S(1)} %get-tuple-element.18.cos_ref, ...), custom_call_target="tpu_custom_call" | custom-call | flops 12884901888 | bytes 100663296 | tf_op jit(solution)/shard_map/qkv/pallas_call | solution.py:62
  41.8 0.2 copy.26
  42.1 0.2 copy.27
  42.3 0.0 copy-start.2
  42.3 0.2 copy.28
  42.6 0.0 copy-start.3
  42.6 0.0 copy-done.8
  42.6 0.0 copy-start.1
  42.6 0.0 copy-start.6
  42.6 48.3 %attend.1 = bf16[128,32,128]{2,1,0:T(8,128)(2,1)S(1)} custom-call(s32[128]{0:T(128)S(1)} %select_reduce_fusion.order_ref, s32[128]{0:T(128)S(1)} %copy-done.8, bf16[128,32,128]{2,1,0:T(8,128)(2,1)S(1)} %bitcast.18, bf16[128,32,128]{2,1,0:T(8,128)(2,1)S(1)} %bitcast.14, bf16[128,32,128]{2,1,0:T(8,128)(2,1)S(1)} %bitcast.16, bf16[128,64,32,128]{3,2,1,0:T(8,128)(2,1)} %k_hbm.1, ...), custom_call_target="tpu_custom_call" | custom-call | flops 4294967296 | bytes 67108864 | tf_op jit(solution)/shard_map/attend/pallas_call | solution.py:158
  90.9 0.0 copy-done.2
  90.9 0.0 copy-done.3
  91.0 0.5 copy.31
  91.4 0.0 copy-done.1
  91.4 0.0 copy-done.6
  91.4 15.0 %project.1 = (bf16[128,4096]{1,0:T(8,128)(2,1)S(1)}, bf16[128,4224]{1,0:T(8,128)(2,1)S(1)}, f32[128,128]{1,0:T(8,128)S(1)}) custom-call(bf16[128,4096]{1,0:T(8,128)(2,1)S(1)} %bitcast.20, bf16[128,4096]{1,0:T(8,128)(2,1)S(1)} %copy-done.1, bf16[8,4096]{1,0:T(8,128)(2,1)S(1)} %select_select_fusion.1.norm_ref.b_ref.refs_2_, bf16[16,4096]{1,0:T(8,128)(2,1)S(1)} %bitcast.24, ...), custom_call_target="tpu_custom_call" | custom-call | flops 4294967296 | bytes 33554432 | tf_op jit(solution)/shard_map/project/pallas_call | solution.py:210
  106.4 0.0 copy-start.4
  106.4 1.1 copy-done.4
  107.5 0.0 copy-start.5
  107.5 1.0 copy-done.5
  108.5 0.0 copy-start.7
  108.5 0.6 copy-done.7
  109.1 136.5 %moe.1 = (bf16[128,4096]{1,0:T(8,128)(2,1)}, bf16[8,128,4224]{2,1,0:T(8,128)(2,1)}) custom-call(bf16[128,4224]{1,0:T(8,128)(2,1)} %copy-done.4, bf16[128,4096]{1,0:T(8,128)(2,1)} %copy-done.5, f32[128,128]{1,0:T(8,128)} %copy-done.7, bf16[2,688,4096]{2,1,0:T(8,128)(2,1)} %bitcast.25, bf16[2,688,4096]{2,1,0:T(8,128)(2,1)} %bitcast.26, ...), custom_call_target="tpu_custom_call" | custom-call | tf_op jit(solution)/shard_map/moe/pallas_call | solution.py:450
  245.6 2.3 copy.33
  (7 shorter events, 0.0 us)
Async XLA Ops:
  4.5 1.2 copy-start
  5.8 36.8 %copy-start.8 = (s32[128]{0:T(128)S(1)}, s32[128]{0:T(128)}, u32[]{:S(2)}) copy-start(s32[128]{0:T(128)} %pos_ref.1) | copy-start | bytes 1540
  42.3 48.6 %copy-start.2 = (bf16[16,8,32,128]{3,2,1,0:T(8,128)(2,1)}, bf16[16,8,32,128]{3,2,1,0:T(8,128)(2,1)S(1)}, u32[]{:S(2)}) copy-start(bf16[16,8,32,128]{3,2,1,0:T(8,128)(2,1)S(1)} %copy.27) | copy-start | bytes 3145732
  42.6 48.4 %copy-start.3 = (bf16[16,8,32,128]{3,2,1,0:T(8,128)(2,1)}, bf16[16,8,32,128]{3,2,1,0:T(8,128)(2,1)S(1)}, u32[]{:S(2)}) copy-start(bf16[16,8,32,128]{3,2,1,0:T(8,128)(2,1)S(1)} %copy.28) | copy-start | bytes 3145732
  42.6 48.8 %copy-start.1 = (bf16[128,4096]{1,0:T(8,128)(2,1)S(1)}, bf16[128,4096]{1,0:T(8,128)(2,1)}, u32[]{:S(2)}) copy-start(bf16[128,4096]{1,0:T(8,128)(2,1)} %refs_1_.1) | copy-start | bytes 3145732
  42.6 48.8 %copy-start.6 = (bf16[4096,16]{0,1:T(8,128)(2,1)S(1)}, bf16[4096,16]{0,1:T(8,128)(2,1)}, u32[]{:S(2)}) copy-start(bf16[4096,16]{0,1:T(8,128)(2,1)} %param.42) | copy-start | bytes 393220
  106.4 1.1 copy-start.4
  107.5 1.0 copy-start.5
  108.5 0.6 copy-start.7

commit v4 on v3

v4 whole, which is shorter than its diff:
```python
import jax
import jax.numpy as jnp
from jax import lax
from jax.experimental import pallas as pl
from jax.experimental.pallas import tpu as pltpu
from jax.sharding import PartitionSpec as P

ROPE_BASE = 10000.0
LN_EPS = 1e-5


def rope_tables(positions, head_dim):
    half_dim = head_dim // 2
    inv_freq = ROPE_BASE ** (jnp.arange(half_dim, dtype=jnp.float32) * (-2.0 / head_dim))
    angles = positions.astype(jnp.float32)[:, None] * inv_freq[None, :]
    angles = jnp.concatenate([angles, angles], axis=-1)
    return jnp.cos(angles), jnp.sin(angles)


def norm_rows(x_val, gain, bias):
    mean_val = jnp.mean(x_val, axis=-1, keepdims=True)
    centered = x_val - mean_val
    var_val = jnp.mean(centered * centered, axis=-1, keepdims=True)
    return centered * lax.rsqrt(var_val + LN_EPS) * gain.astype(jnp.float32) + bias.astype(jnp.float32)


def row_stack(vectors):
    which = lax.broadcasted_iota(jnp.int32, (len(vectors), vectors[0].shape[0]), 0)
    out = jnp.zeros((len(vectors), vectors[0].shape[0]), vectors[0].dtype)
    for n, vec in enumerate(vectors):
        out = jnp.where(which == n, vec[None, :], out)
    return out


AHEAD = 4


def qkv_kernel(x_ref, vec_ref, cos_ref, sin_ref, wq_hbm, wk_hbm, wv_hbm, q_ref, k_ref, v_ref, h_ref, w_buf, sems):
    rows, d_model = x_ref.shape
    tile = w_buf.shape[3]
    count = q_ref.shape[1] // tile
    head_dim = cos_ref.shape[1]

    def copies(j, slot):
        cols = pl.ds(pl.multiple_of(j * tile, tile), tile)
        return [pltpu.make_async_copy(hbm.at[:, cols], w_buf.at[slot, n], sems.at[slot, n]) for n, hbm in enumerate((wq_hbm, wk_hbm, wv_hbm))]

    for j in range(AHEAD):
        for copy in copies(j, j):
            copy.start()
    h_ref[...] = norm_rows(x_ref[...].astype(jnp.float32), vec_ref[0:1], vec_ref[1:2]).astype(jnp.bfloat16)

    @pl.loop(0, count)
    def _(j):
        slot = lax.rem(j, AHEAD)
        cols = pl.ds(pl.multiple_of(j * tile, tile), tile)
        now = copies(j, slot)
        for n, o_ref in enumerate((q_ref, k_ref, v_ref)):
            now[n].wait()
            lin = jnp.dot(h_ref[...], w_buf[slot, n], preferred_element_type=jnp.float32) + vec_ref[2 + n:3 + n, cols].astype(jnp.float32)
            if n == 2:
                o_ref[:, cols] = lin.astype(jnp.bfloat16)
            else:
                parts = []
                for c in range(tile // head_dim):
                    part = lin[:, c * head_dim:(c + 1) * head_dim]
                    parts.append(part * cos_ref[...] + pltpu.roll(part, head_dim // 2, 1) * sin_ref[...])
                o_ref[:, cols] = jnp.concatenate(parts, axis=1).astype(jnp.bfloat16)

        @pl.when(j + AHEAD < count)
        def _():
            for copy in copies(j + AHEAD, slot):
                copy.start()


def qkv_call(tokens, vectors, cos_tab, sin_signed, w_query, w_key, w_value):
    rows, d_model = tokens.shape
    cols = w_query.shape[1]
    tile = 256
    vmem = pl.BlockSpec(memory_space=pltpu.VMEM)
    hbm = pl.BlockSpec(memory_space=pl.ANY)
    shape = jax.ShapeDtypeStruct((rows, cols), jnp.bfloat16)
    return pl.pallas_call(
        qkv_kernel,
        in_specs=[vmem, vmem, vmem, vmem, hbm, hbm, hbm],
        out_specs=[vmem, vmem, vmem],
        out_shape=[shape, shape, shape],
        scratch_shapes=[pltpu.VMEM((rows, d_model), jnp.bfloat16), pltpu.VMEM((AHEAD, 3, d_model, tile), jnp.bfloat16), pltpu.SemaphoreType.DMA((AHEAD, 3))],
        compiler_params=pltpu.CompilerParams(vmem_limit_bytes=44 * 2 ** 20),
        cost_estimate=pl.CostEstimate(flops=6 * rows * d_model * cols, bytes_accessed=6 * d_model * cols, transcendentals=0),
        name='qkv',
    )(tokens, vectors, cos_tab, sin_signed, w_query, w_key, w_value)


GROUP = 4
SLOTS = 4
STEP = 16


def attend_kernel(order_ref, pos_ref, q_ref, kn_ref, vn_ref, k_hbm, v_hbm, out_ref, k_buf, v_buf, sid_ref, sems):
    rows, heads, head_dim = q_ref.shape
    seq = k_hbm.shape[1]
    groups = rows // GROUP
    scale = head_dim ** -0.5
    key_id = lax.broadcasted_iota(jnp.int32, sid_ref.shape, 1)
    row_id = lax.broadcasted_iota(jnp.int32, sid_ref.shape, 0)
    sid_ref[...] = jnp.where(lax.rem(key_id, heads) == row_id, lax.div(key_id, heads), seq)

    @pl.loop(0, GROUP * SLOTS)
    def _(i):
        v_buf[i // GROUP, i % GROUP] = jnp.zeros(v_buf.shape[2:], v_buf.dtype)

    def group_at(n):
        return jnp.where(n & 1 == 0, n // 2, groups - 1 - n // 2)

    def each_size(grp, act):
        need = (pos_ref[order_ref[grp * GROUP]] + 3) & -4
        size = seq
        while size >= 4:
            @pl.when((need & size) != 0)
            def _(size=size):
                act(need & (-2 * size), size)

            size //= 2

    def fetch(n):
        grp = group_at(n)
        slot = n & (SLOTS - 1)

        def act(first, size):
            src = pl.ds(first, size)
            for i in range(GROUP):
                tok = order_ref[grp * GROUP + i]
                pltpu.make_async_copy(k_hbm.at[tok, src], k_buf.at[slot, i, src], sems.at[0, slot]).start()
                pltpu.make_async_copy(v_hbm.at[tok, src], v_buf.at[slot, i, src], sems.at[1, slot]).start()

        each_size(grp, act)

    def settle(n):
        slot = n & (SLOTS - 1)

        def act(first, size):
            src = pl.ds(0, size)
            pltpu.make_async_copy(k_hbm.at[pl.ds(0, GROUP), src], k_buf.at[slot, :, src], sems.at[0, slot]).wait()
            pltpu.make_async_copy(v_hbm.at[pl.ds(0, GROUP), src], v_buf.at[slot, :, src], sems.at[1, slot]).wait()

        each_size(group_at(n), act)

    def compute(n, steps):
        grp = group_at(n)
        slot = n & (SLOTS - 1)
        keys = steps * STEP * heads
        toks = [order_ref[grp * GROUP + i] for i in range(GROUP)]
        q_val = [q_ref[t] for t in toks]
        scores = []
        for i in range(GROUP):
            k_val = k_buf[slot, i, pl.ds(0, steps * STEP)].reshape(keys, head_dim)
            raw = lax.dot_general(q_val[i], k_val, (((1,), (1,)), ((), ())), preferred_element_type=jnp.float32)
            scores.append(jnp.where(sid_ref[:, :keys] < pos_ref[toks[i]], raw * scale, -jnp.inf))
        for i in range(GROUP):
            t = toks[i]
            s_new = jnp.sum(q_val[i].astype(jnp.float32) * kn_ref[t].astype(jnp.float32), axis=-1, keepdims=True) * scale
            top = jnp.maximum(jnp.max(scores[i], axis=-1, keepdims=True), s_new)
            e_val = jnp.exp(scores[i] - top)
            e_new = jnp.exp(s_new - top)
            inv = 1.0 / (jnp.sum(e_val, axis=-1, keepdims=True) + e_new)
            p_val = (e_val * inv).astype(jnp.bfloat16)
            p_new = (e_new * inv).astype(jnp.bfloat16).astype(jnp.float32)
            v_val = v_buf[slot, i, pl.ds(0, steps * STEP)].reshape(keys, head_dim)
            res = jnp.dot(p_val, v_val, preferred_element_type=jnp.float32) + p_new * vn_ref[t].astype(jnp.float32)
            out_ref[t] = res.astype(jnp.bfloat16)

    for n in range(SLOTS - 1):
        fetch(n)

    @pl.loop(0, groups)
    def _(n):
        @pl.when(n + SLOTS - 1 < groups)
        def _():
            fetch(n + SLOTS - 1)

        settle(n)
        most = pos_ref[order_ref[group_at(n) * GROUP]]
        steps = jnp.maximum((most + STEP - 1) // STEP, 1)
        for k in range(1, seq // STEP + 1):
            @pl.when(steps == k)
            def _(k=k):
                compute(n, k)


def attend_call(order, positions, q_rot, key_new, value_new, k_cache, v_cache):
    rows, seq, heads, head_dim = k_cache.shape
    vmem = pl.BlockSpec(memory_space=pltpu.VMEM)
    smem = pl.BlockSpec(memory_space=pltpu.SMEM)
    hbm = pl.BlockSpec(memory_space=pl.ANY)
    return pl.pallas_call(
        attend_kernel,
        in_specs=[smem, smem, vmem, vmem, vmem, hbm, hbm],
        out_specs=vmem,
        out_shape=jax.ShapeDtypeStruct((rows, heads, head_dim), jnp.bfloat16),
        scratch_shapes=[
            pltpu.VMEM((SLOTS, GROUP, seq, heads, head_dim), jnp.bfloat16),
            pltpu.VMEM((SLOTS, GROUP, seq, heads, head_dim), jnp.bfloat16),
            pltpu.VMEM((heads, seq * heads), jnp.int32),
            pltpu.SemaphoreType.DMA((2, SLOTS)),
        ],
        compiler_params=pltpu.CompilerParams(vmem_limit_bytes=40 * 2 ** 20),
        cost_estimate=pl.CostEstimate(flops=4 * rows * seq * heads * heads * head_dim, bytes_accessed=2 * rows * seq * heads * head_dim, transcendentals=0),
        name='attend',
    )(order, positions, q_rot, key_new, value_new, k_cache, v_cache)


def out_kernel(a_ref, x_ref, vec_ref, wr_ref, pick_ref, w_hbm, mid_ref, h_ref, gate_ref, w_buf, sems):
    count, _, tile = w_buf.shape

    def weight(j):
        cols = pl.ds(pl.multiple_of(j * tile, tile), tile)
        return pltpu.make_async_copy(w_hbm.at[:, cols], w_buf.at[j], sems.at[j])

    for j in range(count):
        weight(j).start()

    @pl.loop(0, count)
    def _(j):
        weight(j).wait()
        cols = pl.ds(pl.multiple_of(j * tile, tile), tile)
        mid = x_ref[:, cols].astype(jnp.float32) + jnp.dot(a_ref[...], w_buf[j], preferred_element_type=jnp.float32) + vec_ref[5:6, cols].astype(jnp.float32)
        mid_ref[:, cols] = mid.astype(jnp.bfloat16)

    h_two = norm_rows(mid_ref[...].astype(jnp.float32), vec_ref[6:7], vec_ref[7:8]).astype(jnp.bfloat16)
    lanes = lax.broadcasted_iota(jnp.int32, (h_two.shape[0], 128), 1)
    pick_val = jnp.transpose(pick_ref[...].astype(jnp.float32))
    picks = jnp.where(lanes < 2, pick_val, 0.0)
    h_ref[:, :h_two.shape[1]] = h_two
    h_ref[:, h_two.shape[1]:] = picks.astype(jnp.bfloat16)
    logits = lax.dot_general(h_two, wr_ref[...], (((1,), (1,)), ((), ())), preferred_element_type=jnp.float32)
    ids = lax.broadcasted_iota(jnp.int32, logits.shape, 1).astype(jnp.float32)
    hit_one = ids == pick_val[:, 0:1]
    hit_two = ids == pick_val[:, 1:2]
    keep_one = pick_val[:, 2:2 + logits.shape[1]] == 1.0
    gates = []
    for keep, hit in ((keep_one, hit_one), (keep_one & jnp.logical_not(hit_one), hit_two)):
        masked = jnp.where(keep, logits, -jnp.inf)
        e_val = jnp.exp(masked - jnp.max(masked, axis=-1, keepdims=True))
        top = jnp.sum(jnp.where(hit, e_val, 0.0), axis=-1, keepdims=True)
        gates.append(top / jnp.sum(e_val, axis=-1, keepdims=True))
    lane = lax.broadcasted_iota(jnp.int32, gate_ref.shape, 1)
    gate_ref[...] = jnp.where(lane == 0, gates[0], jnp.where(lane == 1, gates[1], 0.0))


def out_call(attn_flat, tokens, vectors, w_router, picks, w_out):
    rows, d_model = tokens.shape
    tile = 256
    vmem = pl.BlockSpec(memory_space=pltpu.VMEM)
    shape = lambda cols, kind: jax.ShapeDtypeStruct((rows, cols), kind)
    return pl.pallas_call(
        out_kernel,
        in_specs=[vmem] * 5 + [pl.BlockSpec(memory_space=pl.ANY)],
        out_specs=[vmem] * 3,
        out_shape=[shape(d_model, jnp.bfloat16), shape(d_model + 128, jnp.bfloat16), shape(128, jnp.float32)],
        scratch_shapes=[pltpu.VMEM((d_model // tile, w_out.shape[0], tile), jnp.bfloat16), pltpu.SemaphoreType.DMA((d_model // tile,))],
        compiler_params=pltpu.CompilerParams(vmem_limit_bytes=48 * 2 ** 20),
        cost_estimate=pl.CostEstimate(flops=2 * rows * d_model * d_model, bytes_accessed=2 * d_model * d_model, transcendentals=0),
        name='project',
    )(attn_flat, tokens, vectors, w_router, picks, w_out)


def attention_order(positions):
    ids = jnp.arange(positions.shape[0], dtype=jnp.int32)
    ahead = (positions[None, :] > positions[:, None]) | ((positions[None, :] == positions[:, None]) & (ids[None, :] < ids[:, None]))
    rank = jnp.sum(ahead.astype(jnp.int32), axis=1)
    return jnp.sum(jnp.where(rank[:, None] == ids[None, :], ids[:, None], 0), axis=0)


def moe_kernel(h_in, x_ref, gate_ref, wg_hbm, wu_hbm, wd_hbm, out_ref, hb, wg, wu, wd, xblk, zt_ref, z_ref, acc, stg, d2d, p1a, p1b, p2a, p2b, wsem, xsem, gsend, grecv, dsend, drecv, rsend, rrecv, credit):
    me = lax.axis_index('ep')
    core = lax.rem(me, 2)
    x_pos = lax.rem(lax.div(me, 2), 2)
    y_pos = lax.div(me, 4)
    partner = me + 1 - 2 * core
    xn = me + 2 - 4 * x_pos
    yn = me + 4 - 8 * y_pos
    rows = h_in.shape[0]
    mid = rows // 2
    d_model = x_ref.shape[1]
    half = d_model // 2
    ff = wd.shape[1]
    tile = 512
    mesh_id = pl.DeviceIdType.MESH
    part_rows = (pl.ds(0, mid), pl.ds(mid, mid))

    def remote(src, dst, send, recv, dev):
        return pltpu.make_async_remote_copy(src_ref=src, dst_ref=dst, send_sem=send, recv_sem=recv, device_id=(dev,), device_id_type=mesh_id)

    gather = []

    def add_gather(src, dst, dev):
        n = len(gather)
        gather.append(remote(src, dst, gsend.at[n], grecv.at[n], dev))
        return gather[-1]

    own = add_gather(h_in, hb.at[1], partner)
    from_x = [add_gather(h_in.at[p], hb.at[2, p], xn) for p in part_rows]
    from_y = [add_gather(h_in.at[p], hb.at[4, p], yn) for p in part_rows]
    share_x = [add_gather(hb.at[2, p], hb.at[3, p], partner) for p in part_rows]
    share_y = [add_gather(hb.at[4, p], hb.at[5, p], partner) for p in part_rows]
    far = [add_gather(hb.at[2, part_rows[0]], hb.at[6, part_rows[0]], yn), add_gather(hb.at[4, part_rows[1]], hb.at[6, part_rows[1]], xn)]
    share_far = [add_gather(hb.at[6, p], hb.at[7, p], partner) for p in part_rows]

    scatter = []

    def add_scatter(src, dst, dev):
        n = len(scatter)
        scatter.append(remote(src, dst, rsend.at[n], rrecv.at[n], dev))
        return scatter[-1]

    x_first = [add_scatter(acc.at[1 + h, 0, :, part_rows[0]], p1a.at[0, h], xn) for h in range(2)]
    y_first = [add_scatter(acc.at[1 + h, 1, :, part_rows[1]], p1b.at[0, h], yn) for h in range(2)]
    x_far = [add_scatter(acc.at[3, 0, :, part_rows[h]], p1a.at[1, h], xn) for h in range(2)]
    y_far = [add_scatter(acc.at[3, 1, :, part_rows[h]], p1b.at[1, h], yn) for h in range(2)]
    y_last = [add_scatter(acc.at[1 + h, 0, :, part_rows[1]], p2a.at[h], yn) for h in range(2)]
    x_last = [add_scatter(acc.at[1 + h, 1, :, part_rows[0]], p2b.at[h], xn) for h in range(2)]

    def weight(e):
        return [pltpu.make_async_copy(hbm.at[e], buf.at[e], wsem.at[n, e]) for n, (hbm, buf) in enumerate(((wg_hbm, wg), (wu_hbm, wu), (wd_hbm, wd)))]

    barrier = pltpu.get_barrier_semaphore()
    for dev in (partner, xn, yn):
        pl.semaphore_signal(barrier, inc=1, device_id=(dev,), device_id_type=mesh_id)
    for e in range(2):
        for copy in weight(e):
            copy.start()
    zt_ref[...] = jnp.zeros_like(zt_ref)
    pl.semaphore_wait(barrier, 3)
    for h in range(2):
        from_x[h].start()
        from_y[h].start()
    own.start()

    def load(sources):
        step = 2 * rows // len(sources)
        copies = [pltpu.make_async_copy(src, xblk.at[pl.ds(n * step, step)], xsem.at[n]) for n, src in enumerate(sources)]
        for copy in copies:
            copy.start()
        for copy in copies:
            copy.wait()

    def merge(dst, src):
        count = dst.shape[1] // 32

        @pl.loop(0, 2 * count)
        def _(i):
            slot = lax.div(i, count)
            at = pl.ds(pl.multiple_of(lax.rem(i, count) * 32, 32), 32)
            dst[slot, at] = dst[slot, at] + src[slot, at]

    def shared(r, part):
        return remote(stg.at[part], d2d.at[lax.rem(r, 2), part], dsend.at[part], drecv.at[r, part], partner)

    def gather_step(h):
        from_x[h].wait_recv()
        share_x[h].start()
        if h == 0:
            far[0].start()
        from_y[h].wait_recv()
        share_y[h].start()
        if h == 1:
            far[1].start()

    def merge_high(r, finish):
        shared(r, 1).wait_recv()
        merge(acc.at[r, 1], d2d.at[lax.rem(r, 2), 1])
        if not finish:
            for h in range(2):
                @pl.when(r == 1 + h)
                def _(h=h):
                    y_first[h].start()

            @pl.when(r < 2)
            def _():
                pl.semaphore_signal(credit, inc=1, device_id=(partner,), device_id_type=mesh_id)

    @pl.loop(0, 4)
    def _(r):
        @pl.when(r == 0)
        def _():
            pltpu.sync_copy(h_in, xblk.at[pl.ds(0, rows)])
            own.wait_recv()
            copy = pltpu.make_async_copy(hb.at[1], xblk.at[pl.ds(rows, rows)], xsem.at[0])
            copy.start()
            copy.wait()

        for h in range(2):
            @pl.when(r == 1 + h)
            def _(h=h):
                share_x[h].wait_recv()
                share_y[h].wait_recv()
                load([hb.at[n, part_rows[h]] for n in (2, 4, 3, 5)])

        @pl.when(r == 3)
        def _():
            share_far[0].wait_recv()
            share_far[1].wait_recv()
            load([hb.at[6], hb.at[7]])

        @pl.loop(0, 2)
        def _(e):
            @pl.when(r == 0)
            def _():
                for copy in weight(e)[:2]:
                    copy.wait()

            x_val = xblk[:, :d_model]
            dims = (((1,), (1,)), ((), ()))
            u_val = lax.dot_general(wg[e], x_val, dims, preferred_element_type=jnp.float32)
            v_val = lax.dot_general(wu[e], x_val, dims, preferred_element_type=jnp.float32)
            zt_ref[:ff] = (jax.nn.silu(u_val) * v_val).astype(jnp.bfloat16)
            z_ref[e] = jnp.transpose(zt_ref[...])

            @pl.when((r > 0) & (e == 0))
            def _():
                merge_high(r - 1, False)

            for h in range(2):
                @pl.when((r == h) & (e == 0))
                def _(h=h):
                    gather_step(h)

        @pl.when(r == 0)
        def _():
            for e in range(2):
                weight(e)[2].wait()

        @pl.when(r == 2)
        def _():
            for h in range(2):
                far[h].wait_recv()
                share_far[h].start()

        @pl.loop(0, 2)
        def _(part):
            @pl.when(r > 0)
            def _():
                shared(r - 1, part).wait_send()

            @pl.loop(0, half // tile)
            def _(n):
                wide = pl.ds(pl.multiple_of(part * half + n * tile, tile), tile)
                slim = pl.ds(pl.multiple_of(n * tile, tile), tile)
                first = jnp.dot(z_ref[0, :, :ff], wd[0, :, wide], preferred_element_type=jnp.float32)
                second = jnp.dot(z_ref[1, :, :ff], wd[1, :, wide], preferred_element_type=jnp.float32)
                for slot in range(2):
                    choice = xblk[:, d_model:][:, slot:slot + 1].astype(jnp.float32)
                    lead = (2 * me).astype(jnp.float32)
                    val = jnp.where(choice == lead, first, jnp.where(choice == lead + 1.0, second, 0.0)).astype(jnp.bfloat16)
                    acc[r, part, slot, :, slim] = val[:rows]
                    stg[part, slot, :, slim] = val[rows:]

            @pl.when((r >= 2) & (part == 0))
            def _():
                pl.semaphore_wait(credit, 1)

            shared(r, part).start()

        shared(r, 0).wait_recv()
        merge(acc.at[r, 0], d2d.at[lax.rem(r, 2), 0])
        for h in range(2):
            @pl.when(r == 1 + h)
            def _(h=h):
                x_first[h].start()

        @pl.when(r == 3)
        def _():
            x_far[0].start()
            x_far[1].start()

    merge_high(3, True)
    y_far[0].start()
    y_far[1].start()
    for h in range(2):
        x_far[h].wait_recv()
        merge(acc.at[1 + h, 0, :, part_rows[1]], p1a.at[1, h])
        y_last[h].start()
        y_far[h].wait_recv()
        merge(acc.at[1 + h, 1, :, part_rows[0]], p1b.at[1, h])
        x_last[h].start()
    for h in range(2):
        x_first[h].wait_recv()
        merge(acc.at[0, 0, :, part_rows[h]], p1a.at[0, h])
        y_first[h].wait_recv()
        merge(acc.at[0, 1, :, part_rows[h]], p1b.at[0, h])
    for h in range(2):
        for part, last, buf in ((0, y_last, p2a), (1, x_last, p2b)):
            last[h].wait_recv()

            @pl.loop(0, mid // 16)
            def _(i, h=h, part=part, buf=buf):
                near = pl.ds(pl.multiple_of(i * 16, 16), 16)
                at = pl.ds(pl.multiple_of(h * mid + i * 16, 16), 16)
                wide = pl.ds(part * half, half)
                gates = gate_ref[at]
                y_val = [(acc[0, part, slot, at] + buf[h, slot, near]).astype(jnp.float32) * gates[:, slot:slot + 1] for slot in range(2)]
                out_ref[at, wide] = (x_ref[at, wide].astype(jnp.float32) + (y_val[0] + y_val[1])).astype(jnp.bfloat16)

    for copy in gather + scatter:
        copy.wait_send()
    for part in range(2):
        shared(3, part).wait_send()


def moe_call(h_ext, x_mid, gates, w_gate, w_up, w_down):
    rows, d_model = x_mid.shape
    half = d_model // 2
    ff = w_gate.shape[2]
    ff_pad = pl.cdiv(ff, 128) * 128
    width = h_ext.shape[1]
    vmem = pl.BlockSpec(memory_space=pltpu.VMEM)
    hbm = pl.BlockSpec(memory_space=pl.ANY)
    bf = jnp.bfloat16
    dma = pltpu.SemaphoreType.DMA
    out, _ = pl.pallas_call(
        moe_kernel,
        in_specs=[vmem, vmem, vmem, hbm, hbm, hbm],
        out_specs=[vmem, hbm],
        out_shape=[jax.ShapeDtypeStruct((rows, d_model), bf), jax.ShapeDtypeStruct((8, rows, width), bf)],
        scratch_shapes=[
            pltpu.VMEM((2, ff, d_model), bf),
            pltpu.VMEM((2, ff, d_model), bf),
            pltpu.VMEM((2, ff, d_model), bf),
            pltpu.VMEM((2 * rows, width), bf),
            pltpu.VMEM((ff_pad, 2 * rows), bf),
            pltpu.VMEM((2, 2 * rows, ff_pad), bf),
            pltpu.VMEM((4, 2, 2, rows, half), bf),
            pltpu.VMEM((2, 2, rows, half), bf),
            pltpu.VMEM((2, 2, 2, rows, half), bf),
            pltpu.VMEM((2, 2, 2, rows // 2, half), bf),
            pltpu.VMEM((2, 2, 2, rows // 2, half), bf),
            pltpu.VMEM((2, 2, rows // 2, half), bf),
            pltpu.VMEM((2, 2, rows // 2, half), bf),
            dma((3, 2)),
            dma((4,)),
            dma((13,)),
            dma((13,)),
            dma((2,)),
            dma((4, 2)),
            dma((12,)),
            dma((12,)),
            pltpu.SemaphoreType.REGULAR,
        ],
        compiler_params=pltpu.CompilerParams(vmem_limit_bytes=67043328, collective_id=0, has_side_effects=True),
        name='moe',
    )(h_ext, x_mid, gates, jnp.swapaxes(w_gate, 1, 2), jnp.swapaxes(w_up, 1, 2), w_down)
    return out


def solution(mesh):
    def local_step(tokens, k_cache, v_cache, positions, expert_one, expert_two, eligible, ln1_gain, ln1_bias, w_query, b_query, w_key, b_key, w_value, b_value, w_out, b_out, ln2_gain, ln2_bias, w_router, w_gate, w_up, w_down):
        tok_count, seq_len, heads, head_dim = k_cache.shape
        d_model = tokens.shape[1]
        cos_tab, sin_tab = rope_tables(positions, head_dim)
        sign = jnp.where(jnp.arange(head_dim) < head_dim // 2, -1.0, 1.0)
        vectors = row_stack([ln1_gain, ln1_bias, b_query, b_key, b_value, b_out, ln2_gain, ln2_bias])
        which = lax.broadcasted_iota(jnp.int32, (128, tok_count), 0)
        picks = jnp.where(which == 0, expert_one[None, :], jnp.where(which == 1, expert_two[None, :], jnp.pad(eligible.T, ((2, 110), (0, 0)))))
        q_flat, k_flat, v_flat = qkv_call(tokens, vectors, cos_tab, sin_tab * sign[None, :], w_query, w_key, w_value)
        split = lambda t: t.reshape(tok_count, heads, head_dim)
        key_new, value_new = split(k_flat), split(v_flat)
        attn = attend_call(attention_order(positions), positions, split(q_flat), key_new, value_new, k_cache, v_cache)
        x_mid, h_ext, gates = out_call(attn.reshape(tok_count, heads * head_dim), tokens, vectors, w_router.T, picks, w_out)
        tokens_out = moe_call(h_ext, x_mid, gates, w_gate, w_up, w_down)
        return tokens_out, key_new, value_new

    row_spec = P('ep', None)
    cache_spec = P('ep', None, None, None)
    vec_spec = P('ep')
    rep_one = P(None)
    rep_two = P(None, None)
    expert_spec = P('ep', None, None)
    in_specs = (row_spec, cache_spec, cache_spec, vec_spec, vec_spec, vec_spec, row_spec, rep_one, rep_one, rep_two, rep_one, rep_two, rep_one, rep_two, rep_one, rep_two, rep_one, rep_one, rep_one, rep_two, expert_spec, expert_spec, expert_spec)
    out_specs = (row_spec, expert_spec, expert_spec)
    return jax.shard_map(local_step, mesh=mesh, in_specs=in_specs, out_specs=out_specs, check_vma=False)
```

time: 249 us -> 217 us (0.87)
  Pallas kernels: 236 us -> 205 us
    pallas_call x3, Pallas kernels: 188 us -> 166 us  [the longest x1 119 us: moe_call(): pl.pallas_call(moe_kernel, in_specs=[vmem, vmem, vmem, hbm, hbm, hbm], ou...]
    pallas_call x1, Pallas kernels: 48.3 us -> 39.1 us  [attend_call(): pl.pallas_call(attend_kernel, in_specs=[smem, smem, vmem, vmem, vmem, hbm...]
where the time goes in v4:
time: 217 us
  Pallas kernels  205 us (94%)
  local copies, waits for them, and re-layouts  7.37 us (3%)
  other arithmetic  3.84 us (2%)
    pallas_call x1, Pallas kernels, moe_call(): pl.pallas_call(moe_kernel, in_specs=[vmem, vmem, vmem, hbm, hbm, hbm], ou...  119 us
    pallas_call x1, Pallas kernels, attend_call(): pl.pallas_call(attend_kernel, in_specs=[smem, smem, vmem, vmem, vmem, hbm...  39.1 us
    pallas_call x1, Pallas kernels, qkv_call(): pl.pallas_call(qkv_kernel, in_specs=[vmem, vmem, vmem, vmem, hbm, hbm, hb...  33.6 us
    pallas_call x1, Pallas kernels, out_call(): pl.pallas_call(out_kernel, in_specs=[vmem] * 5 + [pl.BlockSpec(memory_spa...  12.8 us
    unnamed x23, local copies, waits for them, and re-layouts  7.37 us

profile of v4, /device:TPU:0, one launch (start us, length us, event | category | flops | bytes accessed | tf_op | source)
XLA Modules:
  0.0 216.9 jit_solution(3947373942060150027)
XLA Ops:
  0.6 0.9 convert_reduce_fusion
  1.5 0.1 select_reduce_fusion.order_ref
  1.6 0.7 convert_element_type.7
  2.4 0.9 select_select_fusion.1.vec_ref
  3.3 0.8 select_select_fusion.pick_ref
  4.1 0.1 broadcast_multiply_fusion
  4.2 0.3 sine_multiply_fusion
  4.5 0.0 copy-start
  4.5 1.2 copy-done
  5.8 0.0 copy-start.8
  5.8 33.6 %qkv.1 = (bf16[128,4096]{1,0:T(8,128)(2,1)S(1)}, bf16[128,4096]{1,0:T(8,128)(2,1)S(1)}, bf16[128,4096]{1,0:T(8,128)(2,1)S(1)}) custom-call(bf16[128,4096]{1,0:T(8,128)(2,1)S(1)} %copy-done, bf16[8,4096]{1,0:T(8,128)(2,1)S(1)} %select_select_fusion.1.vec_ref, f32[128,128]{1,0:T(8,128)S(1)} %get-tuple-element.18.cos_ref, ...), custom_call_target="tpu_custom_call" | custom-call | flops 12884901888 | bytes 100663296 | tf_op jit(solution)/shard_map/qkv/pallas_call | solution.py:83
  39.4 0.2 copy.26
  39.6 0.2 copy.27
  39.9 0.0 copy-start.2
  39.9 0.2 copy.28
  40.1 0.0 copy-start.3
  40.1 0.0 copy-done.8
  40.1 0.0 copy-start.1
  40.2 0.0 copy-start.6
  40.2 39.1 %attend.1 = bf16[128,32,128]{2,1,0:T(8,128)(2,1)S(1)} custom-call(s32[128]{0:T(128)S(1)} %select_reduce_fusion.order_ref, s32[128]{0:T(128)S(1)} %copy-done.8, bf16[128,32,128]{2,1,0:T(8,128)(2,1)S(1)} %bitcast.18, bf16[128,32,128]{2,1,0:T(8,128)(2,1)S(1)} %bitcast.14, bf16[128,32,128]{2,1,0:T(8,128)(2,1)S(1)} %bitcast.16, bf16[128,64,32,128]{3,2,1,0:T(8,128)(2,1)} %k_hbm.1, ...), custom_call_target="tpu_custom_call" | custom-call | flops 4294967296 | bytes 67108864 | tf_op jit(solution)/shard_map/attend/pallas_call | solution.py:196
  79.3 0.0 copy-done.2
  79.3 0.0 copy-done.3
  79.3 0.5 copy.31
  79.7 0.0 copy-done.1
  79.8 0.0 copy-done.6
  79.8 12.8 %project.1 = (bf16[128,4096]{1,0:T(8,128)(2,1)S(1)}, bf16[128,4224]{1,0:T(8,128)(2,1)S(1)}, f32[128,128]{1,0:T(8,128)S(1)}) custom-call(bf16[128,4096]{1,0:T(8,128)(2,1)S(1)} %bitcast.20, bf16[128,4096]{1,0:T(8,128)(2,1)S(1)} %copy-done.1, bf16[8,4096]{1,0:T(8,128)(2,1)S(1)} %select_select_fusion.1.vec_ref, bf16[16,4096]{1,0:T(8,128)(2,1)S(1)} %bitcast.24, ...), custom_call_target="tpu_custom_call" | custom-call | flops 4294967296 | bytes 33554432 | tf_op jit(solution)/shard_map/project/pallas_call | solution.py:256
  92.6 0.0 copy-start.4
  92.6 1.1 copy-done.4
  93.7 0.0 copy-start.5
  93.7 1.0 copy-done.5
  94.6 0.0 copy-start.7
  94.6 0.6 copy-done.7
  95.3 119.3 %moe.1 = (bf16[128,4096]{1,0:T(8,128)(2,1)}, bf16[8,128,4224]{2,1,0:T(8,128)(2,1)}) custom-call(bf16[128,4224]{1,0:T(8,128)(2,1)} %copy-done.4, bf16[128,4096]{1,0:T(8,128)(2,1)} %copy-done.5, f32[128,128]{1,0:T(8,128)} %copy-done.7, bf16[2,688,4096]{2,1,0:T(8,128)(2,1)} %bitcast.25, bf16[2,688,4096]{2,1,0:T(8,128)(2,1)} %bitcast.26, ...), custom_call_target="tpu_custom_call" | custom-call | tf_op jit(solution)/shard_map/moe/pallas_call | solution.py:521
  214.6 2.3 %copy.33 = bf16[128,4096]{1,0:T(8,128)(2,1)} copy(bf16[128,4096]{1,0:T(8,128)(2,1)} %get-tuple-element.32) | data formatting | bytes 2097152
  (7 shorter events, 0.0 us)
Async XLA Ops:
  4.5 1.2 copy-start
  5.8 34.4 %copy-start.8 = (s32[128]{0:T(128)S(1)}, s32[128]{0:T(128)}, u32[]{:S(2)}) copy-start(s32[128]{0:T(128)} %pos_ref.1) | copy-start | bytes 1540
  39.9 39.4 %copy-start.2 = (bf16[16,8,32,128]{3,2,1,0:T(8,128)(2,1)}, bf16[16,8,32,128]{3,2,1,0:T(8,128)(2,1)S(1)}, u32[]{:S(2)}) copy-start(bf16[16,8,32,128]{3,2,1,0:T(8,128)(2,1)S(1)} %copy.27) | copy-start | bytes 3145732
  40.1 39.2 %copy-start.3 = (bf16[16,8,32,128]{3,2,1,0:T(8,128)(2,1)}, bf16[16,8,32,128]{3,2,1,0:T(8,128)(2,1)S(1)}, u32[]{:S(2)}) copy-start(bf16[16,8,32,128]{3,2,1,0:T(8,128)(2,1)S(1)} %copy.28) | copy-start | bytes 3145732
  40.1 39.6 %copy-start.1 = (bf16[128,4096]{1,0:T(8,128)(2,1)S(1)}, bf16[128,4096]{1,0:T(8,128)(2,1)}, u32[]{:S(2)}) copy-start(bf16[128,4096]{1,0:T(8,128)(2,1)} %x_ref.3) | copy-start | bytes 3145732
  40.2 39.6 %copy-start.6 = (bf16[4096,16]{0,1:T(8,128)(2,1)S(1)}, bf16[4096,16]{0,1:T(8,128)(2,1)}, u32[]{:S(2)}) copy-start(bf16[4096,16]{0,1:T(8,128)(2,1)} %param.42) | copy-start | bytes 393220
  92.6 1.1 copy-start.4
  93.7 1.0 copy-start.5
  94.6 0.6 copy-start.7

commit v5 on v4

--- a/solution.py
+++ b/solution.py
@@ -54,9 +54,9 @@
     def _(j):
         slot = lax.rem(j, AHEAD)
         cols = pl.ds(pl.multiple_of(j * tile, tile), tile)
-        now = copies(j, slot)
+        for copy in copies(j, slot):
+            copy.wait()
         for n, o_ref in enumerate((q_ref, k_ref, v_ref)):
-            now[n].wait()
             lin = jnp.dot(h_ref[...], w_buf[slot, n], preferred_element_type=jnp.float32) + vec_ref[2 + n:3 + n, cols].astype(jnp.float32)
             if n == 2:
                 o_ref[:, cols] = lin.astype(jnp.bfloat16)
@@ -92,9 +92,10 @@
     )(tokens, vectors, cos_tab, sin_signed, w_query, w_key, w_value)
 
 
-GROUP = 4
-SLOTS = 4
+GROUP = 8
+SLOTS = 3
 STEP = 16
+CHUNK = 8
 
 
 def attend_kernel(order_ref, pos_ref, q_ref, kn_ref, vn_ref, k_hbm, v_hbm, out_ref, k_buf, v_buf, sid_ref, sems):
@@ -113,42 +114,38 @@
     def group_at(n):
         return jnp.where(n & 1 == 0, n // 2, groups - 1 - n // 2)
 
-    def each_size(grp, act):
-        need = (pos_ref[order_ref[grp * GROUP]] + 3) & -4
-        size = seq
-        while size >= 4:
-            @pl.when((need & size) != 0)
-            def _(size=size):
-                act(need & (-2 * size), size)
-
-            size //= 2
+    def chunks_at(n):
+        return (pos_ref[order_ref[group_at(n) * GROUP]] + CHUNK - 1) // CHUNK
 
     def fetch(n):
         grp = group_at(n)
-        slot = n & (SLOTS - 1)
-
-        def act(first, size):
-            src = pl.ds(first, size)
-            for i in range(GROUP):
-                tok = order_ref[grp * GROUP + i]
-                pltpu.make_async_copy(k_hbm.at[tok, src], k_buf.at[slot, i, src], sems.at[0, slot]).start()
-                pltpu.make_async_copy(v_hbm.at[tok, src], v_buf.at[slot, i, src], sems.at[1, slot]).start()
-
-        each_size(grp, act)
+        slot = lax.rem(n, SLOTS)
+        chunks = chunks_at(n)
+        for k in range(1, seq // CHUNK + 1):
+            @pl.when(chunks == k)
+            def _(k=k):
+                src = pl.ds(0, k * CHUNK)
+                for i in range(GROUP):
+                    tok = order_ref[grp * GROUP + i]
+                    pltpu.make_async_copy(k_hbm.at[tok, src], k_buf.at[slot, i, src], sems.at[0, slot]).start()
+                    pltpu.make_async_copy(v_hbm.at[tok, src], v_buf.at[slot, i, src], sems.at[1, slot]).start()
 
     def settle(n):
-        slot = n & (SLOTS - 1)
-
-        def act(first, size):
-            src = pl.ds(0, size)
-            pltpu.make_async_copy(k_hbm.at[pl.ds(0, GROUP), src], k_buf.at[slot, :, src], sems.at[0, slot]).wait()
-            pltpu.make_async_copy(v_hbm.at[pl.ds(0, GROUP), src], v_buf.at[slot, :, src], sems.at[1, slot]).wait()
-
-        each_size(group_at(n), act)
+        slot = lax.rem(n, SLOTS)
+        chunks = chunks_at(n)
+        size = seq // CHUNK
+        while size >= 1:
+            @pl.when((chunks & size) != 0)
+            def _(size=size):
+                src = pl.ds(0, size * CHUNK)
+                pltpu.make_async_copy(k_hbm.at[pl.ds(0, GROUP), src], k_buf.at[slot, :, src], sems.at[0, slot]).wait()
+                pltpu.make_async_copy(v_hbm.at[pl.ds(0, GROUP), src], v_buf.at[slot, :, src], sems.at[1, slot]).wait()
+
+            size //= 2
 
     def compute(n, steps):
         grp = group_at(n)
-        slot = n & (SLOTS - 1)
+        slot = lax.rem(n, SLOTS)
         keys = steps * STEP * heads
         toks = [order_ref[grp * GROUP + i] for i in range(GROUP)]
         q_val = [q_ref[t] for t in toks]
@@ -204,13 +201,16 @@
             pltpu.VMEM((heads, seq * heads), jnp.int32),
             pltpu.SemaphoreType.DMA((2, SLOTS)),
         ],
-        compiler_params=pltpu.CompilerParams(vmem_limit_bytes=40 * 2 ** 20),
+        compiler_params=pltpu.CompilerParams(vmem_limit_bytes=48 * 2 ** 20),
         cost_estimate=pl.CostEstimate(flops=4 * rows * seq * heads * heads * head_dim, bytes_accessed=2 * rows * seq * heads * head_dim, transcendentals=0),
         name='attend',
     )(order, positions, q_rot, key_new, value_new, k_cache, v_cache)
 
 
-def out_kernel(a_ref, x_ref, vec_ref, wr_ref, pick_ref, w_hbm, mid_ref, h_ref, gate_ref, w_buf, sems):
+def out_kernel(a_ref, x_hbm, vec_ref, wr_ref, pick_ref, w_hbm, mid_hbm, h_hbm, gate_hbm, x_ref, mid_ref, h_ref, gate_ref, w_buf, sems, io_sems):
+    x_copy = pltpu.make_async_copy(x_hbm, x_ref, io_sems.at[0])
+    results = [pltpu.make_async_copy(src, dst, io_sems.at[1 + n]) for n, (src, dst) in enumerate(((mid_ref, mid_hbm), (h_ref, h_hbm), (gate_ref, gate_hbm)))]
+    x_copy.start()
     count, _, tile = w_buf.shape
 
     def weight(j):
@@ -219,6 +219,7 @@
 
     for j in range(count):
         weight(j).start()
+    x_copy.wait()
 
     @pl.loop(0, count)
     def _(j):
@@ -227,12 +228,14 @@
         mid = x_ref[:, cols].astype(jnp.float32) + jnp.dot(a_ref[...], w_buf[j], preferred_element_type=jnp.float32) + vec_ref[5:6, cols].astype(jnp.float32)
         mid_ref[:, cols] = mid.astype(jnp.bfloat16)
 
+    results[0].start()
     h_two = norm_rows(mid_ref[...].astype(jnp.float32), vec_ref[6:7], vec_ref[7:8]).astype(jnp.bfloat16)
     lanes = lax.broadcasted_iota(jnp.int32, (h_two.shape[0], 128), 1)
     pick_val = jnp.transpose(pick_ref[...].astype(jnp.float32))
     picks = jnp.where(lanes < 2, pick_val, 0.0)
     h_ref[:, :h_two.shape[1]] = h_two
     h_ref[:, h_two.shape[1]:] = picks.astype(jnp.bfloat16)
+    results[1].start()
     logits = lax.dot_general(h_two, wr_ref[...], (((1,), (1,)), ((), ())), preferred_element_type=jnp.float32)
     ids = lax.broadcasted_iota(jnp.int32, logits.shape, 1).astype(jnp.float32)
     hit_one = ids == pick_val[:, 0:1]
@@ -246,20 +249,32 @@
         gates.append(top / jnp.sum(e_val, axis=-1, keepdims=True))
     lane = lax.broadcasted_iota(jnp.int32, gate_ref.shape, 1)
     gate_ref[...] = jnp.where(lane == 0, gates[0], jnp.where(lane == 1, gates[1], 0.0))
+    results[2].start()
+    for copy in results:
+        copy.wait()
 
 
 def out_call(attn_flat, tokens, vectors, w_router, picks, w_out):
     rows, d_model = tokens.shape
     tile = 256
     vmem = pl.BlockSpec(memory_space=pltpu.VMEM)
+    hbm = pl.BlockSpec(memory_space=pl.ANY)
     shape = lambda cols, kind: jax.ShapeDtypeStruct((rows, cols), kind)
     return pl.pallas_call(
         out_kernel,
-        in_specs=[vmem] * 5 + [pl.BlockSpec(memory_space=pl.ANY)],
-        out_specs=[vmem] * 3,
+        in_specs=[vmem, hbm, vmem, vmem, vmem, hbm],
+        out_specs=[pl.BlockSpec(memory_space=pltpu.HBM)] * 3,
         out_shape=[shape(d_model, jnp.bfloat16), shape(d_model + 128, jnp.bfloat16), shape(128, jnp.float32)],
-        scratch_shapes=[pltpu.VMEM((d_model // tile, w_out.shape[0], tile), jnp.bfloat16), pltpu.SemaphoreType.DMA((d_model // tile,))],
-        compiler_params=pltpu.CompilerParams(vmem_limit_bytes=48 * 2 ** 20),
+        scratch_shapes=[
+            pltpu.VMEM((rows, d_model), jnp.bfloat16),
+            pltpu.VMEM((rows, d_model), jnp.bfloat16),
+            pltpu.VMEM((rows, d_model + 128), jnp.bfloat16),
+            pltpu.VMEM((rows, 128), jnp.float32),
+            pltpu.VMEM((d_model // tile, w_out.shape[0], tile), jnp.bfloat16),
+            pltpu.SemaphoreType.DMA((d_model // tile,)),
+            pltpu.SemaphoreType.DMA((4,)),
+        ],
+        compiler_params=pltpu.CompilerParams(vmem_limit_bytes=67043328),
         cost_estimate=pl.CostEstimate(flops=2 * rows * d_model * d_model, bytes_accessed=2 * d_model * d_model, transcendentals=0),
         name='project',
     )(attn_flat, tokens, vectors, w_router, picks, w_out)
@@ -272,7 +287,7 @@
     return jnp.sum(jnp.where(rank[:, None] == ids[None, :], ids[:, None], 0), axis=0)
 
 
-def moe_kernel(h_in, x_ref, gate_ref, wg_hbm, wu_hbm, wd_hbm, out_ref, hb, wg, wu, wd, xblk, zt_ref, z_ref, acc, stg, d2d, p1a, p1b, p2a, p2b, wsem, xsem, gsend, grecv, dsend, drecv, rsend, rrecv, credit):
+def moe_kernel(h_in, x_hbm, gate_hbm, wg_hbm, wu_hbm, wd_hbm, out_hbm, hb, wg, wu, wd, gate_ref, xblk, zt_ref, z_ref, acc, stg, d2d, p1a, p1b, p2a, p2b, wsem, xsem, gsend, grecv, dsend, drecv, rsend, rrecv, credit):
     me = lax.axis_index('ep')
     core = lax.rem(me, 2)
     x_pos = lax.rem(lax.div(me, 2), 2)
@@ -282,7 +297,7 @@
     yn = me + 4 - 8 * y_pos
     rows = h_in.shape[0]
     mid = rows // 2
-    d_model = x_ref.shape[1]
+    d_model = x_hbm.shape[1]
     half = d_model // 2
     ff = wd.shape[1]
     tile = 512
@@ -346,12 +361,12 @@
             copy.wait()
 
     def merge(dst, src):
-        count = dst.shape[1] // 32
+        count = dst.shape[1] // 16
 
         @pl.loop(0, 2 * count)
         def _(i):
             slot = lax.div(i, count)
-            at = pl.ds(pl.multiple_of(lax.rem(i, count) * 32, 32), 32)
+            at = pl.ds(pl.multiple_of(lax.rem(i, count) * 16, 16), 16)
             dst[slot, at] = dst[slot, at] + src[slot, at]
 
     def shared(r, part):
@@ -384,11 +399,8 @@
     def _(r):
         @pl.when(r == 0)
         def _():
-            pltpu.sync_copy(h_in, xblk.at[pl.ds(0, rows)])
             own.wait_recv()
-            copy = pltpu.make_async_copy(hb.at[1], xblk.at[pl.ds(rows, rows)], xsem.at[0])
-            copy.start()
-            copy.wait()
+            load([h_in, hb.at[1]])
 
         for h in range(2):
             @pl.when(r == 1 + h)
@@ -474,6 +486,11 @@
             x_far[0].start()
             x_far[1].start()
 
+    x_ref = xblk.at[pl.ds(0, rows), pl.ds(0, d_model)]
+    out_ref = xblk.at[pl.ds(rows, rows), pl.ds(0, d_model)]
+    late = [pltpu.make_async_copy(x_hbm, x_ref, xsem.at[0]), pltpu.make_async_copy(gate_hbm, gate_ref, xsem.at[1])]
+    for copy in late:
+        copy.start()
     merge_high(3, True)
     y_far[0].start()
     y_far[1].start()
@@ -489,6 +506,8 @@
         merge(acc.at[0, 0, :, part_rows[h]], p1a.at[0, h])
         y_first[h].wait_recv()
         merge(acc.at[0, 1, :, part_rows[h]], p1b.at[0, h])
+    for copy in late:
+        copy.wait()
     for h in range(2):
         for part, last, buf in ((0, y_last, p2a), (1, x_last, p2b)):
             last[h].wait_recv()
@@ -502,10 +521,13 @@
                 y_val = [(acc[0, part, slot, at] + buf[h, slot, near]).astype(jnp.float32) * gates[:, slot:slot + 1] for slot in range(2)]
                 out_ref[at, wide] = (x_ref[at, wide].astype(jnp.float32) + (y_val[0] + y_val[1])).astype(jnp.bfloat16)
 
+    out_copy = pltpu.make_async_copy(out_ref, out_hbm, xsem.at[2])
+    out_copy.start()
     for copy in gather + scatter:
         copy.wait_send()
     for part in range(2):
         shared(3, part).wait_send()
+    out_copy.wait()
 
 
 def moe_call(h_ext, x_mid, gates, w_gate, w_up, w_down):
@@ -514,19 +536,19 @@
     ff = w_gate.shape[2]
     ff_pad = pl.cdiv(ff, 128) * 128
     width = h_ext.shape[1]
-    vmem = pl.BlockSpec(memory_space=pltpu.VMEM)
     hbm = pl.BlockSpec(memory_space=pl.ANY)
     bf = jnp.bfloat16
     dma = pltpu.SemaphoreType.DMA
     out, _ = pl.pallas_call(
         moe_kernel,
-        in_specs=[vmem, vmem, vmem, hbm, hbm, hbm],
-        out_specs=[vmem, hbm],
+        in_specs=[hbm] * 6,
+        out_specs=[hbm, hbm],
         out_shape=[jax.ShapeDtypeStruct((rows, d_model), bf), jax.ShapeDtypeStruct((8, rows, width), bf)],
         scratch_shapes=[
             pltpu.VMEM((2, ff, d_model), bf),
             pltpu.VMEM((2, ff, d_model), bf),
             pltpu.VMEM((2, ff, d_model), bf),
+            pltpu.VMEM(gates.shape, gates.dtype),
             pltpu.VMEM((2 * rows, width), bf),
             pltpu.VMEM((ff_pad, 2 * rows), bf),
             pltpu.VMEM((2, 2 * rows, ff_pad), bf),

time: 217 us -> 217 us (level)
    pallas_call x2, Pallas kernels: 132 us -> 139 us  [the longest x1 118 us: moe_call(): pl.pallas_call(moe_kernel, in_specs=[hbm] * 6, out_specs=[hbm, hbm], out_...]
    pallas_call x1, Pallas kernels: 39.1 us -> 34.2 us  [attend_call(): pl.pallas_call(attend_kernel, in_specs=[smem, smem, vmem, vmem, vmem, hbm...]
    unnamed x23 -> x15, local copies, waits for them, and re-layouts: 7.37 us -> 5.68 us
where the time goes in v5:
time: 217 us
  Pallas kernels  206 us (95%)
  local copies, waits for them, and re-layouts  5.68 us (3%)
  other arithmetic  4.48 us (2%)
    pallas_call x1, Pallas kernels, moe_call(): pl.pallas_call(moe_kernel, in_specs=[hbm] * 6, out_specs=[hbm, hbm], out_...  118 us
    pallas_call x1, Pallas kernels, attend_call(): pl.pallas_call(attend_kernel, in_specs=[smem, smem, vmem, vmem, vmem, hbm...  34.2 us
    pallas_call x1, Pallas kernels, qkv_call(): pl.pallas_call(qkv_kernel, in_specs=[vmem, vmem, vmem, vmem, hbm, hbm, hb...  32 us
    pallas_call x1, Pallas kernels, out_call(): pl.pallas_call(out_kernel, in_specs=[vmem, hbm, vmem, vmem, vmem, hbm], o...  21 us
    unnamed x15, local copies, waits for them, and re-layouts  5.68 us

profile of v5, /device:TPU:0, one launch (start us, length us, event | category | flops | bytes accessed | tf_op | source)
XLA Modules:
  0.0 216.6 jit_solution(14293044881677450375)
XLA Ops:
  0.6 0.9 convert_reduce_fusion
  1.5 0.1 select_reduce_fusion.order_ref
  1.6 0.7 convert_element_type.7
  2.4 0.9 select_select_fusion.1.vec_ref
  3.3 0.0 copy-start.3
  3.3 1.5 select_select_fusion.pick_ref
  4.8 0.1 broadcast_multiply_fusion
  4.9 0.3 sine_multiply_fusion
  5.2 0.0 copy-start
  5.2 1.2 copy-done
  6.4 0.0 copy-start.4
  6.4 32.0 %qkv.1 = (bf16[128,4096]{1,0:T(8,128)(2,1)S(1)}, bf16[128,4096]{1,0:T(8,128)(2,1)S(1)}, bf16[128,4096]{1,0:T(8,128)(2,1)S(1)}) custom-call(bf16[128,4096]{1,0:T(8,128)(2,1)S(1)} %copy-done, bf16[8,4096]{1,0:T(8,128)(2,1)S(1)} %select_select_fusion.1.vec_ref, f32[128,128]{1,0:T(8,128)S(1)} %get-tuple-element.18.cos_ref, ...), custom_call_target="tpu_custom_call" | custom-call | flops 12884901888 | bytes 100663296 | tf_op jit(solution)/shard_map/qkv/pallas_call | solution.py:83
  38.5 0.0 copy-done.3
  38.5 0.2 copy.26
  38.7 0.2 copy.27
  39.0 0.0 copy-start.1
  39.0 0.2 copy.28
  39.2 0.0 copy-start.2
  39.3 0.0 copy-done.4
  39.3 34.2 %attend.1 = bf16[128,32,128]{2,1,0:T(8,128)(2,1)S(1)} custom-call(s32[128]{0:T(128)S(1)} %select_reduce_fusion.order_ref, s32[128]{0:T(128)S(1)} %copy-done.4, bf16[128,32,128]{2,1,0:T(8,128)(2,1)S(1)} %bitcast.18, bf16[128,32,128]{2,1,0:T(8,128)(2,1)S(1)} %bitcast.14, bf16[128,32,128]{2,1,0:T(8,128)(2,1)S(1)} %bitcast.16, bf16[128,64,32,128]{3,2,1,0:T(8,128)(2,1)} %k_hbm.1, ...), custom_call_target="tpu_custom_call" | custom-call | flops 4294967296 | bytes 67108864 | tf_op jit(solution)/shard_map/attend/pallas_call | solution.py:193
  73.5 0.0 copy-done.1
  73.5 0.0 copy-done.2
  73.5 1.4 copy.31
  74.9 21.0 %project.1 = (bf16[128,4096]{1,0:T(8,128)(2,1)}, bf16[128,4224]{1,0:T(8,128)(2,1)}, f32[128,128]{1,0:T(8,128)}) custom-call(bf16[128,4096]{1,0:T(8,128)(2,1)} %bitcast.25, bf16[128,4096]{1,0:T(8,128)(2,1)} %x_hbm.1, bf16[8,4096]{1,0:T(8,128)(2,1)} %copy-done.3, bf16[16,4096]{1,0:T(8,128)(2,1)} %bitcast.26, s32[128,128]{1,0:T(8,128)} %select_select_fusion.pick_ref, ...), custom_call_target="tpu_custom_call" | custom-call | flops 4294967296 | bytes 33554432 | tf_op jit(solution)/shard_map/project/pallas_call | solution.py:263
  96.0 118.3 %moe.1 = (bf16[128,4096]{1,0:T(8,128)(2,1)}, bf16[8,128,4224]{2,1,0:T(8,128)(2,1)}) custom-call(bf16[128,4224]{1,0:T(8,128)(2,1)} %get-tuple-element.13.h_in, bf16[128,4096]{1,0:T(8,128)(2,1)} %get-tuple-element.14.x_hbm, f32[128,128]{1,0:T(8,128)} %get-tuple-element.15.gate_hbm, bf16[2,688,4096]{2,1,0:T(8,128)(2,1)} %bitcast.23, ...), custom_call_target="tpu_custom_call" | custom-call | tf_op jit(solution)/shard_map/moe/pallas_call | solution.py:542
  214.3 2.3 %copy.33 = bf16[128,4096]{1,0:T(8,128)(2,1)} copy(bf16[128,4096]{1,0:T(8,128)(2,1)} %get-tuple-element.32) | data formatting | bytes 2097152
  (7 shorter events, 0.0 us)
Async XLA Ops:
  3.3 35.2 %copy-start.3 = (bf16[8,4096]{1,0:T(8,128)(2,1)}, bf16[8,4096]{1,0:T(8,128)(2,1)S(1)}, u32[]{:S(2)}) copy-start(bf16[8,4096]{1,0:T(8,128)(2,1)S(1)} %select_select_fusion.1.vec_ref) | copy-start | bytes 196612
  5.2 1.2 copy-start
  6.4 32.9 %copy-start.4 = (s32[128]{0:T(128)S(1)}, s32[128]{0:T(128)}, u32[]{:S(2)}) copy-start(s32[128]{0:T(128)} %pos_ref.1) | copy-start | bytes 1540
  39.0 34.5 %copy-start.1 = (bf16[16,8,32,128]{3,2,1,0:T(8,128)(2,1)}, bf16[16,8,32,128]{3,2,1,0:T(8,128)(2,1)S(1)}, u32[]{:S(2)}) copy-start(bf16[16,8,32,128]{3,2,1,0:T(8,128)(2,1)S(1)} %copy.27) | copy-start | bytes 3145732
  39.2 34.3 %copy-start.2 = (bf16[16,8,32,128]{3,2,1,0:T(8,128)(2,1)}, bf16[16,8,32,128]{3,2,1,0:T(8,128)(2,1)S(1)}, u32[]{:S(2)}) copy-start(bf16[16,8,32,128]{3,2,1,0:T(8,128)(2,1)S(1)} %copy.28) | copy-start | bytes 3145732

commit v6 on v5

--- a/solution.py
+++ b/solution.py
@@ -94,7 +94,7 @@
 
 GROUP = 8
 SLOTS = 3
-STEP = 16
+STEP = 8
 CHUNK = 8
 
 
@@ -125,7 +125,9 @@
             @pl.when(chunks == k)
             def _(k=k):
                 src = pl.ds(0, k * CHUNK)
-                for i in range(GROUP):
+
+                @pl.loop(0, GROUP)
+                def _(i):
                     tok = order_ref[grp * GROUP + i]
                     pltpu.make_async_copy(k_hbm.at[tok, src], k_buf.at[slot, i, src], sems.at[0, slot]).start()
                     pltpu.make_async_copy(v_hbm.at[tok, src], v_buf.at[slot, i, src], sems.at[1, slot]).start()
@@ -207,10 +209,7 @@
     )(order, positions, q_rot, key_new, value_new, k_cache, v_cache)
 
 
-def out_kernel(a_ref, x_hbm, vec_ref, wr_ref, pick_ref, w_hbm, mid_hbm, h_hbm, gate_hbm, x_ref, mid_ref, h_ref, gate_ref, w_buf, sems, io_sems):
-    x_copy = pltpu.make_async_copy(x_hbm, x_ref, io_sems.at[0])
-    results = [pltpu.make_async_copy(src, dst, io_sems.at[1 + n]) for n, (src, dst) in enumerate(((mid_ref, mid_hbm), (h_ref, h_hbm), (gate_ref, gate_hbm)))]
-    x_copy.start()
+def out_kernel(a_ref, x_ref, vec_ref, wr_ref, pick_ref, w_hbm, mid_ref, h_ref, gate_ref, w_buf, sems):
     count, _, tile = w_buf.shape
 
     def weight(j):
@@ -219,7 +218,6 @@
 
     for j in range(count):
         weight(j).start()
-    x_copy.wait()
 
     @pl.loop(0, count)
     def _(j):
@@ -228,14 +226,12 @@
         mid = x_ref[:, cols].astype(jnp.float32) + jnp.dot(a_ref[...], w_buf[j], preferred_element_type=jnp.float32) + vec_ref[5:6, cols].astype(jnp.float32)
         mid_ref[:, cols] = mid.astype(jnp.bfloat16)
 
-    results[0].start()
     h_two = norm_rows(mid_ref[...].astype(jnp.float32), vec_ref[6:7], vec_ref[7:8]).astype(jnp.bfloat16)
     lanes = lax.broadcasted_iota(jnp.int32, (h_two.shape[0], 128), 1)
     pick_val = jnp.transpose(pick_ref[...].astype(jnp.float32))
     picks = jnp.where(lanes < 2, pick_val, 0.0)
     h_ref[:, :h_two.shape[1]] = h_two
     h_ref[:, h_two.shape[1]:] = picks.astype(jnp.bfloat16)
-    results[1].start()
     logits = lax.dot_general(h_two, wr_ref[...], (((1,), (1,)), ((), ())), preferred_element_type=jnp.float32)
     ids = lax.broadcasted_iota(jnp.int32, logits.shape, 1).astype(jnp.float32)
     hit_one = ids == pick_val[:, 0:1]
@@ -249,32 +245,20 @@
         gates.append(top / jnp.sum(e_val, axis=-1, keepdims=True))
     lane = lax.broadcasted_iota(jnp.int32, gate_ref.shape, 1)
     gate_ref[...] = jnp.where(lane == 0, gates[0], jnp.where(lane == 1, gates[1], 0.0))
-    results[2].start()
-    for copy in results:
-        copy.wait()
 
 
 def out_call(attn_flat, tokens, vectors, w_router, picks, w_out):
     rows, d_model = tokens.shape
     tile = 256
     vmem = pl.BlockSpec(memory_space=pltpu.VMEM)
-    hbm = pl.BlockSpec(memory_space=pl.ANY)
     shape = lambda cols, kind: jax.ShapeDtypeStruct((rows, cols), kind)
     return pl.pallas_call(
         out_kernel,
-        in_specs=[vmem, hbm, vmem, vmem, vmem, hbm],
-        out_specs=[pl.BlockSpec(memory_space=pltpu.HBM)] * 3,
+        in_specs=[vmem] * 5 + [pl.BlockSpec(memory_space=pl.ANY)],
+        out_specs=[vmem] * 3,
         out_shape=[shape(d_model, jnp.bfloat16), shape(d_model + 128, jnp.bfloat16), shape(128, jnp.float32)],
-        scratch_shapes=[
-            pltpu.VMEM((rows, d_model), jnp.bfloat16),
-            pltpu.VMEM((rows, d_model), jnp.bfloat16),
-            pltpu.VMEM((rows, d_model + 128), jnp.bfloat16),
-            pltpu.VMEM((rows, 128), jnp.float32),
-            pltpu.VMEM((d_model // tile, w_out.shape[0], tile), jnp.bfloat16),
-            pltpu.SemaphoreType.DMA((d_model // tile,)),
-            pltpu.SemaphoreType.DMA((4,)),
-        ],
-        compiler_params=pltpu.CompilerParams(vmem_limit_bytes=67043328),
+        scratch_shapes=[pltpu.VMEM((d_model // tile, w_out.shape[0], tile), jnp.bfloat16), pltpu.SemaphoreType.DMA((d_model // tile,))],
+        compiler_params=pltpu.CompilerParams(vmem_limit_bytes=48 * 2 ** 20),
         cost_estimate=pl.CostEstimate(flops=2 * rows * d_model * d_model, bytes_accessed=2 * d_model * d_model, transcendentals=0),
         name='project',
     )(attn_flat, tokens, vectors, w_router, picks, w_out)

time: 217 us -> 207 us (0.954)
  Pallas kernels: 206 us -> 194 us
    pallas_call x1, Pallas kernels: 21 us -> 12.8 us  [out_call(): pl.pallas_call(out_kernel, in_specs=[vmem] * 5 + [pl.BlockSpec(memory_spa...]
    pallas_call x1, Pallas kernels: 34.2 us -> 29.5 us  [attend_call(): pl.pallas_call(attend_kernel, in_specs=[smem, smem, vmem, vmem, vmem, hbm...]
    unnamed x15 -> x23, local copies, waits for them, and re-layouts: 5.68 us -> 7.37 us
where the time goes in v6:
time: 207 us; the launch traced here: 206 us
  Pallas kernels  194 us (94%)
  local copies, waits for them, and re-layouts  7.37 us (4%)
  other arithmetic  3.84 us (2%)
    pallas_call x1, Pallas kernels, moe_call(): pl.pallas_call(moe_kernel, in_specs=[hbm] * 6, out_specs=[hbm, hbm], out_...  120 us
    pallas_call x1, Pallas kernels, qkv_call(): pl.pallas_call(qkv_kernel, in_specs=[vmem, vmem, vmem, vmem, hbm, hbm, hb...  32.1 us
    pallas_call x1, Pallas kernels, attend_call(): pl.pallas_call(attend_kernel, in_specs=[smem, smem, vmem, vmem, vmem, hbm...  29.5 us
    pallas_call x1, Pallas kernels, out_call(): pl.pallas_call(out_kernel, in_specs=[vmem] * 5 + [pl.BlockSpec(memory_spa...  12.8 us
    unnamed x23, local copies, waits for them, and re-layouts  7.37 us

profile of v6, /device:TPU:0, one launch (start us, length us, event | category | flops | bytes accessed | tf_op | source)
XLA Modules:
  0.0 206.3 jit_solution(9387966245484616990)
XLA Ops:
  0.6 0.9 convert_reduce_fusion
  1.5 0.1 select_reduce_fusion.order_ref
  1.6 0.7 convert_element_type.7
  2.4 0.9 select_select_fusion.1.vec_ref
  3.3 0.8 select_select_fusion.pick_ref
  4.1 0.1 broadcast_multiply_fusion
  4.2 0.3 sine_multiply_fusion
  4.5 0.0 copy-start
  4.5 1.2 copy-done
  5.8 0.0 copy-start.8
  5.8 32.1 %qkv.1 = (bf16[128,4096]{1,0:T(8,128)(2,1)S(1)}, bf16[128,4096]{1,0:T(8,128)(2,1)S(1)}, bf16[128,4096]{1,0:T(8,128)(2,1)S(1)}) custom-call(bf16[128,4096]{1,0:T(8,128)(2,1)S(1)} %copy-done, bf16[8,4096]{1,0:T(8,128)(2,1)S(1)} %select_select_fusion.1.vec_ref, f32[128,128]{1,0:T(8,128)S(1)} %get-tuple-element.18.cos_ref, ...), custom_call_target="tpu_custom_call" | custom-call | flops 12884901888 | bytes 100663296 | tf_op jit(solution)/shard_map/qkv/pallas_call | solution.py:83
  37.8 0.2 copy.26
  38.1 0.2 copy.27
  38.3 0.0 copy-start.2
  38.3 0.2 copy.28
  38.6 0.0 copy-start.3
  38.6 0.0 copy-done.8
  38.6 0.0 copy-start.1
  38.6 0.0 copy-start.6
  38.6 29.5 %attend.1 = bf16[128,32,128]{2,1,0:T(8,128)(2,1)S(1)} custom-call(s32[128]{0:T(128)S(1)} %select_reduce_fusion.order_ref, s32[128]{0:T(128)S(1)} %copy-done.8, bf16[128,32,128]{2,1,0:T(8,128)(2,1)S(1)} %bitcast.18, bf16[128,32,128]{2,1,0:T(8,128)(2,1)S(1)} %bitcast.14, bf16[128,32,128]{2,1,0:T(8,128)(2,1)S(1)} %bitcast.16, bf16[128,64,32,128]{3,2,1,0:T(8,128)(2,1)} %k_hbm.1, ...), custom_call_target="tpu_custom_call" | custom-call | flops 4294967296 | bytes 67108864 | tf_op jit(solution)/shard_map/attend/pallas_call | solution.py:195
  68.2 0.0 copy-done.2
  68.2 0.0 copy-done.3
  68.2 0.5 copy.31
  68.7 0.0 copy-done.1
  68.7 0.0 copy-done.6
  68.7 12.8 %project.1 = (bf16[128,4096]{1,0:T(8,128)(2,1)S(1)}, bf16[128,4224]{1,0:T(8,128)(2,1)S(1)}, f32[128,128]{1,0:T(8,128)S(1)}) custom-call(bf16[128,4096]{1,0:T(8,128)(2,1)S(1)} %bitcast.20, bf16[128,4096]{1,0:T(8,128)(2,1)S(1)} %copy-done.1, bf16[8,4096]{1,0:T(8,128)(2,1)S(1)} %select_select_fusion.1.vec_ref, bf16[16,4096]{1,0:T(8,128)(2,1)S(1)} %bitcast.24, ...), custom_call_target="tpu_custom_call" | custom-call | flops 4294967296 | bytes 33554432 | tf_op jit(solution)/shard_map/project/pallas_call | solution.py:255
  81.5 0.0 copy-start.4
  81.5 1.1 copy-done.4
  82.6 0.0 copy-start.5
  82.6 1.0 copy-done.5
  83.6 0.0 copy-start.7
  83.6 0.6 copy-done.7
  84.2 119.9 %moe.1 = (bf16[128,4096]{1,0:T(8,128)(2,1)}, bf16[8,128,4224]{2,1,0:T(8,128)(2,1)}) custom-call(bf16[128,4224]{1,0:T(8,128)(2,1)} %copy-done.4, bf16[128,4096]{1,0:T(8,128)(2,1)} %copy-done.5, f32[128,128]{1,0:T(8,128)} %copy-done.7, bf16[2,688,4096]{2,1,0:T(8,128)(2,1)} %bitcast.25, bf16[2,688,4096]{2,1,0:T(8,128)(2,1)} %bitcast.26, ...), custom_call_target="tpu_custom_call" | custom-call | tf_op jit(solution)/shard_map/moe/pallas_call | solution.py:526
  204.1 2.3 %copy.33 = bf16[128,4096]{1,0:T(8,128)(2,1)} copy(bf16[128,4096]{1,0:T(8,128)(2,1)} %get-tuple-element.32) | data formatting | bytes 2097152
  (7 shorter events, 0.0 us)
Async XLA Ops:
  4.5 1.2 copy-start
  5.8 32.9 %copy-start.8 = (s32[128]{0:T(128)S(1)}, s32[128]{0:T(128)}, u32[]{:S(2)}) copy-start(s32[128]{0:T(128)} %pos_ref.1) | copy-start | bytes 1540
  38.3 29.9 %copy-start.2 = (bf16[16,8,32,128]{3,2,1,0:T(8,128)(2,1)}, bf16[16,8,32,128]{3,2,1,0:T(8,128)(2,1)S(1)}, u32[]{:S(2)}) copy-start(bf16[16,8,32,128]{3,2,1,0:T(8,128)(2,1)S(1)} %copy.27) | copy-start | bytes 3145732
  38.6 29.6 %copy-start.3 = (bf16[16,8,32,128]{3,2,1,0:T(8,128)(2,1)}, bf16[16,8,32,128]{3,2,1,0:T(8,128)(2,1)S(1)}, u32[]{:S(2)}) copy-start(bf16[16,8,32,128]{3,2,1,0:T(8,128)(2,1)S(1)} %copy.28) | copy-start | bytes 3145732
  38.6 30.0 %copy-start.1 = (bf16[128,4096]{1,0:T(8,128)(2,1)S(1)}, bf16[128,4096]{1,0:T(8,128)(2,1)}, u32[]{:S(2)}) copy-start(bf16[128,4096]{1,0:T(8,128)(2,1)} %x_ref.3) | copy-start | bytes 3145732
  38.6 30.0 %copy-start.6 = (bf16[4096,16]{0,1:T(8,128)(2,1)S(1)}, bf16[4096,16]{0,1:T(8,128)(2,1)}, u32[]{:S(2)}) copy-start(bf16[4096,16]{0,1:T(8,128)(2,1)} %param.42) | copy-start | bytes 393220
  81.5 1.1 copy-start.4
  82.6 1.0 copy-start.5
  83.6 0.6 copy-start.7

commit v7 on v6

--- a/solution.py
+++ b/solution.py
@@ -209,30 +209,8 @@
     )(order, positions, q_rot, key_new, value_new, k_cache, v_cache)
 
 
-def out_kernel(a_ref, x_ref, vec_ref, wr_ref, pick_ref, w_hbm, mid_ref, h_ref, gate_ref, w_buf, sems):
-    count, _, tile = w_buf.shape
-
-    def weight(j):
-        cols = pl.ds(pl.multiple_of(j * tile, tile), tile)
-        return pltpu.make_async_copy(w_hbm.at[:, cols], w_buf.at[j], sems.at[j])
-
-    for j in range(count):
-        weight(j).start()
-
-    @pl.loop(0, count)
-    def _(j):
-        weight(j).wait()
-        cols = pl.ds(pl.multiple_of(j * tile, tile), tile)
-        mid = x_ref[:, cols].astype(jnp.float32) + jnp.dot(a_ref[...], w_buf[j], preferred_element_type=jnp.float32) + vec_ref[5:6, cols].astype(jnp.float32)
-        mid_ref[:, cols] = mid.astype(jnp.bfloat16)
-
-    h_two = norm_rows(mid_ref[...].astype(jnp.float32), vec_ref[6:7], vec_ref[7:8]).astype(jnp.bfloat16)
-    lanes = lax.broadcasted_iota(jnp.int32, (h_two.shape[0], 128), 1)
-    pick_val = jnp.transpose(pick_ref[...].astype(jnp.float32))
-    picks = jnp.where(lanes < 2, pick_val, 0.0)
-    h_ref[:, :h_two.shape[1]] = h_two
-    h_ref[:, h_two.shape[1]:] = picks.astype(jnp.bfloat16)
-    logits = lax.dot_general(h_two, wr_ref[...], (((1,), (1,)), ((), ())), preferred_element_type=jnp.float32)
+def router_gates(h_two, wr_val, pick_val):
+    logits = lax.dot_general(h_two, wr_val, (((1,), (1,)), ((), ())), preferred_element_type=jnp.float32)
     ids = lax.broadcasted_iota(jnp.int32, logits.shape, 1).astype(jnp.float32)
     hit_one = ids == pick_val[:, 0:1]
     hit_two = ids == pick_val[:, 1:2]
@@ -243,25 +221,8 @@
         e_val = jnp.exp(masked - jnp.max(masked, axis=-1, keepdims=True))
         top = jnp.sum(jnp.where(hit, e_val, 0.0), axis=-1, keepdims=True)
         gates.append(top / jnp.sum(e_val, axis=-1, keepdims=True))
-    lane = lax.broadcasted_iota(jnp.int32, gate_ref.shape, 1)
-    gate_ref[...] = jnp.where(lane == 0, gates[0], jnp.where(lane == 1, gates[1], 0.0))
-
-
-def out_call(attn_flat, tokens, vectors, w_router, picks, w_out):
-    rows, d_model = tokens.shape
-    tile = 256
-    vmem = pl.BlockSpec(memory_space=pltpu.VMEM)
-    shape = lambda cols, kind: jax.ShapeDtypeStruct((rows, cols), kind)
-    return pl.pallas_call(
-        out_kernel,
-        in_specs=[vmem] * 5 + [pl.BlockSpec(memory_space=pl.ANY)],
-        out_specs=[vmem] * 3,
-        out_shape=[shape(d_model, jnp.bfloat16), shape(d_model + 128, jnp.bfloat16), shape(128, jnp.float32)],
-        scratch_shapes=[pltpu.VMEM((d_model // tile, w_out.shape[0], tile), jnp.bfloat16), pltpu.SemaphoreType.DMA((d_model // tile,))],
-        compiler_params=pltpu.CompilerParams(vmem_limit_bytes=48 * 2 ** 20),
-        cost_estimate=pl.CostEstimate(flops=2 * rows * d_model * d_model, bytes_accessed=2 * d_model * d_model, transcendentals=0),
-        name='project',
-    )(attn_flat, tokens, vectors, w_router, picks, w_out)
+    lane = lax.broadcasted_iota(jnp.int32, pick_val.shape, 1)
+    return jnp.where(lane == 0, gates[0], jnp.where(lane == 1, gates[1], 0.0))
 
 
 def attention_order(positions):
@@ -271,7 +232,7 @@
     return jnp.sum(jnp.where(rank[:, None] == ids[None, :], ids[:, None], 0), axis=0)
 
 
-def moe_kernel(h_in, x_hbm, gate_hbm, wg_hbm, wu_hbm, wd_hbm, out_hbm, hb, wg, wu, wd, gate_ref, xblk, zt_ref, z_ref, acc, stg, d2d, p1a, p1b, p2a, p2b, wsem, xsem, gsend, grecv, dsend, drecv, rsend, rrecv, credit):
+def moe_kernel(a_ref, x_hbm, vec_ref, wr_ref, pick_ref, wo_hbm, wg_hbm, wu_hbm, wd_hbm, out_hbm, hb, wg, wu, wd, sum_ref, mid_ref, h_in, gate_ref, xblk, zt_ref, z_ref, acc, stg, d2d, p1a, p1b, p2a, p2b, wsem, xsem, gsend, grecv, dsend, drecv, rsend, rrecv, osem, credit):
     me = lax.axis_index('ep')
     core = lax.rem(me, 2)
     x_pos = lax.rem(lax.div(me, 2), 2)
@@ -279,7 +240,7 @@
     partner = me + 1 - 2 * core
     xn = me + 2 - 4 * x_pos
     yn = me + 4 - 8 * y_pos
-    rows = h_in.shape[0]
+    rows = x_hbm.shape[0]
     mid = rows // 2
     d_model = x_hbm.shape[1]
     half = d_model // 2
@@ -326,10 +287,44 @@
     barrier = pltpu.get_barrier_semaphore()
     for dev in (partner, xn, yn):
         pl.semaphore_signal(barrier, inc=1, device_id=(dev,), device_id_type=mesh_id)
-    for e in range(2):
-        for copy in weight(e):
-            copy.start()
+    depth = ff // 128 * 128
+    homes = [buf.at[e, pl.ds(0, depth)] for e in range(2) for buf in (wg, wu, wd)]
+    refills = [copy for e in range(2) for copy in weight(e)]
+    spans = [(n * depth, depth) for n in range(len(homes))]
+    rest = d_model - len(homes) * depth
+    homes.append(xblk.at[pl.ds(0, rest), pl.ds(0, d_model)])
+    spans.append((d_model - rest, rest))
+    loads = [pltpu.make_async_copy(wo_hbm.at[pl.ds(*span)], home, osem.at[n]) for n, (span, home) in enumerate(zip(spans, homes))]
+    x_loads = [pltpu.make_async_copy(x_hbm.at[:, pl.ds(n * half, half)], stg.at[0, n], xsem.at[n]) for n in range(2)]
+    for copy in x_loads + loads:
+        copy.start()
+    for copy in x_loads:
+        copy.wait()
     zt_ref[...] = jnp.zeros_like(zt_ref)
+    for n, (span, home) in enumerate(zip(spans, homes)):
+        loads[n].wait()
+
+        @pl.loop(0, d_model // tile)
+        def _(i, n=n, span=span, home=home):
+            cols = pl.ds(pl.multiple_of(i * tile, tile), tile)
+            part = jnp.dot(a_ref[:, span[0]:span[0] + span[1]], home[:, cols], preferred_element_type=jnp.float32)
+            if n == 0:
+                sum_ref[:, cols] = part
+            elif n < len(homes) - 1:
+                sum_ref[:, cols] += part
+            else:
+                slim = pl.ds(pl.multiple_of(lax.rem(i, half // tile) * tile, tile), tile)
+                val = stg[0, lax.div(i, half // tile), :, slim].astype(jnp.float32) + (sum_ref[:, cols] + part) + vec_ref[5:6, cols].astype(jnp.float32)
+                mid_ref[:, cols] = val.astype(jnp.bfloat16)
+
+        if n < len(refills):
+            refills[n].start()
+    h_two = norm_rows(mid_ref[...].astype(jnp.float32), vec_ref[6:7], vec_ref[7:8]).astype(jnp.bfloat16)
+    pick_val = jnp.transpose(pick_ref[...].astype(jnp.float32))
+    lanes = lax.broadcasted_iota(jnp.int32, pick_val.shape, 1)
+    h_in[:, :d_model] = h_two
+    h_in[:, d_model:] = jnp.where(lanes < 2, pick_val, 0.0).astype(jnp.bfloat16)
+    gate_ref[...] = router_gates(h_two, wr_ref[...], pick_val)
     pl.semaphore_wait(barrier, 3)
     for h in range(2):
         from_x[h].start()
@@ -384,7 +379,10 @@
         @pl.when(r == 0)
         def _():
             own.wait_recv()
-            load([h_in, hb.at[1]])
+            copy = pltpu.make_async_copy(hb.at[1], xblk.at[pl.ds(rows, rows)], xsem.at[0])
+            copy.start()
+            xblk[:rows] = h_in[...]
+            copy.wait()
 
         for h in range(2):
             @pl.when(r == 1 + h)
@@ -417,13 +415,13 @@
             def _():
                 merge_high(r - 1, False)
 
-            for h in range(2):
-                @pl.when((r == h) & (e == 0))
-                def _(h=h):
-                    gather_step(h)
+            @pl.when((r == 1) & (e == 0))
+            def _():
+                gather_step(1)
 
         @pl.when(r == 0)
         def _():
+            gather_step(0)
             for e in range(2):
                 weight(e)[2].wait()
 
@@ -470,11 +468,7 @@
             x_far[0].start()
             x_far[1].start()
 
-    x_ref = xblk.at[pl.ds(0, rows), pl.ds(0, d_model)]
     out_ref = xblk.at[pl.ds(rows, rows), pl.ds(0, d_model)]
-    late = [pltpu.make_async_copy(x_hbm, x_ref, xsem.at[0]), pltpu.make_async_copy(gate_hbm, gate_ref, xsem.at[1])]
-    for copy in late:
-        copy.start()
     merge_high(3, True)
     y_far[0].start()
     y_far[1].start()
@@ -490,8 +484,6 @@
         merge(acc.at[0, 0, :, part_rows[h]], p1a.at[0, h])
         y_first[h].wait_recv()
         merge(acc.at[0, 1, :, part_rows[h]], p1b.at[0, h])
-    for copy in late:
-        copy.wait()
     for h in range(2):
         for part, last, buf in ((0, y_last, p2a), (1, x_last, p2b)):
             last[h].wait_recv()
@@ -503,7 +495,7 @@
                 wide = pl.ds(part * half, half)
                 gates = gate_ref[at]
                 y_val = [(acc[0, part, slot, at] + buf[h, slot, near]).astype(jnp.float32) * gates[:, slot:slot + 1] for slot in range(2)]
-                out_ref[at, wide] = (x_ref[at, wide].astype(jnp.float32) + (y_val[0] + y_val[1])).astype(jnp.bfloat16)
+                out_ref[at, wide] = (mid_ref[at, wide].astype(jnp.float32) + (y_val[0] + y_val[1])).astype(jnp.bfloat16)
 
     out_copy = pltpu.make_async_copy(out_ref, out_hbm, xsem.at[2])
     out_copy.start()
@@ -514,25 +506,29 @@
     out_copy.wait()
 
 
-def moe_call(h_ext, x_mid, gates, w_gate, w_up, w_down):
-    rows, d_model = x_mid.shape
+def moe_call(attn_flat, tokens, vectors, w_router, picks, w_out, w_gate, w_up, w_down):
+    rows, d_model = tokens.shape
     half = d_model // 2
     ff = w_gate.shape[2]
     ff_pad = pl.cdiv(ff, 128) * 128
-    width = h_ext.shape[1]
+    width = d_model + 128
+    vmem = pl.BlockSpec(memory_space=pltpu.VMEM)
     hbm = pl.BlockSpec(memory_space=pl.ANY)
     bf = jnp.bfloat16
     dma = pltpu.SemaphoreType.DMA
     out, _ = pl.pallas_call(
         moe_kernel,
-        in_specs=[hbm] * 6,
+        in_specs=[vmem, hbm, vmem, vmem, vmem] + [hbm] * 4,
         out_specs=[hbm, hbm],
         out_shape=[jax.ShapeDtypeStruct((rows, d_model), bf), jax.ShapeDtypeStruct((8, rows, width), bf)],
         scratch_shapes=[
             pltpu.VMEM((2, ff, d_model), bf),
             pltpu.VMEM((2, ff, d_model), bf),
             pltpu.VMEM((2, ff, d_model), bf),
-            pltpu.VMEM(gates.shape, gates.dtype),
+            pltpu.VMEM((rows, d_model), jnp.float32),
+            pltpu.VMEM((rows, d_model), bf),
+            pltpu.VMEM((rows, width), bf),
+            pltpu.VMEM((rows, 128), jnp.float32),
             pltpu.VMEM((2 * rows, width), bf),
             pltpu.VMEM((ff_pad, 2 * rows), bf),
             pltpu.VMEM((2, 2 * rows, ff_pad), bf),
@@ -551,11 +547,12 @@
             dma((4, 2)),
             dma((12,)),
             dma((12,)),
+            dma((7,)),
             pltpu.SemaphoreType.REGULAR,
         ],
         compiler_params=pltpu.CompilerParams(vmem_limit_bytes=67043328, collective_id=0, has_side_effects=True),
         name='moe',
-    )(h_ext, x_mid, gates, jnp.swapaxes(w_gate, 1, 2), jnp.swapaxes(w_up, 1, 2), w_down)
+    )(attn_flat, tokens, vectors, w_router, picks, w_out, jnp.swapaxes(w_gate, 1, 2), jnp.swapaxes(w_up, 1, 2), w_down)
     return out
 
 
@@ -572,8 +569,7 @@
         split = lambda t: t.reshape(tok_count, heads, head_dim)
         key_new, value_new = split(k_flat), split(v_flat)
         attn = attend_call(attention_order(positions), positions, split(q_flat), key_new, value_new, k_cache, v_cache)
-        x_mid, h_ext, gates = out_call(attn.reshape(tok_count, heads * head_dim), tokens, vectors, w_router.T, picks, w_out)
-        tokens_out = moe_call(h_ext, x_mid, gates, w_gate, w_up, w_down)
+        tokens_out = moe_call(attn.reshape(tok_count, heads * head_dim), tokens, vectors, w_router.T, picks, w_out, w_gate, w_up, w_down)
         return tokens_out, key_new, value_new
 
     row_spec = P('ep', None)

time: 207 us -> 217 us (1.048)
  Pallas kernels: 194 us -> 206 us
    pallas_call x2 -> x1, Pallas kernels: 133 us -> 143 us  [moe_call(): pl.pallas_call(moe_kernel, in_specs=[vmem, hbm, vmem, vmem, vmem] + [hbm]...]
    unnamed x23 -> x15, local copies, waits for them, and re-layouts: 7.37 us -> 5.68 us
where the time goes in v7:
time: 217 us
  Pallas kernels  206 us (95%)
  local copies, waits for them, and re-layouts  5.68 us (3%)
  other arithmetic  4.48 us (2%)
    pallas_call x1, Pallas kernels, moe_call(): pl.pallas_call(moe_kernel, in_specs=[vmem, hbm, vmem, vmem, vmem] + [hbm]...  143 us
    pallas_call x1, Pallas kernels, qkv_call(): pl.pallas_call(qkv_kernel, in_specs=[vmem, vmem, vmem, vmem, hbm, hbm, hb...  32.1 us
    pallas_call x1, Pallas kernels, attend_call(): pl.pallas_call(attend_kernel, in_specs=[smem, smem, vmem, vmem, vmem, hbm...  30.2 us
    unnamed x15, local copies, waits for them, and re-layouts  5.68 us

profile of v7, /device:TPU:0, one launch (start us, length us, event | category | flops | bytes accessed | tf_op | source)
XLA Modules:
  0.0 216.7 jit_solution(10484043891074760848)
XLA Ops:
  0.6 0.9 convert_reduce_fusion
  1.5 0.1 select_reduce_fusion.order_ref
  1.6 0.7 convert_element_type.7
  2.4 0.9 select_select_fusion.1.vec_ref
  3.3 0.0 copy-start.3
  3.3 1.5 select_select_fusion.pick_ref
  4.8 0.1 broadcast_multiply_fusion
  4.9 0.3 sine_multiply_fusion
  5.2 0.0 copy-start
  5.2 1.2 copy-done
  6.4 0.0 copy-start.4
  6.4 32.1 %qkv.1 = (bf16[128,4096]{1,0:T(8,128)(2,1)S(1)}, bf16[128,4096]{1,0:T(8,128)(2,1)S(1)}, bf16[128,4096]{1,0:T(8,128)(2,1)S(1)}) custom-call(bf16[128,4096]{1,0:T(8,128)(2,1)S(1)} %copy-done, bf16[8,4096]{1,0:T(8,128)(2,1)S(1)} %select_select_fusion.1.vec_ref, f32[128,128]{1,0:T(8,128)S(1)} %get-tuple-element.12.cos_ref, ...), custom_call_target="tpu_custom_call" | custom-call | flops 12884901888 | bytes 100663296 | tf_op jit(solution)/shard_map/qkv/pallas_call | solution.py:83
  38.5 0.0 copy-done.3
  38.5 0.2 copy.26
  38.7 0.2 copy.27
  39.0 0.0 copy-start.1
  39.0 0.2 copy.28
  39.3 0.0 copy-start.2
  39.3 0.0 copy-done.4
  39.3 30.2 %attend.1 = bf16[128,32,128]{2,1,0:T(8,128)(2,1)S(1)} custom-call(s32[128]{0:T(128)S(1)} %select_reduce_fusion.order_ref, s32[128]{0:T(128)S(1)} %copy-done.4, bf16[128,32,128]{2,1,0:T(8,128)(2,1)S(1)} %bitcast.18, bf16[128,32,128]{2,1,0:T(8,128)(2,1)S(1)} %bitcast.14, bf16[128,32,128]{2,1,0:T(8,128)(2,1)S(1)} %bitcast.16, bf16[128,64,32,128]{3,2,1,0:T(8,128)(2,1)} %k_hbm.1, ...), custom_call_target="tpu_custom_call" | custom-call | flops 4294967296 | bytes 67108864 | tf_op jit(solution)/shard_map/attend/pallas_call | solution.py:195
  69.5 0.0 copy-done.1
  69.5 0.0 copy-done.2
  69.5 1.4 copy.31
  70.9 143.4 %moe.1 = (bf16[128,4096]{1,0:T(8,128)(2,1)}, bf16[8,128,4224]{2,1,0:T(8,128)(2,1)}) custom-call(bf16[128,4096]{1,0:T(8,128)(2,1)} %bitcast.25, bf16[128,4096]{1,0:T(8,128)(2,1)} %x_hbm.1, bf16[8,4096]{1,0:T(8,128)(2,1)} %copy-done.3, bf16[16,4096]{1,0:T(8,128)(2,1)} %bitcast.26, s32[128,128]{1,0:T(8,128)} %select_select_fusion.pick_ref, ...), custom_call_target="tpu_custom_call" | custom-call | tf_op jit(solution)/shard_map/moe/pallas_call | solution.py:519
  214.4 2.3 %copy.33 = bf16[128,4096]{1,0:T(8,128)(2,1)} copy(bf16[128,4096]{1,0:T(8,128)(2,1)} %get-tuple-element.26) | data formatting | bytes 2097152
  (7 shorter events, 0.0 us)
Async XLA Ops:
  3.3 35.2 %copy-start.3 = (bf16[8,4096]{1,0:T(8,128)(2,1)}, bf16[8,4096]{1,0:T(8,128)(2,1)S(1)}, u32[]{:S(2)}) copy-start(bf16[8,4096]{1,0:T(8,128)(2,1)S(1)} %select_select_fusion.1.vec_ref) | copy-start | bytes 196612
  5.2 1.2 copy-start
  6.4 32.9 %copy-start.4 = (s32[128]{0:T(128)S(1)}, s32[128]{0:T(128)}, u32[]{:S(2)}) copy-start(s32[128]{0:T(128)} %pos_ref.1) | copy-start | bytes 1540
  39.0 30.5 %copy-start.1 = (bf16[16,8,32,128]{3,2,1,0:T(8,128)(2,1)}, bf16[16,8,32,128]{3,2,1,0:T(8,128)(2,1)S(1)}, u32[]{:S(2)}) copy-start(bf16[16,8,32,128]{3,2,1,0:T(8,128)(2,1)S(1)} %copy.27) | copy-start | bytes 3145732
  39.3 30.3 %copy-start.2 = (bf16[16,8,32,128]{3,2,1,0:T(8,128)(2,1)}, bf16[16,8,32,128]{3,2,1,0:T(8,128)(2,1)S(1)}, u32[]{:S(2)}) copy-start(bf16[16,8,32,128]{3,2,1,0:T(8,128)(2,1)S(1)} %copy.28) | copy-start | bytes 3145732

commit v8 on v6

--- a/solution.py
+++ b/solution.py
@@ -326,9 +326,8 @@
     barrier = pltpu.get_barrier_semaphore()
     for dev in (partner, xn, yn):
         pl.semaphore_signal(barrier, inc=1, device_id=(dev,), device_id_type=mesh_id)
-    for e in range(2):
-        for copy in weight(e):
-            copy.start()
+    for copy in weight(0)[:2]:
+        copy.start()
     zt_ref[...] = jnp.zeros_like(zt_ref)
     pl.semaphore_wait(barrier, 3)
     for h in range(2):
@@ -406,6 +405,11 @@
                 for copy in weight(e)[:2]:
                     copy.wait()
 
+                @pl.when(e == 0)
+                def _():
+                    for copy in weight(1)[:2] + [weight(0)[2], weight(1)[2]]:
+                        copy.start()
+
             x_val = xblk[:, :d_model]
             dims = (((1,), (1,)), ((), ()))
             u_val = lax.dot_general(wg[e], x_val, dims, preferred_element_type=jnp.float32)
@@ -417,10 +421,9 @@
             def _():
                 merge_high(r - 1, False)
 
-            for h in range(2):
-                @pl.when((r == h) & (e == 0))
-                def _(h=h):
-                    gather_step(h)
+        @pl.when(r == 1)
+        def _():
+            gather_step(1)
 
         @pl.when(r == 0)
         def _():
@@ -457,6 +460,10 @@
                 pl.semaphore_wait(credit, 1)
 
             shared(r, part).start()
+
+        @pl.when(r == 0)
+        def _():
+            gather_step(0)
 
         shared(r, 0).wait_recv()
         merge(acc.at[r, 0], d2d.at[lax.rem(r, 2), 0])

time: 207 us -> 206 us (level)
    pallas_call x1, Pallas kernels: 120 us -> 118 us  [moe_call(): pl.pallas_call(moe_kernel, in_specs=[hbm] * 6, out_specs=[hbm, hbm], out_...]
where the time goes in v8:
time: 206 us; the launch traced here: 205 us
  Pallas kernels  193 us (94%)
  local copies, waits for them, and re-layouts  7.37 us (4%)
  other arithmetic  3.84 us (2%)
    pallas_call x1, Pallas kernels, moe_call(): pl.pallas_call(moe_kernel, in_specs=[hbm] * 6, out_specs=[hbm, hbm], out_...  118 us
    pallas_call x1, Pallas kernels, qkv_call(): pl.pallas_call(qkv_kernel, in_specs=[vmem, vmem, vmem, vmem, hbm, hbm, hb...  32.1 us
    pallas_call x1, Pallas kernels, attend_call(): pl.pallas_call(attend_kernel, in_specs=[smem, smem, vmem, vmem, vmem, hbm...  30.7 us
    pallas_call x1, Pallas kernels, out_call(): pl.pallas_call(out_kernel, in_specs=[vmem] * 5 + [pl.BlockSpec(memory_spa...  12.8 us
    unnamed x23, local copies, waits for them, and re-layouts  7.37 us

profile of v8, /device:TPU:0, one launch (start us, length us, event | category | flops | bytes accessed | tf_op | source)
XLA Modules:
  0.0 205.3 jit_solution(1384807643307673943)
XLA Ops:
  0.6 0.9 convert_reduce_fusion
  1.5 0.1 select_reduce_fusion.order_ref
  1.6 0.7 convert_element_type.7
  2.4 0.9 select_select_fusion.1.vec_ref
  3.3 0.8 select_select_fusion.pick_ref
  4.1 0.1 broadcast_multiply_fusion
  4.2 0.3 sine_multiply_fusion
  4.5 0.0 copy-start
  4.5 1.2 copy-done
  5.8 0.0 copy-start.8
  5.8 32.1 %qkv.1 = (bf16[128,4096]{1,0:T(8,128)(2,1)S(1)}, bf16[128,4096]{1,0:T(8,128)(2,1)S(1)}, bf16[128,4096]{1,0:T(8,128)(2,1)S(1)}) custom-call(bf16[128,4096]{1,0:T(8,128)(2,1)S(1)} %copy-done, bf16[8,4096]{1,0:T(8,128)(2,1)S(1)} %select_select_fusion.1.vec_ref, f32[128,128]{1,0:T(8,128)S(1)} %get-tuple-element.18.cos_ref, ...), custom_call_target="tpu_custom_call" | custom-call | flops 12884901888 | bytes 100663296 | tf_op jit(solution)/shard_map/qkv/pallas_call | solution.py:83
  37.8 0.2 copy.26
  38.1 0.2 copy.27
  38.3 0.0 copy-start.2
  38.3 0.2 copy.28
  38.6 0.0 copy-start.3
  38.6 0.0 copy-done.8
  38.6 0.0 copy-start.1
  38.6 0.0 copy-start.6
  38.6 30.7 %attend.1 = bf16[128,32,128]{2,1,0:T(8,128)(2,1)S(1)} custom-call(s32[128]{0:T(128)S(1)} %select_reduce_fusion.order_ref, s32[128]{0:T(128)S(1)} %copy-done.8, bf16[128,32,128]{2,1,0:T(8,128)(2,1)S(1)} %bitcast.18, bf16[128,32,128]{2,1,0:T(8,128)(2,1)S(1)} %bitcast.14, bf16[128,32,128]{2,1,0:T(8,128)(2,1)S(1)} %bitcast.16, bf16[128,64,32,128]{3,2,1,0:T(8,128)(2,1)} %k_hbm.1, ...), custom_call_target="tpu_custom_call" | custom-call | flops 4294967296 | bytes 67108864 | tf_op jit(solution)/shard_map/attend/pallas_call | solution.py:195
  69.4 0.0 copy-done.2
  69.4 0.0 copy-done.3
  69.4 0.5 copy.31
  69.9 0.0 copy-done.1
  69.9 0.0 copy-done.6
  69.9 12.8 %project.1 = (bf16[128,4096]{1,0:T(8,128)(2,1)S(1)}, bf16[128,4224]{1,0:T(8,128)(2,1)S(1)}, f32[128,128]{1,0:T(8,128)S(1)}) custom-call(bf16[128,4096]{1,0:T(8,128)(2,1)S(1)} %bitcast.20, bf16[128,4096]{1,0:T(8,128)(2,1)S(1)} %copy-done.1, bf16[8,4096]{1,0:T(8,128)(2,1)S(1)} %select_select_fusion.1.vec_ref, bf16[16,4096]{1,0:T(8,128)(2,1)S(1)} %bitcast.24, ...), custom_call_target="tpu_custom_call" | custom-call | flops 4294967296 | bytes 33554432 | tf_op jit(solution)/shard_map/project/pallas_call | solution.py:255
  82.7 0.0 copy-start.4
  82.7 1.1 copy-done.4
  83.8 0.0 copy-start.5
  83.8 1.0 copy-done.5
  84.8 0.0 copy-start.7
  84.8 0.6 copy-done.7
  85.4 117.6 %moe.1 = (bf16[128,4096]{1,0:T(8,128)(2,1)}, bf16[8,128,4224]{2,1,0:T(8,128)(2,1)}) custom-call(bf16[128,4224]{1,0:T(8,128)(2,1)} %copy-done.4, bf16[128,4096]{1,0:T(8,128)(2,1)} %copy-done.5, f32[128,128]{1,0:T(8,128)} %copy-done.7, bf16[2,688,4096]{2,1,0:T(8,128)(2,1)} %bitcast.25, bf16[2,688,4096]{2,1,0:T(8,128)(2,1)} %bitcast.26, ...), custom_call_target="tpu_custom_call" | custom-call | tf_op jit(solution)/shard_map/moe/pallas_call | solution.py:533
  203.0 2.3 %copy.33 = bf16[128,4096]{1,0:T(8,128)(2,1)} copy(bf16[128,4096]{1,0:T(8,128)(2,1)} %get-tuple-element.32) | data formatting | bytes 2097152
  (7 shorter events, 0.0 us)
Async XLA Ops:
  4.5 1.2 copy-start
  5.8 32.9 %copy-start.8 = (s32[128]{0:T(128)S(1)}, s32[128]{0:T(128)}, u32[]{:S(2)}) copy-start(s32[128]{0:T(128)} %pos_ref.1) | copy-start | bytes 1540
  38.3 31.1 %copy-start.2 = (bf16[16,8,32,128]{3,2,1,0:T(8,128)(2,1)}, bf16[16,8,32,128]{3,2,1,0:T(8,128)(2,1)S(1)}, u32[]{:S(2)}) copy-start(bf16[16,8,32,128]{3,2,1,0:T(8,128)(2,1)S(1)} %copy.27) | copy-start | bytes 3145732
  38.6 30.8 %copy-start.3 = (bf16[16,8,32,128]{3,2,1,0:T(8,128)(2,1)}, bf16[16,8,32,128]{3,2,1,0:T(8,128)(2,1)S(1)}, u32[]{:S(2)}) copy-start(bf16[16,8,32,128]{3,2,1,0:T(8,128)(2,1)S(1)} %copy.28) | copy-start | bytes 3145732
  38.6 31.3 %copy-start.1 = (bf16[128,4096]{1,0:T(8,128)(2,1)S(1)}, bf16[128,4096]{1,0:T(8,128)(2,1)}, u32[]{:S(2)}) copy-start(bf16[128,4096]{1,0:T(8,128)(2,1)} %x_ref.3) | copy-start | bytes 3145732
  38.6 31.3 %copy-start.6 = (bf16[4096,16]{0,1:T(8,128)(2,1)S(1)}, bf16[4096,16]{0,1:T(8,128)(2,1)}, u32[]{:S(2)}) copy-start(bf16[4096,16]{0,1:T(8,128)(2,1)} %param.42) | copy-start | bytes 393220
  82.7 1.1 copy-start.4
  83.8 1.0 copy-start.5
  84.8 0.6 copy-start.7

commit v9 on v8

--- a/solution.py
+++ b/solution.py
@@ -93,8 +93,7 @@
 
 
 GROUP = 8
-SLOTS = 3
-STEP = 8
+SLOTS = 4
 CHUNK = 8
 
 
@@ -107,15 +106,11 @@
     row_id = lax.broadcasted_iota(jnp.int32, sid_ref.shape, 0)
     sid_ref[...] = jnp.where(lax.rem(key_id, heads) == row_id, lax.div(key_id, heads), seq)
 
-    @pl.loop(0, GROUP * SLOTS)
-    def _(i):
-        v_buf[i // GROUP, i % GROUP] = jnp.zeros(v_buf.shape[2:], v_buf.dtype)
-
     def group_at(n):
         return jnp.where(n & 1 == 0, n // 2, groups - 1 - n // 2)
 
     def chunks_at(n):
-        return (pos_ref[order_ref[group_at(n) * GROUP]] + CHUNK - 1) // CHUNK
+        return jnp.maximum((pos_ref[order_ref[group_at(n) * GROUP]] + CHUNK - 1) // CHUNK, 1)
 
     def fetch(n):
         grp = group_at(n)
@@ -148,12 +143,12 @@
     def compute(n, steps):
         grp = group_at(n)
         slot = lax.rem(n, SLOTS)
-        keys = steps * STEP * heads
+        keys = steps * CHUNK * heads
         toks = [order_ref[grp * GROUP + i] for i in range(GROUP)]
         q_val = [q_ref[t] for t in toks]
         scores = []
         for i in range(GROUP):
-            k_val = k_buf[slot, i, pl.ds(0, steps * STEP)].reshape(keys, head_dim)
+            k_val = k_buf[slot, i, pl.ds(0, steps * CHUNK)].reshape(keys, head_dim)
             raw = lax.dot_general(q_val[i], k_val, (((1,), (1,)), ((), ())), preferred_element_type=jnp.float32)
             scores.append(jnp.where(sid_ref[:, :keys] < pos_ref[toks[i]], raw * scale, -jnp.inf))
         for i in range(GROUP):
@@ -165,7 +160,7 @@
             inv = 1.0 / (jnp.sum(e_val, axis=-1, keepdims=True) + e_new)
             p_val = (e_val * inv).astype(jnp.bfloat16)
             p_new = (e_new * inv).astype(jnp.bfloat16).astype(jnp.float32)
-            v_val = v_buf[slot, i, pl.ds(0, steps * STEP)].reshape(keys, head_dim)
+            v_val = v_buf[slot, i, pl.ds(0, steps * CHUNK)].reshape(keys, head_dim)
             res = jnp.dot(p_val, v_val, preferred_element_type=jnp.float32) + p_new * vn_ref[t].astype(jnp.float32)
             out_ref[t] = res.astype(jnp.bfloat16)
 
@@ -179,9 +174,8 @@
             fetch(n + SLOTS - 1)
 
         settle(n)
-        most = pos_ref[order_ref[group_at(n) * GROUP]]
-        steps = jnp.maximum((most + STEP - 1) // STEP, 1)
-        for k in range(1, seq // STEP + 1):
+        steps = chunks_at(n)
+        for k in range(1, seq // CHUNK + 1):
             @pl.when(steps == k)
             def _(k=k):
                 compute(n, k)

time: 206 us -> 204 us (level)
  no operation moved by 1% of the time
where the time goes in v9:
time: 204 us
  Pallas kernels  192 us (94%)
  local copies, waits for them, and re-layouts  7.37 us (4%)
  other arithmetic  3.84 us (2%)
    pallas_call x1, Pallas kernels, moe_call(): pl.pallas_call(moe_kernel, in_specs=[hbm] * 6, out_specs=[hbm, hbm], out_...  118 us
    pallas_call x1, Pallas kernels, qkv_call(): pl.pallas_call(qkv_kernel, in_specs=[vmem, vmem, vmem, vmem, hbm, hbm, hb...  32.1 us
    pallas_call x1, Pallas kernels, attend_call(): pl.pallas_call(attend_kernel, in_specs=[smem, smem, vmem, vmem, vmem, hbm...  28.8 us
    pallas_call x1, Pallas kernels, out_call(): pl.pallas_call(out_kernel, in_specs=[vmem] * 5 + [pl.BlockSpec(memory_spa...  12.8 us
    unnamed x23, local copies, waits for them, and re-layouts  7.37 us

profile of v9, /device:TPU:0, one launch (start us, length us, event | category | flops | bytes accessed | tf_op | source)
XLA Modules:
  0.0 204.0 jit_solution(12298666927267180021)
XLA Ops:
  0.6 0.9 convert_reduce_fusion
  1.5 0.1 select_reduce_fusion.order_ref
  1.6 0.7 convert_element_type.7
  2.4 0.9 select_select_fusion.1.vec_ref
  3.3 0.8 select_select_fusion.pick_ref
  4.1 0.1 broadcast_multiply_fusion
  4.2 0.3 sine_multiply_fusion
  4.5 0.0 copy-start
  4.5 1.2 copy-done
  5.8 0.0 copy-start.8
  5.8 32.1 %qkv.1 = (bf16[128,4096]{1,0:T(8,128)(2,1)S(1)}, bf16[128,4096]{1,0:T(8,128)(2,1)S(1)}, bf16[128,4096]{1,0:T(8,128)(2,1)S(1)}) custom-call(bf16[128,4096]{1,0:T(8,128)(2,1)S(1)} %copy-done, bf16[8,4096]{1,0:T(8,128)(2,1)S(1)} %select_select_fusion.1.vec_ref, f32[128,128]{1,0:T(8,128)S(1)} %get-tuple-element.18.cos_ref, ...), custom_call_target="tpu_custom_call" | custom-call | flops 12884901888 | bytes 100663296 | tf_op jit(solution)/shard_map/qkv/pallas_call | solution.py:83
  37.8 0.2 copy.26
  38.1 0.2 copy.27
  38.3 0.0 copy-start.2
  38.3 0.2 copy.28
  38.6 0.0 copy-start.3
  38.6 0.0 copy-done.8
  38.6 0.0 copy-start.1
  38.6 0.0 copy-start.6
  38.6 28.8 %attend.1 = bf16[128,32,128]{2,1,0:T(8,128)(2,1)S(1)} custom-call(s32[128]{0:T(128)S(1)} %select_reduce_fusion.order_ref, s32[128]{0:T(128)S(1)} %copy-done.8, bf16[128,32,128]{2,1,0:T(8,128)(2,1)S(1)} %bitcast.18, bf16[128,32,128]{2,1,0:T(8,128)(2,1)S(1)} %bitcast.14, bf16[128,32,128]{2,1,0:T(8,128)(2,1)S(1)} %bitcast.16, bf16[128,64,32,128]{3,2,1,0:T(8,128)(2,1)} %k_hbm.1, ...), custom_call_target="tpu_custom_call" | custom-call | flops 4294967296 | bytes 67108864 | tf_op jit(solution)/shard_map/attend/pallas_call | solution.py:189
  67.4 0.0 copy-done.2
  67.5 0.0 copy-done.3
  67.5 0.5 copy.31
  67.9 0.0 copy-done.1
  67.9 0.0 copy-done.6
  67.9 12.8 %project.1 = (bf16[128,4096]{1,0:T(8,128)(2,1)S(1)}, bf16[128,4224]{1,0:T(8,128)(2,1)S(1)}, f32[128,128]{1,0:T(8,128)S(1)}) custom-call(bf16[128,4096]{1,0:T(8,128)(2,1)S(1)} %bitcast.20, bf16[128,4096]{1,0:T(8,128)(2,1)S(1)} %copy-done.1, bf16[8,4096]{1,0:T(8,128)(2,1)S(1)} %select_select_fusion.1.vec_ref, bf16[16,4096]{1,0:T(8,128)(2,1)S(1)} %bitcast.24, ...), custom_call_target="tpu_custom_call" | custom-call | flops 4294967296 | bytes 33554432 | tf_op jit(solution)/shard_map/project/pallas_call | solution.py:249
  80.8 0.0 copy-start.4
  80.8 1.1 copy-done.4
  81.8 0.0 copy-start.5
  81.9 1.0 copy-done.5
  82.8 0.0 copy-start.7
  82.8 0.6 copy-done.7
  83.4 118.2 %moe.1 = (bf16[128,4096]{1,0:T(8,128)(2,1)}, bf16[8,128,4224]{2,1,0:T(8,128)(2,1)}) custom-call(bf16[128,4224]{1,0:T(8,128)(2,1)} %copy-done.4, bf16[128,4096]{1,0:T(8,128)(2,1)} %copy-done.5, f32[128,128]{1,0:T(8,128)} %copy-done.7, bf16[2,688,4096]{2,1,0:T(8,128)(2,1)} %bitcast.25, bf16[2,688,4096]{2,1,0:T(8,128)(2,1)} %bitcast.26, ...), custom_call_target="tpu_custom_call" | custom-call | tf_op jit(solution)/shard_map/moe/pallas_call | solution.py:527
  201.7 2.3 %copy.33 = bf16[128,4096]{1,0:T(8,128)(2,1)} copy(bf16[128,4096]{1,0:T(8,128)(2,1)} %get-tuple-element.32) | data formatting | bytes 2097152
  (7 shorter events, 0.0 us)
Async XLA Ops:
  4.5 1.2 copy-start
  5.8 32.9 %copy-start.8 = (s32[128]{0:T(128)S(1)}, s32[128]{0:T(128)}, u32[]{:S(2)}) copy-start(s32[128]{0:T(128)} %pos_ref.1) | copy-start | bytes 1540
  38.3 29.1 %copy-start.2 = (bf16[16,8,32,128]{3,2,1,0:T(8,128)(2,1)}, bf16[16,8,32,128]{3,2,1,0:T(8,128)(2,1)S(1)}, u32[]{:S(2)}) copy-start(bf16[16,8,32,128]{3,2,1,0:T(8,128)(2,1)S(1)} %copy.27) | copy-start | bytes 3145732
  38.6 28.9 %copy-start.3 = (bf16[16,8,32,128]{3,2,1,0:T(8,128)(2,1)}, bf16[16,8,32,128]{3,2,1,0:T(8,128)(2,1)S(1)}, u32[]{:S(2)}) copy-start(bf16[16,8,32,128]{3,2,1,0:T(8,128)(2,1)S(1)} %copy.28) | copy-start | bytes 3145732
  38.6 29.3 %copy-start.1 = (bf16[128,4096]{1,0:T(8,128)(2,1)S(1)}, bf16[128,4096]{1,0:T(8,128)(2,1)}, u32[]{:S(2)}) copy-start(bf16[128,4096]{1,0:T(8,128)(2,1)} %x_ref.3) | copy-start | bytes 3145732
  38.6 29.3 %copy-start.6 = (bf16[4096,16]{0,1:T(8,128)(2,1)S(1)}, bf16[4096,16]{0,1:T(8,128)(2,1)}, u32[]{:S(2)}) copy-start(bf16[4096,16]{0,1:T(8,128)(2,1)} %param.42) | copy-start | bytes 393220
  80.8 1.1 copy-start.4
  81.8 1.0 copy-start.5
  82.8 0.6 copy-start.7
